TPU v7x, 32 devices: a whole 2x2x4 slice. The times are simulated.
32 devices in a mesh: mem: 8 (over y, x, core), sub: 4 (over z).
Axes of the slice: x: 2, y: 2, z: 4, core: 2. Of those that a mesh axis runs over, the one named last changes fastest.
Arguments:
- control: bfloat16 [64, 1024, 128], P('mem', 'sub'), may hold values from -6 to 6
- perturb: bfloat16 [64, 1024, 128], P('mem', 'sub'), may hold values from -6 to 6
- obs_column: int32 [8, 4, 1024], P('mem', 'sub'), may hold values from 0 to 255
- obs_count: int32 [8, 4], P('mem', 'sub'), may hold values from 128 to 1024, as said below
- obs_background: bfloat16 [8, 4, 1024, 128], P('mem', 'sub'), may hold values from -6 to 6
- obs_value: bfloat16 [8, 4, 1024, 128], P('mem', 'sub'), may hold values from -6 to 6
- obs_weight: float32 [8, 4, 1024], P('mem', 'sub'), may hold values from 0.05 to 0.5
- w_in: bfloat16 [128, 2048], replicated, may hold values from -0.5 to 0.5
- b_in: float32 [2048], replicated, may hold values from -3 to 3
- w_out: bfloat16 [2048, 128], replicated, may hold values from -0.125 to 0.125
Outputs:
- increment: float32 [1024, 128], P(('sub', 'mem'))
- grad_columns: float32 [1024, 128], P(('sub', 'mem'))
Inputs may be any that keep to these rules, and one draw needn't show every extreme that they name: `obs_count`: at least one batch has all 1024 slots live in every draw.
All inputs are finite; a program needn't handle non-finite values.
Results may differ from a plain program's by a relative error of at most 0.0025.
Values sent between devices are 32-bit elements; how exact they have to be, the bound alone decides.
No kernel may reach another device: no remote copies, remote signals or barrier semaphores. Data moves between devices by JAX's collectives and lax.ppermute only.
A program may use at most 64 MiB of HBM per device.

v0:
```python
import jax
import jax.numpy as jnp
from jax import lax
from jax.sharding import PartitionSpec as P

SWEEPS = 4


diffusion = 0.4


def padded_2(block, sides, width):
    for axis, dim in sides:
        count = lax.axis_size(axis)
        forward = [(i, i + 1) for i in range(count - 1)]
        forward.append((count - 1, 0))
        backward = [(target, source) for source, target in forward]
        low = lax.ppermute(
            lax.slice_in_dim(block, block.shape[dim] - width, None, axis=dim), axis, forward
        )
        high = lax.ppermute(lax.slice_in_dim(block, 0, width, axis=dim), axis, backward)
        block = jnp.concatenate([low, block, high], axis=dim)
    return block


def gelu_tanh(values):
    return jax.nn.gelu(values, approximate=True)


def sweep(padded):
    middle = padded[:, 1:-1]
    return middle + diffusion * (padded[:, :-2] - 2.0 * middle + padded[:, 2:])


def observe_block(whole_cols, indices, live, background, targets, weights, w_in, b_in, w_out):
    sampled = jnp.take(whole_cols, indices, axis=0)
    inputs = (background.astype(jnp.float32) + sampled).astype(jnp.bfloat16)
    hidden_pre = jnp.dot(inputs, w_in, preferred_element_type=jnp.float32) + b_in
    hidden, pullback = jax.vjp(gelu_tanh, hidden_pre)
    hidden_low = hidden.astype(jnp.bfloat16)
    outputs = jnp.dot(hidden_low, w_out, preferred_element_type=jnp.float32)
    misfit = ((outputs - targets.astype(jnp.float32)) * (weights * live)[:, None]).astype(
        jnp.bfloat16
    )
    back_hidden = lax.dot_general(
        misfit, w_out, (((1,), (1,)), ((), ())), preferred_element_type=jnp.float32
    )
    (back_pre,) = pullback(back_hidden)
    back_pre = back_pre.astype(jnp.bfloat16)
    back_input = lax.dot_general(
        back_pre, w_in, (((1,), (1,)), ((), ())), preferred_element_type=jnp.float32
    )
    back_input = back_input.astype(jnp.bfloat16)
    column_ids = lax.broadcasted_iota(jnp.int32, (indices.shape[0], whole_cols.shape[0]), 1)
    one_hot = (indices[:, None] == column_ids).astype(jnp.bfloat16)
    return lax.dot_general(
        one_hot, back_input, (((0,), (0,)), ((), ())), preferred_element_type=jnp.float32
    )


def per_device(
    control,
    perturb,
    obs_column,
    obs_count,
    obs_background,
    obs_value,
    obs_weight,
    w_in,
    b_in,
    w_out,
):
    field = control.astype(jnp.float32)
    padded = padded_2(field, (("sub", 1),), SWEEPS)
    for sweep_index in range(SWEEPS):
        padded = sweep(padded)
    field = padded
    partial_sum = jnp.sum(field * perturb.astype(jnp.float32), axis=0)
    members = perturb.shape[0] * lax.axis_size("mem")
    scale = (members - 1) ** (-0.5)
    owned = partial_sum.shape[0] // lax.axis_size("mem")
    whole_cols = lax.psum(partial_sum, "mem") * scale
    increment = lax.dynamic_slice_in_dim(whole_cols, lax.axis_index("mem") * owned, owned, 0)
    indices = obs_column.reshape(-1)
    background = obs_background.reshape(indices.shape[0], -1)
    targets = obs_value.reshape(indices.shape[0], -1)
    weights = obs_weight.reshape(-1)
    live_count = obs_count.reshape(())
    slot_ids = lax.broadcasted_iota(jnp.int32, (indices.shape[0],), 0)
    live = (slot_ids < live_count).astype(jnp.float32)
    gradient = observe_block(
        whole_cols, indices, live, background, targets, weights, w_in, b_in, w_out
    )
    grad_columns = lax.psum_scatter(gradient, "mem", scatter_dimension=0, tiled=True)
    return (increment, grad_columns)


def solution(mesh):
    return jax.shard_map(
        per_device,
        mesh=mesh,
        in_specs=(
            P("mem", "sub", None),
            P("mem", "sub", None),
            P("mem", "sub", None),
            P("mem", "sub"),
            P("mem", "sub", None, None),
            P("mem", "sub", None, None),
            P("mem", "sub", None),
            P(),
            P(),
            P(),
        ),
        out_specs=(P(("sub", "mem"), None), P(("sub", "mem"), None)),
        check_vma=False,
    )
```

profile of v0, /device:TPU:0, one launch (start us, length us, event | category | flops | bytes accessed | tf_op | source)
XLA Modules:
  0.0 135.8 jit_solution(15653344673557643430)
XLA Ops:
  7.2 0.0 all-reduce.2.cloned.1.call-start
  7.2 0.8 fusion.48
  8.0 5.1 %collective-permute-start.1 = (f32[8,4,128]{2,1,0:T(4,128)S(1)}, f32[8,4,128]{2,1,0:T(4,128)S(1)}, u32[]{:S(2)}, u32[]{:S(2)}) collective-permute-start(f32[8,4,128]{2,1,0:T(4,128)S(1)} %get-tuple-element.3), channel_id=1, source_target_pairs={{1,0},{2,1},{3,2},{0,3},{5,4},{6,5},{7,6},{4,7},{9,8},{10,9},{11,1... | collective-permute-start | bytes 49160 | tf_op jit(solution)/shard_map/ppermute | solution.py:21
  13.2 0.7 compare_select_fusion
  14.5 0.7 fusion.36
  15.2 1.1 convert_element_type.35
  16.3 2.4 %collective-permute-done = f32[8,4,128]{2,1,0:T(4,128)S(1)} collective-permute-done((f32[8,4,128]{2,1,0:T(4,128)S(1)}, f32[8,4,128]{2,1,0:T(4,128)S(1)}, u32[]{:S(2)}, u32[]{:S(2)}) %collective-permute-start) | collective-permute-done | bytes 16416 | tf_op jit(solution)/shard_map/ppermute | solution.py:18
  18.7 0.1 pad_maximum_fusion
  18.8 0.3 fusion.23
  19.1 0.3 fusion.21
  19.5 0.3 fusion.19
  19.8 1.1 fusion.27
  20.9 0.0 all-reduce.2.cloned.1.call-update
  20.9 0.0 reduce-scatter.2.cloned.1.call-start
  21.0 52.6 %all-reduce.2.cloned.1.call-done = f32[256,128]{1,0:T(8,128)} async-done(((f32[256,128]{1,0:T(8,128)}), f32[256,128]{1,0:T(8,128)}) %all-reduce.2.cloned.1.call-update) | async-done | bytes 131088 | tf_op jit(solution)/shard_map/psum | solution.py:82
  73.6 0.9 broadcast_multiply_fusion
  74.5 2.8 %gather_fusion = f32[1024,128]{1,0:T(8,128)S(1)} fusion(f32[256,128]{1,0:T(8,128)S(1)} %broadcast_multiply_fusion, s32[1024]{0:T(1024)S(1)} %broadcast_clamp_fusion), kind=kCustom, calls=%fused_computation | custom fusion | bytes 1052672 | tf_op jit(solution)/shard_map/jit(_take)/gather | solution.py:36
  77.4 1.3 fusion.31
  78.7 3.2 %copy-done.1 = f32[1024,2048]{1,0:T(8,128)} copy-done((f32[1024,2048]{1,0:T(8,128)}, f32[1024,2048]{1,0:T(8,128)S(1)}, u32[]{:S(2)}) %copy-start.1) | copy-done | bytes 8388632
  81.9 3.2 %fusion.14 = bf16[1024,128]{1,0:T(8,128)(2,1)S(1)} fusion(bf16[2048,128]{1,0:T(8,128)(2,1)S(1)} %copy-done.5, f32[1024,2048]{1,0:T(8,128)S(1)} %fusion.31, f32[2048]{0:T(1024)S(1)} %copy-done.7, bf16[1,1,1024,128]{3,2,1,0:T(8,128)(2,1)S(1)} %copy-done.6, f32[1024]{0:T(1024)S(1)} %fusion.36), kind=kOutput, calls=%fused_computation.16 | convolution fusion | flops 558366720 | bytes 9449472 | tf_op jit(solution)/shard_map/dot_general | solution.py:41
  85.1 9.4 %fusion.15 = bf16[1024,128]{1,0:T(8,128)(2,1)S(1)} fusion(bf16[128,2048]{1,0:T(8,128)(2,1)S(1)} %copy-done, f32[1024,2048]{1,0:T(8,128)} %copy-done.1, f32[2048]{0:T(1024)S(1)} %copy-done.7, bf16[1024,128]{1,0:T(8,128)(2,1)S(1)} %fusion.14, bf16[2048,128]{1,0:T(8,128)(2,1)S(1)} %copy-done.5), kind=kOutput, calls=%fused_computation.17 | convolution fusion | flops 1117913088 | bytes 9969664 | tf_op jit(solution)/shard_map/dot_general | solution.py:50
  94.6 1.3 fusion.28
  95.9 0.6 constant_dynamic-slice_fusion
  96.5 32.5 %reduce-scatter.2.cloned.1.call-done = f32[32,128]{1,0:T(8,128)} async-done(((f32[256,128]{1,0:T(8,128)}), f32[32,128]{1,0:T(8,128)}) %reduce-scatter.2.cloned.1.call-update) | async-done | bytes 16400 | tf_op jit(solution)/shard_map/reduce_scatter | solution.py:94
  (20 shorter events, 0.1 us)
Async XLA Ops:
  7.2 70.2 %copy-start = (bf16[128,2048]{1,0:T(8,128)(2,1)S(1)}, bf16[128,2048]{1,0:T(8,128)(2,1)}, u32[]{:S(2)}) copy-start(bf16[128,2048]{1,0:T(8,128)(2,1)} %param.17) | copy-start | bytes 1572868
  7.2 66.4 %all-reduce.2.cloned.1.call-start = ((), (), s32[]{:S(2)}) async-start(), calls=%async_computation.1 | async-start | bytes 262144 | tf_op jit(solution)/shard_map/psum | solution.py:82
  8.0 11.8 %copy-start.3 = (bf16[8,256,128]{2,1,0:T(8,128)(2,1)S(1)}, bf16[8,256,128]{2,1,0:T(8,128)(2,1)}, u32[]{:S(2)}) copy-start(bf16[8,256,128]{2,1,0:T(8,128)(2,1)} %param.11) | copy-start | bytes 1572868
  8.0 8.3 %collective-permute-start.1 = (f32[8,4,128]{2,1,0:T(4,128)S(1)}, f32[8,4,128]{2,1,0:T(4,128)S(1)}, u32[]{:S(2)}, u32[]{:S(2)}) collective-permute-start(f32[8,4,128]{2,1,0:T(4,128)S(1)} %get-tuple-element.3), channel_id=1, source_target_pairs={{1,0},{2,1},{3,2},{0,3},{5,4},{6,5},{7,6},{4,7},{9,8},{10,9},{11,1... | collective-permute-start | bytes 49160 | tf_op jit(solution)/shard_map/ppermute | solution.py:21
  13.2 5.5 %collective-permute-start = (f32[8,4,128]{2,1,0:T(4,128)S(1)}, f32[8,4,128]{2,1,0:T(4,128)S(1)}, u32[]{:S(2)}, u32[]{:S(2)}) collective-permute-start(f32[8,4,128]{2,1,0:T(4,128)S(1)} %get-tuple-element.2), channel_id=1, source_target_pairs={{0,1},{1,2},{2,3},{3,0},{4,5},{5,6},{6,7},{7,4},{8,9},{9,10},{10,1... | collective-permute-start | bytes 49160 | tf_op jit(solution)/shard_map/ppermute | solution.py:18
  18.8 2.2 %copy-start.4 = (s32[1,1,1024]{2,1,0:T(1,128)S(1)}, s32[1,1,1024]{2,1,0:T(1,128)}, u32[]{:S(2)}) copy-start(s32[1,1,1024]{2,1,0:T(1,128)} %param.12) | copy-start | bytes 12292
  19.1 58.3 %copy-start.2 = (bf16[1,1,1024,128]{3,2,1,0:T(8,128)(2,1)S(1)}, bf16[1,1,1024,128]{3,2,1,0:T(8,128)(2,1)}, u32[]{:S(2)}) copy-start(bf16[1,1,1024,128]{3,2,1,0:T(8,128)(2,1)} %param.14) | copy-start | bytes 786436
  20.9 108.1 %reduce-scatter.2.cloned.1.call-start = ((), (), s32[]{:S(2)}) async-start(), calls=%async_computation.2 | async-start | bytes 147456 | tf_op jit(solution)/shard_map/reduce_scatter | solution.py:94
  74.5 7.4 %copy-start.5 = (bf16[2048,128]{1,0:T(8,128)(2,1)S(1)}, bf16[2048,128]{1,0:T(8,128)(2,1)}, u32[]{:S(2)}) copy-start(bf16[2048,128]{1,0:T(8,128)(2,1)} %param.19) | copy-start | bytes 1572868
  74.5 7.4 %copy-start.6 = (bf16[1,1,1024,128]{3,2,1,0:T(8,128)(2,1)S(1)}, bf16[1,1,1024,128]{3,2,1,0:T(8,128)(2,1)}, u32[]{:S(2)}) copy-start(bf16[1,1,1024,128]{3,2,1,0:T(8,128)(2,1)} %param.15) | copy-start | bytes 786436
  74.5 7.4 %copy-start.7 = (f32[2048]{0:T(1024)S(1)}, f32[2048]{0:T(1024)}, u32[]{:S(2)}) copy-start(f32[2048]{0:T(1024)} %param.18) | copy-start | bytes 24580
  78.7 3.2 %copy-start.1 = (f32[1024,2048]{1,0:T(8,128)}, f32[1024,2048]{1,0:T(8,128)S(1)}, u32[]{:S(2)}) copy-start(f32[1024,2048]{1,0:T(8,128)S(1)} %fusion.31) | copy-start | bytes 25165828
Sparse Core Ops, SparseCore 0:
  21.0 52.5 all-reduce.1
  96.0 32.9 reduce-scatter.1
where the time goes:
time: 136 us
  waiting for transfers between devices  87.5 us (64%)
  matrix products  15.2 us (11%)
  between operations  14.8 us (11%)
  local copies, waits for them, and re-layouts  7.49 us (6%)
  other arithmetic  5.53 us (4%)
  starting transfers between devices  5.21 us (4%)
    psum x1, waiting for transfers between devices, per_device(): whole_cols = lax.psum(partial_sum, 'mem') * scale  52.6 us
    reduce_scatter x1, waiting for transfers between devices, per_device(): lax.psum_scatter(gradient, 'mem', scatter_dimension=0, tiled=True)  32.5 us
    dot_general x1, matrix products, observe_block(): lax.dot_general(back_pre, w_in, (((1,), (1,)), ((), ())), preferred_eleme...  9.44 us
    ppermute x1, starting transfers between devices, padded_2(): lax.ppermute(lax.slice_in_dim(block, 0, width, axis=dim), axis, backward)  5.13 us
    unnamed x16, local copies, waits for them, and re-layouts  3.27 us
    dot_general x1, matrix products, observe_block(): outputs = jnp.dot(hidden_low, w_out, preferred_element_type=jnp.float32)  3.19 us
    gather x1, local copies, waits for them, and re-layouts, observe_block(): sampled = jnp.take(whole_cols, indices, axis=0)  2.81 us
  transfers between devices with their start and end apart: 4, of which 3 were waited for; matrix products, arithmetic and copies ran while one was open for 2% of the time, Pallas kernels for 0%

commit v1 on v0

--- a/solution.py
+++ b/solution.py
@@ -30,6 +30,48 @@
 def sweep(padded):
     middle = padded[:, 1:-1]
     return middle + diffusion * (padded[:, :-2] - 2.0 * middle + padded[:, 2:])
+
+
+def bit_swap(block, axis, bit):
+    count = lax.axis_size(axis)
+    return lax.ppermute(block, axis, [(i, i ^ bit) for i in range(count)])
+
+
+def pick(block, dim, which):
+    return lax.squeeze(lax.dynamic_slice_in_dim(block, which, 1, dim), (dim,))
+
+
+def reduce_whole(block, axis):
+    count = lax.axis_size(axis)
+    if count < 2 or count & (count - 1):
+        return lax.psum(block, axis)
+    core = lax.axis_index(axis) & 1
+    halves = block.reshape((2, block.shape[0] // 2) + block.shape[1:])
+    mine = pick(halves, 0, core) + bit_swap(pick(halves, 0, 1 - core), axis, 1)
+    bit = 2
+    while bit < count:
+        mine = mine + bit_swap(mine, axis, bit)
+        bit *= 2
+    other = bit_swap(mine, axis, 1)
+    low = jnp.where(core == 0, mine, other)
+    high = jnp.where(core == 0, other, mine)
+    return jnp.concatenate([low, high], axis=0)
+
+
+def reduce_owned(block, axis):
+    count = lax.axis_size(axis)
+    if count & (count - 1):
+        return lax.psum_scatter(block, axis, scatter_dimension=0, tiled=True)
+    me = lax.axis_index(axis)
+    owned = block.shape[0] // count
+    block = block.reshape((count, owned) + block.shape[1:])
+    bit = 1
+    while bit < count:
+        side = (me // bit) & 1
+        pairs = block.reshape((block.shape[0] // 2, 2) + block.shape[1:])
+        block = pick(pairs, 1, side) + bit_swap(pick(pairs, 1, 1 - side), axis, bit)
+        bit *= 2
+    return block.reshape(block.shape[1:])
 
 
 def observe_block(whole_cols, indices, live, background, targets, weights, w_in, b_in, w_out):
@@ -79,7 +121,7 @@
     members = perturb.shape[0] * lax.axis_size("mem")
     scale = (members - 1) ** (-0.5)
     owned = partial_sum.shape[0] // lax.axis_size("mem")
-    whole_cols = lax.psum(partial_sum, "mem") * scale
+    whole_cols = reduce_whole(partial_sum, "mem") * scale
     increment = lax.dynamic_slice_in_dim(whole_cols, lax.axis_index("mem") * owned, owned, 0)
     indices = obs_column.reshape(-1)
     background = obs_background.reshape(indices.shape[0], -1)
@@ -91,7 +133,7 @@
     gradient = observe_block(
         whole_cols, indices, live, background, targets, weights, w_in, b_in, w_out
     )
-    grad_columns = lax.psum_scatter(gradient, "mem", scatter_dimension=0, tiled=True)
+    grad_columns = reduce_owned(gradient, "mem")
     return (increment, grad_columns)
 
 

time: 136 us -> 55.9 us (0.41)
  waiting for transfers between devices: 87.5 us -> 16.8 us
  between operations: 14.8 us -> 1.55 us
  starting transfers between devices: 5.21 us -> 11.8 us
  other arithmetic: 5.53 us -> 3.27 us
    psum x1 -> x0, waiting for transfers between devices: 52.6 us -> none  [per_device(): whole_cols = lax.psum(partial_sum, 'mem') * scale]
    reduce_scatter x1 -> x0, waiting for transfers between devices: 32.5 us -> none  [per_device(): lax.psum_scatter(gradient, 'mem', scatter_dimension=0, tiled=True)]
    ppermute x0 -> x7, waiting for transfers between devices: none -> 12.4 us  [bit_swap(): return lax.ppermute(block, axis, [(i, i ^ bit) for i in range(count)])]
    ppermute x0 -> x7, starting transfers between devices: none -> 6.65 us  [bit_swap(): return lax.ppermute(block, axis, [(i, i ^ bit) for i in range(count)])]
    ppermute x1, waiting for transfers between devices: 2.37 us -> 4.09 us  [padded_2(): lax.ppermute(lax.slice_in_dim(block, block.shape[dim] - width, None, axis...]
    unnamed x16 -> x18, local copies, waits for them, and re-layouts: 3.27 us -> 3.27 us
  transfers between devices with their start and end apart: 4 -> 9, of which waited for: 3 -> 9; matrix products, arithmetic and copies ran while one was open for 2% -> 3% of each run, Pallas kernels for 0% -> 0%
where the time goes in v1:
time: 55.9 us; the launch traced here: 55.7 us
  waiting for transfers between devices  16.8 us (30%)
  matrix products  14.5 us (26%)
  starting transfers between devices  11.8 us (21%)
  local copies, waits for them, and re-layouts  7.75 us (14%)
  other arithmetic  3.27 us (6%)
  between operations  1.55 us (3%)
    ppermute x7, waiting for transfers between devices, bit_swap(): return lax.ppermute(block, axis, [(i, i ^ bit) for i in range(count)])  12.4 us
    dot_general x1, matrix products, observe_block(): lax.dot_general(back_pre, w_in, (((1,), (1,)), ((), ())), preferred_eleme...  9.45 us
    ppermute x7, starting transfers between devices, bit_swap(): return lax.ppermute(block, axis, [(i, i ^ bit) for i in range(count)])  6.65 us
    ppermute x1, starting transfers between devices, padded_2(): lax.ppermute(lax.slice_in_dim(block, 0, width, axis=dim), axis, backward)  5.12 us
    ppermute x1, waiting for transfers between devices, padded_2(): lax.ppermute(lax.slice_in_dim(block, block.shape[dim] - width, None, axis...  4.09 us
    unnamed x18, local copies, waits for them, and re-layouts  3.27 us
    dot_general x1, matrix products, observe_block(): outputs = jnp.dot(hidden_low, w_out, preferred_element_type=jnp.float32)  3.17 us
    gather x1, local copies, waits for them, and re-layouts, observe_block(): sampled = jnp.take(whole_cols, indices, axis=0)  2.99 us
  transfers between devices with their start and end apart: 9, of which 9 were waited for; matrix products, arithmetic and copies ran while one was open for 3% of the time, Pallas kernels for 0%

profile of v1, /device:TPU:0, one launch (start us, length us, event | category | flops | bytes accessed | tf_op | source)
XLA Modules:
  0.0 55.7 jit_solution(11524208020432214931)
XLA Ops:
  0.7 0.8 %fusion.48 = (f32[8,4,128]{2,1,0:T(4,128)S(1)}, f32[8,4,128]{2,1,0:T(4,128)S(1)}) fusion(bf16[8,256,128]{2,1,0:T(8,128)(2,1)} %param.10), kind=kLoop, calls=%fused_computation.75 | loop fusion | bytes 65536 | tf_op jit(solution)/shard_map/slice | solution.py:19
  1.5 5.1 %collective-permute-start.1 = (f32[8,4,128]{2,1,0:T(4,128)S(1)}, f32[8,4,128]{2,1,0:T(4,128)S(1)}, u32[]{:S(2)}, u32[]{:S(2)}) collective-permute-start(f32[8,4,128]{2,1,0:T(4,128)S(1)} %get-tuple-element.3), channel_id=1, source_target_pairs={{1,0},{2,1},{3,2},{0,3},{5,4},{6,5},{7,6},{4,7},{9,8},{10,9},{11,1... | collective-permute-start | bytes 49160 | tf_op jit(solution)/shard_map/ppermute | solution.py:21
  6.6 1.1 %convert_element_type.35 = f32[8,256,128]{2,1,0:T(8,128)S(1)} convert(bf16[8,256,128]{2,1,0:T(8,128)(2,1)} %param.10) | non-fusion elementwise | flops 262144 | bytes 1572864 | tf_op jit(solution)/shard_map/convert_element_type | solution.py:115
  8.0 4.1 %collective-permute-done = f32[8,4,128]{2,1,0:T(4,128)S(1)} collective-permute-done((f32[8,4,128]{2,1,0:T(4,128)S(1)}, f32[8,4,128]{2,1,0:T(4,128)S(1)}, u32[]{:S(2)}, u32[]{:S(2)}) %collective-permute-start) | collective-permute-done | bytes 16416 | tf_op jit(solution)/shard_map/ppermute | solution.py:18
  13.2 0.4 fusion.27
  13.8 1.2 %collective-permute-done.2 = f32[128,128]{1,0:T(8,128)S(1)} collective-permute-done((f32[128,128]{1,0:T(8,128)S(1)}, f32[128,128]{1,0:T(8,128)S(1)}, u32[]{:S(2)}, u32[]{:S(2)}) %collective-permute-start.2) | collective-permute-done | bytes 65568 | tf_op jit(solution)/shard_map/ppermute | solution.py:37
  15.0 1.6 %collective-permute-start.3 = (f32[128,128]{1,0:T(8,128)S(1)}, f32[128,128]{1,0:T(8,128)S(1)}, u32[]{:S(2)}, u32[]{:S(2)}) collective-permute-start(f32[128,128]{1,0:T(8,128)S(1)} %bitcast_add_fusion.1), channel_id=1, source_target_pairs={{0,8},{4,12},{8,0},{12,4},{16,24},{20,28},{24,16},{28,20},{1,9},{5... | collective-permute-start | bytes 196616 | tf_op jit(solution)/shard_map/ppermute | solution.py:37
  17.2 2.1 %collective-permute-done.3 = f32[128,128]{1,0:T(8,128)S(1)} collective-permute-done((f32[128,128]{1,0:T(8,128)S(1)}, f32[128,128]{1,0:T(8,128)S(1)}, u32[]{:S(2)}, u32[]{:S(2)}) %collective-permute-start.3) | collective-permute-done | bytes 65568 | tf_op jit(solution)/shard_map/ppermute | solution.py:37
  19.4 1.6 %collective-permute-start.4 = (f32[128,128]{1,0:T(8,128)S(1)}, f32[128,128]{1,0:T(8,128)S(1)}, u32[]{:S(2)}, u32[]{:S(2)}) collective-permute-start(f32[128,128]{1,0:T(8,128)S(1)} %add.122), channel_id=1, source_target_pairs={{0,16},{4,20},{8,24},{12,28},{16,0},{20,4},{24,8},{28,12},{1,17},{... | collective-permute-start | bytes 196616 | tf_op jit(solution)/shard_map/ppermute | solution.py:37
  21.0 2.7 %collective-permute-done.4 = f32[128,128]{1,0:T(8,128)S(1)} collective-permute-done((f32[128,128]{1,0:T(8,128)S(1)}, f32[128,128]{1,0:T(8,128)S(1)}, u32[]{:S(2)}, u32[]{:S(2)}) %collective-permute-start.4) | collective-permute-done | bytes 65568 | tf_op jit(solution)/shard_map/ppermute | solution.py:37
  23.8 1.2 %collective-permute-done.5 = f32[128,128]{1,0:T(8,128)S(1)} collective-permute-done((f32[128,128]{1,0:T(8,128)S(1)}, f32[128,128]{1,0:T(8,128)S(1)}, u32[]{:S(2)}, u32[]{:S(2)}) %collective-permute-start.5) | collective-permute-done | bytes 65568 | tf_op jit(solution)/shard_map/ppermute | solution.py:37
  25.1 3.0 %gather_fusion = f32[1024,128]{1,0:T(8,128)S(1)} fusion(f32[256,128]{1,0:T(8,128)S(1)} %maximum_multiply_fusion, s32[1024]{0:T(1024)S(1)} %broadcast_clamp_fusion), kind=kCustom, calls=%fused_computation | custom fusion | bytes 1052672 | tf_op jit(solution)/shard_map/jit(_take)/gather | solution.py:78
  28.1 1.3 %fusion.31 = f32[1024,2048]{1,0:T(8,128)S(1)} fusion(bf16[128,2048]{1,0:T(8,128)(2,1)S(1)} %copy-done, f32[1024,128]{1,0:T(8,128)S(1)} %gather_fusion, bf16[1,1,1024,128]{3,2,1,0:T(8,128)(2,1)S(1)} %copy-done.2, pred[1024]{0:T(1024)(128)(4,1)S(1)} %compare_and_fusion), kind=kOutput, calls=%fused_computation.42 | convolution fusion | flops 537395200 | bytes 9700352 | tf_op jit(solution)/shard_map/dot_general | solution.py:80
  29.4 3.2 %copy-done.1 = f32[1024,2048]{1,0:T(8,128)} copy-done((f32[1024,2048]{1,0:T(8,128)}, f32[1024,2048]{1,0:T(8,128)S(1)}, u32[]{:S(2)}) %copy-start.1) | copy-done | bytes 8388632
  32.7 3.2 %fusion.14 = bf16[1024,128]{1,0:T(8,128)(2,1)S(1)} fusion(bf16[2048,128]{1,0:T(8,128)(2,1)S(1)} %copy-done.6, f32[1024,2048]{1,0:T(8,128)S(1)} %fusion.31, f32[2048]{0:T(1024)S(1)} %copy-done.8, bf16[1,1,1024,128]{3,2,1,0:T(8,128)(2,1)S(1)} %copy-done.7, f32[1024]{0:T(1024)S(1)} %fusion.36), kind=kOutput, calls=%fused_computation.16 | convolution fusion | flops 558366720 | bytes 9449472 | tf_op jit(solution)/shard_map/dot_general | solution.py:83
  35.8 9.5 %fusion.15 = bf16[1024,128]{1,0:T(8,128)(2,1)S(1)} fusion(bf16[128,2048]{1,0:T(8,128)(2,1)S(1)} %copy-done, f32[1024,2048]{1,0:T(8,128)} %copy-done.1, f32[2048]{0:T(1024)S(1)} %copy-done.8, bf16[1024,128]{1,0:T(8,128)(2,1)S(1)} %fusion.14, bf16[2048,128]{1,0:T(8,128)(2,1)S(1)} %copy-done.6), kind=kOutput, calls=%fused_computation.17 | convolution fusion | flops 1117913088 | bytes 9969664 | tf_op jit(solution)/shard_map/dot_general | solution.py:92
  45.3 0.6 %fusion.28 = f32[256,128]{1,0:T(8,128)S(1)} fusion(bf16[1024,128]{1,0:T(8,128)(2,1)S(1)} %fusion.15, s32[1024]{0:T(1024)S(1)} %bitcast.46), kind=kOutput, calls=%fused_computation.38 | convolution fusion | flops 67371008 | bytes 397312 | tf_op jit(solution)/shard_map/dot_general | solution.py:98
  46.2 1.1 %collective-permute-done.6 = f32[4,32,128]{2,1,0:T(8,128)S(1)} collective-permute-done((f32[4,32,128]{2,1,0:T(8,128)S(1)}, f32[4,32,128]{2,1,0:T(8,128)S(1)}, u32[]{:S(2)}, u32[]{:S(2)}) %collective-permute-start.6) | collective-permute-done | bytes 65568 | tf_op jit(solution)/shard_map/ppermute | solution.py:37
  47.3 1.6 %collective-permute-start.7 = (f32[2,32,128]{2,1,0:T(8,128)S(1)}, f32[2,32,128]{2,1,0:T(8,128)S(1)}, u32[]{:S(2)}, u32[]{:S(2)}) collective-permute-start(f32[2,32,128]{2,1,0:T(8,128)S(1)} %dynamic-slice_bitcast_fusion.2), channel_id=1, source_target_pairs={{0,8},{4,12},{8,0},{12,4},{16,24},{20,28},{24,16},{28,20},{1,9},{5... | collective-permute-start | bytes 98312 | tf_op jit(solution)/shard_map/ppermute | solution.py:37
  48.9 2.4 %collective-permute-done.7 = f32[2,32,128]{2,1,0:T(8,128)S(1)} collective-permute-done((f32[2,32,128]{2,1,0:T(8,128)S(1)}, f32[2,32,128]{2,1,0:T(8,128)S(1)}, u32[]{:S(2)}, u32[]{:S(2)}) %collective-permute-start.7) | collective-permute-done | bytes 32800 | tf_op jit(solution)/shard_map/ppermute | solution.py:37
  51.3 1.6 %collective-permute-start.8 = (f32[1,32,128]{2,1,0:T(8,128)S(1)}, f32[1,32,128]{2,1,0:T(8,128)S(1)}, u32[]{:S(2)}, u32[]{:S(2)}) collective-permute-start(f32[1,32,128]{2,1,0:T(8,128)S(1)} %constant_dynamic-slice_fusion), channel_id=1, source_target_pairs={{0,16},{4,20},{8,24},{12,28},{16,0},{20,4},{24,8},{28,12},{1,17},{... | collective-permute-start | bytes 49160 | tf_op jit(solution)/shard_map/ppermute | solution.py:37
  52.9 0.6 %constant_dynamic-slice_fusion.1 = f32[32,128]{1,0:T(8,128)} fusion(f32[256,128]{1,0:T(8,128)S(1)} %maximum_multiply_fusion, s32[]{:T(128)S(6)} %select_n.69), kind=kLoop, calls=%fused_computation.62 | loop fusion | bytes 32772 | tf_op jit(solution)/shard_map/dynamic_slice | solution.py:125
  53.5 1.6 %collective-permute-done.8 = f32[1,32,128]{2,1,0:T(8,128)S(1)} collective-permute-done((f32[1,32,128]{2,1,0:T(8,128)S(1)}, f32[1,32,128]{2,1,0:T(8,128)S(1)}, u32[]{:S(2)}, u32[]{:S(2)}) %collective-permute-start.8) | collective-permute-done | bytes 16416 | tf_op jit(solution)/shard_map/ppermute | solution.py:37
  55.1 0.6 %add_bitcast_fusion = f32[32,128]{1,0:T(8,128)} fusion(f32[1,32,128]{2,1,0:T(8,128)S(1)} %collective-permute-done.8, f32[2,32,128]{2,1,0:T(8,128)S(1)} %bitcast_add_fusion.2, s32[]{:T(128)S(6)} %select_n.77), kind=kLoop, calls=%fused_computation.56 | loop fusion | flops 4096 | bytes 49156 | tf_op jit(solution)/shard_map/reshape | solution.py:74
  (41 shorter events, 1.9 us)
Async XLA Ops:
  0.6 27.5 %copy-start = (bf16[128,2048]{1,0:T(8,128)(2,1)S(1)}, bf16[128,2048]{1,0:T(8,128)(2,1)}, u32[]{:S(2)}) copy-start(bf16[128,2048]{1,0:T(8,128)(2,1)} %param.17) | copy-start | bytes 1572868
  0.6 12.6 %copy-start.3 = (bf16[8,256,128]{2,1,0:T(8,128)(2,1)S(1)}, bf16[8,256,128]{2,1,0:T(8,128)(2,1)}, u32[]{:S(2)}) copy-start(bf16[8,256,128]{2,1,0:T(8,128)(2,1)} %param.11) | copy-start | bytes 1572868
  1.5 6.6 %collective-permute-start.1 = (f32[8,4,128]{2,1,0:T(4,128)S(1)}, f32[8,4,128]{2,1,0:T(4,128)S(1)}, u32[]{:S(2)}, u32[]{:S(2)}) collective-permute-start(f32[8,4,128]{2,1,0:T(4,128)S(1)} %get-tuple-element.3), channel_id=1, source_target_pairs={{1,0},{2,1},{3,2},{0,3},{5,4},{6,5},{7,6},{4,7},{9,8},{10,9},{11,1... | collective-permute-start | bytes 49160 | tf_op jit(solution)/shard_map/ppermute | solution.py:21
  6.6 5.5 %collective-permute-start = (f32[8,4,128]{2,1,0:T(4,128)S(1)}, f32[8,4,128]{2,1,0:T(4,128)S(1)}, u32[]{:S(2)}, u32[]{:S(2)}) collective-permute-start(f32[8,4,128]{2,1,0:T(4,128)S(1)} %get-tuple-element.2), channel_id=1, source_target_pairs={{0,1},{1,2},{2,3},{3,0},{4,5},{5,6},{6,7},{7,4},{8,9},{9,10},{10,1... | collective-permute-start | bytes 49160 | tf_op jit(solution)/shard_map/ppermute | solution.py:18
  12.2 1.5 %copy-start.4 = (s32[1,1,1024]{2,1,0:T(1,128)S(1)}, s32[1,1,1024]{2,1,0:T(1,128)}, u32[]{:S(2)}) copy-start(s32[1,1,1024]{2,1,0:T(1,128)} %param.12) | copy-start | bytes 12292
  12.2 8.7 %copy-start.5 = (f32[1,1,1024]{2,1,0:T(1,128)S(1)}, f32[1,1,1024]{2,1,0:T(1,128)}, u32[]{:S(2)}) copy-start(f32[1,1,1024]{2,1,0:T(1,128)} %param.16) | copy-start | bytes 12292
  12.6 15.5 %copy-start.2 = (bf16[1,1,1024,128]{3,2,1,0:T(8,128)(2,1)S(1)}, bf16[1,1,1024,128]{3,2,1,0:T(8,128)(2,1)}, u32[]{:S(2)}) copy-start(bf16[1,1,1024,128]{3,2,1,0:T(8,128)(2,1)} %param.14) | copy-start | bytes 786436
  13.7 1.3 %collective-permute-start.2 = (f32[128,128]{1,0:T(8,128)S(1)}, f32[128,128]{1,0:T(8,128)S(1)}, u32[]{:S(2)}, u32[]{:S(2)}) collective-permute-start(f32[128,128]{1,0:T(8,128)S(1)} %dynamic-slice_bitcast_fusion.1), channel_id=1, source_target_pairs={{0,4},{4,0},{8,12},{12,8},{16,20},{20,16},{24,28},{28,24},{1,5},{5... | collective-permute-start | bytes 196616 | tf_op jit(solution)/shard_map/ppermute | solution.py:37
  15.0 4.3 %collective-permute-start.3 = (f32[128,128]{1,0:T(8,128)S(1)}, f32[128,128]{1,0:T(8,128)S(1)}, u32[]{:S(2)}, u32[]{:S(2)}) collective-permute-start(f32[128,128]{1,0:T(8,128)S(1)} %bitcast_add_fusion.1), channel_id=1, source_target_pairs={{0,8},{4,12},{8,0},{12,4},{16,24},{20,28},{24,16},{28,20},{1,9},{5... | collective-permute-start | bytes 196616 | tf_op jit(solution)/shard_map/ppermute | solution.py:37
  19.4 4.3 %collective-permute-start.4 = (f32[128,128]{1,0:T(8,128)S(1)}, f32[128,128]{1,0:T(8,128)S(1)}, u32[]{:S(2)}, u32[]{:S(2)}) collective-permute-start(f32[128,128]{1,0:T(8,128)S(1)} %add.122), channel_id=1, source_target_pairs={{0,16},{4,20},{8,24},{12,28},{16,0},{20,4},{24,8},{28,12},{1,17},{... | collective-permute-start | bytes 196616 | tf_op jit(solution)/shard_map/ppermute | solution.py:37
  23.7 1.3 %collective-permute-start.5 = (f32[128,128]{1,0:T(8,128)S(1)}, f32[128,128]{1,0:T(8,128)S(1)}, u32[]{:S(2)}, u32[]{:S(2)}) collective-permute-start(f32[128,128]{1,0:T(8,128)S(1)} %add.123), channel_id=1, source_target_pairs={{0,4},{4,0},{8,12},{12,8},{16,20},{20,16},{24,28},{28,24},{1,5},{5... | collective-permute-start | bytes 196616 | tf_op jit(solution)/shard_map/ppermute | solution.py:37
  25.1 7.6 %copy-start.6 = (bf16[2048,128]{1,0:T(8,128)(2,1)S(1)}, bf16[2048,128]{1,0:T(8,128)(2,1)}, u32[]{:S(2)}) copy-start(bf16[2048,128]{1,0:T(8,128)(2,1)} %param.19) | copy-start | bytes 1572868
  25.1 7.6 %copy-start.7 = (bf16[1,1,1024,128]{3,2,1,0:T(8,128)(2,1)S(1)}, bf16[1,1,1024,128]{3,2,1,0:T(8,128)(2,1)}, u32[]{:S(2)}) copy-start(bf16[1,1,1024,128]{3,2,1,0:T(8,128)(2,1)} %param.15) | copy-start | bytes 786436
  25.1 7.6 %copy-start.8 = (f32[2048]{0:T(1024)S(1)}, f32[2048]{0:T(1024)}, u32[]{:S(2)}) copy-start(f32[2048]{0:T(1024)} %param.18) | copy-start | bytes 24580
  29.4 3.2 %copy-start.1 = (f32[1024,2048]{1,0:T(8,128)}, f32[1024,2048]{1,0:T(8,128)S(1)}, u32[]{:S(2)}) copy-start(f32[1024,2048]{1,0:T(8,128)S(1)} %fusion.31) | copy-start | bytes 25165828
  46.0 1.3 %collective-permute-start.6 = (f32[4,32,128]{2,1,0:T(8,128)S(1)}, f32[4,32,128]{2,1,0:T(8,128)S(1)}, u32[]{:S(2)}, u32[]{:S(2)}) collective-permute-start(f32[4,32,128]{2,1,0:T(8,128)S(1)} %dynamic-slice_bitcast_fusion), channel_id=1, source_target_pairs={{0,4},{4,0},{8,12},{12,8},{16,20},{20,16},{24,28},{28,24},{1,5},{5... | collective-permute-start | bytes 196616 | tf_op jit(solution)/shard_map/ppermute | solution.py:37
  47.3 4.0 %collective-permute-start.7 = (f32[2,32,128]{2,1,0:T(8,128)S(1)}, f32[2,32,128]{2,1,0:T(8,128)S(1)}, u32[]{:S(2)}, u32[]{:S(2)}) collective-permute-start(f32[2,32,128]{2,1,0:T(8,128)S(1)} %dynamic-slice_bitcast_fusion.2), channel_id=1, source_target_pairs={{0,8},{4,12},{8,0},{12,4},{16,24},{20,28},{24,16},{28,20},{1,9},{5... | collective-permute-start | bytes 98312 | tf_op jit(solution)/shard_map/ppermute | solution.py:37
  51.3 3.8 %collective-permute-start.8 = (f32[1,32,128]{2,1,0:T(8,128)S(1)}, f32[1,32,128]{2,1,0:T(8,128)S(1)}, u32[]{:S(2)}, u32[]{:S(2)}) collective-permute-start(f32[1,32,128]{2,1,0:T(8,128)S(1)} %constant_dynamic-slice_fusion), channel_id=1, source_target_pairs={{0,16},{4,20},{8,24},{12,28},{16,0},{20,4},{24,8},{28,12},{1,17},{... | collective-permute-start | bytes 49160 | tf_op jit(solution)/shard_map/ppermute | solution.py:37

commit v2 on v0

v2 whole, which is shorter than its diff:
```python
import functools

import jax
import jax.numpy as jnp
from jax import lax
from jax.experimental import pallas as pl
from jax.experimental.pallas import tpu as pltpu
from jax.sharding import PartitionSpec as P

SWEEPS = 4


diffusion = 0.4
GELU_ROOT = 0.7978845608028654
GELU_CUBE = 0.044715

def padded_2(block, sides, width):
    for axis, dim in sides:
        count = lax.axis_size(axis)
        forward = [(i, i + 1) for i in range(count - 1)]
        forward.append((count - 1, 0))
        backward = [(target, source) for source, target in forward]
        low = lax.ppermute(
            lax.slice_in_dim(block, block.shape[dim] - width, None, axis=dim), axis, forward
        )
        high = lax.ppermute(lax.slice_in_dim(block, 0, width, axis=dim), axis, backward)
        block = jnp.concatenate([low, block, high], axis=dim)
    return block


def sweep(padded):
    middle = padded[:, 1:-1]
    return middle + diffusion * (padded[:, :-2] - 2.0 * middle + padded[:, 2:])


def pair_swap(block, axis, low_bit, high_bit):
    count = lax.axis_size(axis)
    pairs = [(i, i ^ (high_bit if i & 1 else low_bit)) for i in range(count)]
    return lax.ppermute(block, axis, pairs)


def pick(block, dim, which):
    return lax.squeeze(lax.dynamic_slice_in_dim(block, which, 1, dim), (dim,))


def chip_bits(count):
    return [1 << step for step in range(1, count.bit_length() - 1)]


def reduce_pairs(block, axis):
    count = lax.axis_size(axis)
    core = lax.axis_index(axis) & 1
    sides = block.reshape((count // 2, 2, block.shape[0] // count) + block.shape[1:])
    mine = pick(sides, 1, core) + pair_swap(pick(sides, 1, 1 - core), axis, 1, 1)
    bits = chip_bits(count)
    for low_bit, high_bit in zip(bits, bits[::-1]):
        mine = mine + pair_swap(mine, axis, low_bit, high_bit)
    mine = mine.reshape((-1,) + block.shape[1:])
    return mine, pair_swap(mine, axis, 1, 1)


def scatter_pairs(keep, send, axis):
    count = lax.axis_size(axis)
    me = lax.axis_index(axis)
    block = keep + pair_swap(send, axis, 1, 1)
    for bit in chip_bits(count):
        side = (me // bit) & 1
        halves = block.reshape((-1, 2) + keep.shape[1:])
        block = pick(halves, 1, side) + pair_swap(pick(halves, 1, 1 - side), axis, bit, bit)
    return block.reshape(keep.shape[1:])


def observe_kernel(
    mine, other, indices, weights, background, targets, w_in, b_in, w_out, keep, send, slope, *, scale, block, chunk
):
    slots, levels = background.shape
    half_columns = mine.shape[0]
    columns = 2 * half_columns
    hidden = w_in.shape[1]
    increment = jnp.concatenate([mine[...], other[...]], axis=0) * scale
    top = increment.astype(jnp.bfloat16)
    rest = (increment - top.astype(jnp.float32)).astype(jnp.bfloat16)
    table = jnp.concatenate([top, rest], axis=1)

    def start(index):
        base = index * block
        row = indices[0:1, base:base + block]
        across = lax.broadcasted_iota(jnp.int32, (columns, block), 0) == row
        picked = across.astype(jnp.float32).astype(jnp.bfloat16)
        pair = lax.dot_general(picked, table, (((0,), (0,)), ((), ())), preferred_element_type=jnp.float32)
        sampled = pair[:, :levels] + pair[:, levels:]
        inputs = (background[base:base + block, :].astype(jnp.float32) + sampled).astype(jnp.bfloat16)
        return dict(base=base, slot=index % 2, picked=picked, inputs=inputs, outputs=None, back=None)

    def forward(st, c):
        sl = slice(c, c + chunk)
        pre = jnp.dot(st["inputs"], w_in[:, sl], preferred_element_type=jnp.float32) + b_in[0:1, sl]
        square = pre * pre
        bend = jnp.tanh(pre * (GELU_ROOT + GELU_ROOT * GELU_CUBE * square))
        half = 0.5 * pre
        lift = 1.0 + bend
        st_hidden = (half * lift).astype(jnp.bfloat16)
        rise = GELU_ROOT + 3.0 * GELU_ROOT * GELU_CUBE * square
        tilt = lift * (0.5 + half * ((1.0 - bend) * rise))
        slope[st["slot"], :, sl] = tilt
        part = jnp.dot(st_hidden, w_out[sl, :], preferred_element_type=jnp.float32)
        st["outputs"] = part if st["outputs"] is None else st["outputs"] + part

    def middle(st):
        base = st["base"]
        row = weights[0:1, base:base + block]
        col = jnp.transpose(jnp.broadcast_to(row, (targets.shape[1], block)))
        st["misfit"] = ((st["outputs"] - targets[base:base + block, :].astype(jnp.float32)) * col).astype(jnp.bfloat16)

    def backward(st, c):
        sl = slice(c, c + chunk)
        back = lax.dot_general(st["misfit"], w_out[sl, :], (((1,), (1,)), ((), ())), preferred_element_type=jnp.float32)
        back = (back * slope[st["slot"], :, sl]).astype(jnp.bfloat16)
        part = lax.dot_general(back, w_in[:, sl], (((1,), (1,)), ((), ())), preferred_element_type=jnp.float32)
        st["back"] = part if st["back"] is None else st["back"] + part

    def finish(st, total):
        part = jnp.dot(st["picked"], st["back"].astype(jnp.bfloat16), preferred_element_type=jnp.float32)
        return part if total is None else total + part

    blocks = slots // block
    total = None
    behind = None
    for index in range(blocks + 1):
        ahead = start(index) if index < blocks else None
        for c in range(0, hidden, chunk):
            if ahead is not None:
                forward(ahead, c)
            if behind is not None:
                backward(behind, c)
        if behind is not None:
            total = finish(behind, total)
        if ahead is not None:
            middle(ahead)
        behind = ahead
    keep[...] = total[:half_columns]
    send[...] = total[half_columns:]


def largest_part(size, limit):
    part = min(size, limit)
    while size % part:
        part -= 1
    return part


def observe_call(mine, other, indices, weights, background, targets, w_in, b_in, w_out, scale):
    vm = pl.BlockSpec(memory_space=pltpu.VMEM)
    block = largest_part(background.shape[0], 512)
    chunk = largest_part(w_in.shape[1], 256)
    half = jax.ShapeDtypeStruct(mine.shape, jnp.float32)
    return pl.pallas_call(
        functools.partial(observe_kernel, scale=scale, block=block, chunk=chunk),
        out_shape=(half, half),
        in_specs=[vm] * 9,
        out_specs=(vm, vm),
        scratch_shapes=[pltpu.VMEM((2, block, w_in.shape[1]), jnp.float32)],
        name="observe",
    )(mine, other, indices, weights, background, targets, w_in, b_in, w_out)


def per_device(
    control,
    perturb,
    obs_column,
    obs_count,
    obs_background,
    obs_value,
    obs_weight,
    w_in,
    b_in,
    w_out,
):
    field = control.astype(jnp.float32)
    padded = padded_2(field, (("sub", 1),), SWEEPS)
    for sweep_index in range(SWEEPS):
        padded = sweep(padded)
    field = padded
    partial_sum = jnp.sum(field * perturb.astype(jnp.float32), axis=0)
    members = perturb.shape[0] * lax.axis_size("mem")
    scale = (members - 1) ** (-0.5)
    count = lax.axis_size("mem")
    me = lax.axis_index("mem")
    columns = partial_sum.shape[0]
    owned = columns // count
    indices = obs_column.reshape(1, -1)
    slots = indices.shape[1]
    paired = count > 1 and count & (count - 1) == 0
    if paired:
        owner = indices // owned
        side = ((owner ^ me) & 1) * (columns // 2)
        indices = side + (owner // 2) * owned + indices % owned
        mine, other = reduce_pairs(partial_sum, "mem")
        increment = pick(mine.reshape(count // 2, owned, -1), 0, me // 2) * scale
    else:
        summed = lax.psum(partial_sum, "mem")
        mine, other = summed[: columns // 2], summed[columns // 2 :]
        increment = lax.dynamic_slice_in_dim(summed, me * owned, owned, 0) * scale
    slot_ids = lax.broadcasted_iota(jnp.int32, (1, slots), 1)
    live = (slot_ids < obs_count.reshape(())).astype(jnp.float32)
    keep, send = observe_call(
        mine,
        other,
        indices,
        obs_weight.reshape(1, slots) * live,
        obs_background.reshape(slots, -1),
        obs_value.reshape(slots, -1),
        w_in,
        b_in.reshape(1, -1),
        w_out,
        scale,
    )
    if paired:
        halves = (count // 2, owned, keep.shape[1])
        grad_columns = scatter_pairs(keep.reshape(halves), send.reshape(halves), "mem")
    else:
        gradient = jnp.concatenate([keep, send], axis=0)
        grad_columns = lax.psum_scatter(gradient, "mem", scatter_dimension=0, tiled=True)
    return (increment, grad_columns)


def solution(mesh):
    return jax.shard_map(
        per_device,
        mesh=mesh,
        in_specs=(
            P("mem", "sub", None),
            P("mem", "sub", None),
            P("mem", "sub", None),
            P("mem", "sub"),
            P("mem", "sub", None, None),
            P("mem", "sub", None, None),
            P("mem", "sub", None),
            P(),
            P(),
            P(),
        ),
        out_specs=(P(("sub", "mem"), None), P(("sub", "mem"), None)),
        check_vma=False,
    )
```

time: 136 us -> 46.8 us (0.34)
  waiting for transfers between devices: 87.5 us -> 15.1 us
  matrix products: 15.2 us -> 0 us
  between operations: 14.8 us -> 1.4 us
  Pallas kernels: 0 us -> 9.39 us
  starting transfers between devices: 5.21 us -> 11.7 us
  local copies, waits for them, and re-layouts: 7.49 us -> 2.13 us
    psum x1 -> x0, waiting for transfers between devices: 52.6 us -> none  [per_device(): whole_cols = lax.psum(partial_sum, 'mem') * scale]
    reduce_scatter x1 -> x0, waiting for transfers between devices: 32.5 us -> none  [per_device(): lax.psum_scatter(gradient, 'mem', scatter_dimension=0, tiled=True)]
    dot_general x4 -> x0, matrix products: 15.2 us -> none  [the longest x1 9.44 us: observe_block(): lax.dot_general(back_pre, w_in, (((1,), (1,)), ((), ())), preferred_eleme...]
    ppermute x0 -> x7, waiting for transfers between devices: none -> 10.7 us  [pair_swap(): return lax.ppermute(block, axis, pairs)]
    pallas_call x0 -> x1, Pallas kernels: none -> 9.39 us  [observe_call(): pl.pallas_call(functools.partial(observe_kernel, scale=scale, block=block...]
    ppermute x0 -> x7, starting transfers between devices: none -> 6.58 us  [pair_swap(): return lax.ppermute(block, axis, pairs)]
    gather x1 -> x0, local copies, waits for them, and re-layouts: 2.81 us -> none  [observe_block(): sampled = jnp.take(whole_cols, indices, axis=0)]
    unnamed x16 -> x10, local copies, waits for them, and re-layouts: 3.27 us -> 1.35 us
  transfers between devices with their start and end apart: 4 -> 9, of which waited for: 3 -> 9; matrix products, arithmetic and copies ran while one was open for 2% -> 8% of each run, Pallas kernels for 0% -> 0%
where the time goes in v2:
time: 46.8 us; the launch traced here: 46.4 us
  waiting for transfers between devices  15.1 us (32%)
  starting transfers between devices  11.7 us (25%)
  Pallas kernels  9.39 us (20%)
  other arithmetic  6.63 us (14%)
  local copies, waits for them, and re-layouts  2.13 us (5%)
  between operations  1.4 us (3%)
    ppermute x7, waiting for transfers between devices, pair_swap(): return lax.ppermute(block, axis, pairs)  10.7 us
    pallas_call x1, Pallas kernels, observe_call(): pl.pallas_call(functools.partial(observe_kernel, scale=scale, block=block...  9.39 us
    ppermute x7, starting transfers between devices, pair_swap(): return lax.ppermute(block, axis, pairs)  6.58 us
    ppermute x1, starting transfers between devices, padded_2(): lax.ppermute(lax.slice_in_dim(block, 0, width, axis=dim), axis, backward)  5.12 us
    ppermute x1, waiting for transfers between devices, padded_2(): lax.ppermute(lax.slice_in_dim(block, block.shape[dim] - width, None, axis...  4.09 us
    unnamed x10, local copies, waits for them, and re-layouts  1.35 us
    mul x1, other arithmetic, per_device(): increment = pick(mine.reshape(count // 2, owned, -1), 0, me // 2) * scale  1.32 us
    convert_element_type x1, other arithmetic, per_device(): field = control.astype(jnp.float32)  1.11 us
  transfers between devices with their start and end apart: 9, of which 9 were waited for; matrix products, arithmetic and copies ran while one was open for 8% of the time, Pallas kernels for 0%

profile of v2, /device:TPU:0, one launch (start us, length us, event | category | flops | bytes accessed | tf_op | source)
XLA Modules:
  0.0 46.4 jit_solution(4216155013201905020)
XLA Ops:
  0.6 0.7 %fusion.11 = (f32[8,4,128]{2,1,0:T(4,128)S(1)}, f32[8,4,128]{2,1,0:T(4,128)S(1)}) fusion(bf16[8,256,128]{2,1,0:T(8,128)(2,1)} %param.10), kind=kLoop, calls=%fused_computation.38 | loop fusion | bytes 65536 | tf_op jit(solution)/shard_map/slice | solution.py:24
  1.4 5.1 %collective-permute-start.1 = (f32[8,4,128]{2,1,0:T(4,128)S(1)}, f32[8,4,128]{2,1,0:T(4,128)S(1)}, u32[]{:S(2)}, u32[]{:S(2)}) collective-permute-start(f32[8,4,128]{2,1,0:T(4,128)S(1)} %get-tuple-element.7), channel_id=1, source_target_pairs={{1,0},{2,1},{3,2},{0,3},{5,4},{6,5},{7,6},{4,7},{9,8},{10,9},{11,1... | collective-permute-start | bytes 49160 | tf_op jit(solution)/shard_map/ppermute | solution.py:26
  6.5 1.1 %convert_element_type.7 = f32[8,256,128]{2,1,0:T(8,128)S(1)} convert(bf16[8,256,128]{2,1,0:T(8,128)(2,1)} %param.10) | non-fusion elementwise | flops 262144 | bytes 1572864 | tf_op jit(solution)/shard_map/convert_element_type | solution.py:179
  7.9 4.1 %collective-permute-done = f32[8,4,128]{2,1,0:T(4,128)S(1)} collective-permute-done((f32[8,4,128]{2,1,0:T(4,128)S(1)}, f32[8,4,128]{2,1,0:T(4,128)S(1)}, u32[]{:S(2)}, u32[]{:S(2)}) %collective-permute-start) | collective-permute-done | bytes 16416 | tf_op jit(solution)/shard_map/ppermute | solution.py:23
  13.1 0.7 %copy-done = bf16[8,256,128]{2,1,0:T(8,128)(2,1)S(1)} copy-done((bf16[8,256,128]{2,1,0:T(8,128)(2,1)S(1)}, bf16[8,256,128]{2,1,0:T(8,128)(2,1)}, u32[]{:S(2)}) %copy-start) | copy-done | bytes 524312
  13.8 0.4 fusion.9
  14.3 1.2 %collective-permute-done.2 = f32[4,32,128]{2,1,0:T(8,128)S(1)} collective-permute-done((f32[4,32,128]{2,1,0:T(8,128)S(1)}, f32[4,32,128]{2,1,0:T(8,128)S(1)}, u32[]{:S(2)}, u32[]{:S(2)}) %collective-permute-start.2) | collective-permute-done | bytes 65568 | tf_op jit(solution)/shard_map/ppermute | solution.py:39
  15.6 1.6 %collective-permute-start.3 = (f32[4,32,128]{2,1,0:T(8,128)S(1)}, f32[4,32,128]{2,1,0:T(8,128)S(1)}, u32[]{:S(2)}, u32[]{:S(2)}) collective-permute-start(f32[4,32,128]{2,1,0:T(8,128)S(1)} %bitcast_add_fusion), channel_id=1, source_target_pairs={{0,8},{4,20},{8,0},{12,28},{16,24},{20,4},{24,16},{28,12},{1,9},{5... | collective-permute-start | bytes 196616 | tf_op jit(solution)/shard_map/ppermute | solution.py:39
  17.1 2.8 %collective-permute-done.3 = f32[4,32,128]{2,1,0:T(8,128)S(1)} collective-permute-done((f32[4,32,128]{2,1,0:T(8,128)S(1)}, f32[4,32,128]{2,1,0:T(8,128)S(1)}, u32[]{:S(2)}, u32[]{:S(2)}) %collective-permute-start.3) | collective-permute-done | bytes 65568 | tf_op jit(solution)/shard_map/ppermute | solution.py:39
  19.9 1.6 %collective-permute-start.4 = (f32[4,32,128]{2,1,0:T(8,128)S(1)}, f32[4,32,128]{2,1,0:T(8,128)S(1)}, u32[]{:S(2)}, u32[]{:S(2)}) collective-permute-start(f32[4,32,128]{2,1,0:T(8,128)S(1)} %add.125), channel_id=1, source_target_pairs={{0,16},{4,12},{8,24},{12,4},{16,0},{20,28},{24,8},{28,20},{1,17},{... | collective-permute-start | bytes 196616 | tf_op jit(solution)/shard_map/ppermute | solution.py:39
  21.5 0.7 %fusion.10.indices = s32[1,1024]{1,0:T(1,128)} fusion(s32[1,1,1024]{2,1,0:T(1,128)S(1)} %copy-done.3, s32[]{:T(128)S(6)} %axis_index.11), kind=kLoop, calls=%fused_computation.35 | loop fusion | flops 40960 | bytes 8196 | tf_op jit(solution)/shard_map/add | solution.py:197
  22.8 1.4 %collective-permute-done.4 = f32[4,32,128]{2,1,0:T(8,128)S(1)} collective-permute-done((f32[4,32,128]{2,1,0:T(8,128)S(1)}, f32[4,32,128]{2,1,0:T(8,128)S(1)}, u32[]{:S(2)}, u32[]{:S(2)}) %collective-permute-start.4) | collective-permute-done | bytes 65568 | tf_op jit(solution)/shard_map/ppermute | solution.py:39
  24.4 0.6 %compare_select_fusion.weights = f32[1,1024]{1,0:T(1,128)} fusion(f32[1,1,1024]{2,1,0:T(1,128)S(1)} %copy-done.4, s32[]{:T(128)} %bitcast.40), kind=kLoop, calls=%fused_computation.25 | loop fusion | flops 2048 | bytes 8196 | tf_op jit(solution)/shard_map/mul | solution.py:210
  25.0 0.6 %collective-permute-done.5.other = f32[128,128]{1,0:T(8,128)S(1)} collective-permute-done((f32[128,128]{1,0:T(8,128)S(1)}, f32[128,128]{1,0:T(8,128)S(1)}, u32[]{:S(2)}, u32[]{:S(2)}) %collective-permute-start.5) | collective-permute-done | bytes 65568 | tf_op jit(solution)/shard_map/ppermute | solution.py:39
  25.6 0.6 %copy-done.2 = f32[128,128]{1,0:T(8,128)} copy-done((f32[128,128]{1,0:T(8,128)}, f32[128,128]{1,0:T(8,128)S(1)}, u32[]{:S(2)}) %copy-start.2) | copy-done | bytes 65560
  26.2 9.4 %observe.1 = (f32[128,128]{1,0:T(8,128)}, f32[128,128]{1,0:T(8,128)}) custom-call(f32[128,128]{1,0:T(8,128)} %bitcast.44, f32[128,128]{1,0:T(8,128)} %copy-done.2, s32[1,1024]{1,0:T(1,128)} %fusion.10.indices, f32[1,1024]{1,0:T(1,128)} %compare_select_fusion.weights, bf16[1024,128]{1,0:T(8,128)(2,1)} %bitcast.47, bf16[1024,128]{1,0:T(8,128)(2,1)} %bitcast.48, ...), custom_call_target="tpu_custom_call" | custom-call | tf_op jit(solution)/shard_map/observe/pallas_call | solution.py:157
  35.8 1.3 %collective-permute-done.6 = f32[4,32,128]{2,1,0:T(8,128)S(1)} collective-permute-done((f32[4,32,128]{2,1,0:T(8,128)}, f32[4,32,128]{2,1,0:T(8,128)S(1)}, u32[]{:S(2)}, u32[]{:S(2)}) %collective-permute-start.6) | collective-permute-done | bytes 65568 | tf_op jit(solution)/shard_map/ppermute | solution.py:39
  37.1 0.8 %add.131 = f32[4,32,128]{2,1,0:T(8,128)S(1)} add(f32[4,32,128]{2,1,0:T(8,128)} %bitcast.49, f32[4,32,128]{2,1,0:T(8,128)S(1)} %collective-permute-done.6) | non-fusion elementwise | flops 16384 | bytes 196608 | tf_op jit(solution)/shard_map/add | solution.py:65
  38.0 1.6 %collective-permute-start.7 = (f32[2,32,128]{2,1,0:T(8,128)S(1)}, f32[2,32,128]{2,1,0:T(8,128)S(1)}, u32[]{:S(2)}, u32[]{:S(2)}) collective-permute-start(f32[2,32,128]{2,1,0:T(8,128)S(1)} %dynamic-slice_bitcast_fusion.1), channel_id=1, source_target_pairs={{0,8},{4,12},{8,0},{12,4},{16,24},{20,28},{24,16},{28,20},{1,9},{5... | collective-permute-start | bytes 98312 | tf_op jit(solution)/shard_map/ppermute | solution.py:39
  39.5 2.4 %collective-permute-done.7 = f32[2,32,128]{2,1,0:T(8,128)S(1)} collective-permute-done((f32[2,32,128]{2,1,0:T(8,128)S(1)}, f32[2,32,128]{2,1,0:T(8,128)S(1)}, u32[]{:S(2)}, u32[]{:S(2)}) %collective-permute-start.7) | collective-permute-done | bytes 32800 | tf_op jit(solution)/shard_map/ppermute | solution.py:39
  42.0 1.6 %collective-permute-start.8 = (f32[1,32,128]{2,1,0:T(8,128)S(1)}, f32[1,32,128]{2,1,0:T(8,128)S(1)}, u32[]{:S(2)}, u32[]{:S(2)}) collective-permute-start(f32[1,32,128]{2,1,0:T(8,128)S(1)} %constant_dynamic-slice_fusion), channel_id=1, source_target_pairs={{0,16},{4,20},{8,24},{12,28},{16,0},{20,4},{24,8},{28,12},{1,17},{... | collective-permute-start | bytes 49160 | tf_op jit(solution)/shard_map/ppermute | solution.py:39
  43.5 1.3 %multiply_bitcast_fusion = f32[32,128]{1,0:T(8,128)} fusion(f32[4,32,128]{2,1,0:T(8,128)} %copy-done.1, s32[]{:T(128)S(6)} %select_n.71), kind=kLoop, calls=%fused_computation.24 | loop fusion | flops 4096 | bytes 32772 | tf_op jit(solution)/shard_map/mul | solution.py:199
  44.9 0.9 %collective-permute-done.8 = f32[1,32,128]{2,1,0:T(8,128)S(1)} collective-permute-done((f32[1,32,128]{2,1,0:T(8,128)S(1)}, f32[1,32,128]{2,1,0:T(8,128)S(1)}, u32[]{:S(2)}, u32[]{:S(2)}) %collective-permute-start.8) | collective-permute-done | bytes 16416 | tf_op jit(solution)/shard_map/ppermute | solution.py:39
  45.8 0.6 %add_bitcast_fusion = f32[32,128]{1,0:T(8,128)} fusion(f32[1,32,128]{2,1,0:T(8,128)S(1)} %collective-permute-done.8, f32[2,32,128]{2,1,0:T(8,128)S(1)} %bitcast_add_fusion.1, s32[]{:T(128)S(6)} %select_n.78), kind=kLoop, calls=%fused_computation.23 | loop fusion | flops 4096 | bytes 49156 | tf_op jit(solution)/shard_map/reshape | solution.py:70
  (24 shorter events, 1.7 us)
Async XLA Ops:
  1.4 6.6 %collective-permute-start.1 = (f32[8,4,128]{2,1,0:T(4,128)S(1)}, f32[8,4,128]{2,1,0:T(4,128)S(1)}, u32[]{:S(2)}, u32[]{:S(2)}) collective-permute-start(f32[8,4,128]{2,1,0:T(4,128)S(1)} %get-tuple-element.7), channel_id=1, source_target_pairs={{1,0},{2,1},{3,2},{0,3},{5,4},{6,5},{7,6},{4,7},{9,8},{10,9},{11,1... | collective-permute-start | bytes 49160 | tf_op jit(solution)/shard_map/ppermute | solution.py:26
  6.5 5.5 %collective-permute-start = (f32[8,4,128]{2,1,0:T(4,128)S(1)}, f32[8,4,128]{2,1,0:T(4,128)S(1)}, u32[]{:S(2)}, u32[]{:S(2)}) collective-permute-start(f32[8,4,128]{2,1,0:T(4,128)S(1)} %get-tuple-element.6), channel_id=1, source_target_pairs={{0,1},{1,2},{2,3},{3,0},{4,5},{5,6},{6,7},{7,4},{8,9},{9,10},{10,1... | collective-permute-start | bytes 49160 | tf_op jit(solution)/shard_map/ppermute | solution.py:23
  12.8 1.0 %copy-start = (bf16[8,256,128]{2,1,0:T(8,128)(2,1)S(1)}, bf16[8,256,128]{2,1,0:T(8,128)(2,1)}, u32[]{:S(2)}) copy-start(bf16[8,256,128]{2,1,0:T(8,128)(2,1)} %param.11) | copy-start | bytes 1572868
  13.8 7.7 %copy-start.3 = (s32[1,1,1024]{2,1,0:T(1,128)S(1)}, s32[1,1,1024]{2,1,0:T(1,128)}, u32[]{:S(2)}) copy-start(s32[1,1,1024]{2,1,0:T(1,128)} %param.12) | copy-start | bytes 12292
  13.8 10.6 %copy-start.4 = (f32[1,1,1024]{2,1,0:T(1,128)S(1)}, f32[1,1,1024]{2,1,0:T(1,128)}, u32[]{:S(2)}) copy-start(f32[1,1,1024]{2,1,0:T(1,128)} %param.16) | copy-start | bytes 12292
  14.2 1.3 %collective-permute-start.2 = (f32[4,32,128]{2,1,0:T(8,128)S(1)}, f32[4,32,128]{2,1,0:T(8,128)S(1)}, u32[]{:S(2)}, u32[]{:S(2)}) collective-permute-start(f32[4,32,128]{2,1,0:T(8,128)S(1)} %dynamic-slice_bitcast_fusion), channel_id=1, source_target_pairs={{0,4},{4,0},{8,12},{12,8},{16,20},{20,16},{24,28},{28,24},{1,5},{5... | collective-permute-start | bytes 196616 | tf_op jit(solution)/shard_map/ppermute | solution.py:39
  15.6 4.3 %collective-permute-start.3 = (f32[4,32,128]{2,1,0:T(8,128)S(1)}, f32[4,32,128]{2,1,0:T(8,128)S(1)}, u32[]{:S(2)}, u32[]{:S(2)}) collective-permute-start(f32[4,32,128]{2,1,0:T(8,128)S(1)} %bitcast_add_fusion), channel_id=1, source_target_pairs={{0,8},{4,20},{8,0},{12,28},{16,24},{20,4},{24,16},{28,12},{1,9},{5... | collective-permute-start | bytes 196616 | tf_op jit(solution)/shard_map/ppermute | solution.py:39
  19.9 4.3 %collective-permute-start.4 = (f32[4,32,128]{2,1,0:T(8,128)S(1)}, f32[4,32,128]{2,1,0:T(8,128)S(1)}, u32[]{:S(2)}, u32[]{:S(2)}) collective-permute-start(f32[4,32,128]{2,1,0:T(8,128)S(1)} %add.125), channel_id=1, source_target_pairs={{0,16},{4,12},{8,24},{12,4},{16,0},{20,28},{24,8},{28,20},{1,17},{... | collective-permute-start | bytes 196616 | tf_op jit(solution)/shard_map/ppermute | solution.py:39
  24.3 1.3 %copy-start.1 = (f32[4,32,128]{2,1,0:T(8,128)}, f32[4,32,128]{2,1,0:T(8,128)S(1)}, u32[]{:S(2)}) copy-start(f32[4,32,128]{2,1,0:T(8,128)S(1)} %add.126) | copy-start | bytes 196612
  24.3 1.3 %collective-permute-start.5 = (f32[128,128]{1,0:T(8,128)S(1)}, f32[128,128]{1,0:T(8,128)S(1)}, u32[]{:S(2)}, u32[]{:S(2)}) collective-permute-start(f32[128,128]{1,0:T(8,128)S(1)} %bitcast.43), channel_id=1, source_target_pairs={{0,4},{4,0},{8,12},{12,8},{16,20},{20,16},{24,28},{28,24},{1,5},{5... | collective-permute-start | bytes 196616 | tf_op jit(solution)/shard_map/ppermute | solution.py:39
  25.6 0.6 %copy-start.2 = (f32[128,128]{1,0:T(8,128)}, f32[128,128]{1,0:T(8,128)S(1)}, u32[]{:S(2)}) copy-start(f32[128,128]{1,0:T(8,128)S(1)} %collective-permute-done.5.other) | copy-start | bytes 196612
  35.6 1.5 %collective-permute-start.6 = (f32[4,32,128]{2,1,0:T(8,128)}, f32[4,32,128]{2,1,0:T(8,128)S(1)}, u32[]{:S(2)}, u32[]{:S(2)}) collective-permute-start(f32[4,32,128]{2,1,0:T(8,128)} %bitcast.51), channel_id=1, source_target_pairs={{0,4},{4,0},{8,12},{12,8},{16,20},{20,16},{24,28},{28,24},{1,5},{5... | collective-permute-start | bytes 196616 | tf_op jit(solution)/shard_map/ppermute | solution.py:39
  38.0 4.0 %collective-permute-start.7 = (f32[2,32,128]{2,1,0:T(8,128)S(1)}, f32[2,32,128]{2,1,0:T(8,128)S(1)}, u32[]{:S(2)}, u32[]{:S(2)}) collective-permute-start(f32[2,32,128]{2,1,0:T(8,128)S(1)} %dynamic-slice_bitcast_fusion.1), channel_id=1, source_target_pairs={{0,8},{4,12},{8,0},{12,4},{16,24},{20,28},{24,16},{28,20},{1,9},{5... | collective-permute-start | bytes 98312 | tf_op jit(solution)/shard_map/ppermute | solution.py:39
  42.0 3.8 %collective-permute-start.8 = (f32[1,32,128]{2,1,0:T(8,128)S(1)}, f32[1,32,128]{2,1,0:T(8,128)S(1)}, u32[]{:S(2)}, u32[]{:S(2)}) collective-permute-start(f32[1,32,128]{2,1,0:T(8,128)S(1)} %constant_dynamic-slice_fusion), channel_id=1, source_target_pairs={{0,16},{4,20},{8,24},{12,28},{16,0},{20,4},{24,8},{28,12},{1,17},{... | collective-permute-start | bytes 49160 | tf_op jit(solution)/shard_map/ppermute | solution.py:39

commit v3 on v2

--- a/solution.py
+++ b/solution.py
@@ -14,60 +14,128 @@
 GELU_ROOT = 0.7978845608028654
 GELU_CUBE = 0.044715
 
-def padded_2(block, sides, width):
-    for axis, dim in sides:
-        count = lax.axis_size(axis)
-        forward = [(i, i + 1) for i in range(count - 1)]
-        forward.append((count - 1, 0))
-        backward = [(target, source) for source, target in forward]
-        low = lax.ppermute(
-            lax.slice_in_dim(block, block.shape[dim] - width, None, axis=dim), axis, forward
-        )
-        high = lax.ppermute(lax.slice_in_dim(block, 0, width, axis=dim), axis, backward)
-        block = jnp.concatenate([low, block, high], axis=dim)
-    return block
-
-
-def sweep(padded):
-    middle = padded[:, 1:-1]
-    return middle + diffusion * (padded[:, :-2] - 2.0 * middle + padded[:, 2:])
-
-
-def pair_swap(block, axis, low_bit, high_bit):
+ON_CHIP = pl.BlockSpec(memory_space=pltpu.VMEM)
+EDGE = 8 * -(-SWEEPS // 8)
+
+
+def near(*arrays):
+    return [pltpu.with_memory_space_constraint(a, pltpu.VMEM) for a in arrays]
+
+
+def edge_columns(block, axis):
     count = lax.axis_size(axis)
-    pairs = [(i, i ^ (high_bit if i & 1 else low_bit)) for i in range(count)]
-    return lax.ppermute(block, axis, pairs)
+    forward = [(i, (i + 1) % count) for i in range(count)]
+    backward = [(target, source) for source, target in forward]
+    first = block[:, :EDGE].astype(jnp.float32)
+    last = block[:, -EDGE:].astype(jnp.float32)
+    return lax.ppermute(last, axis, forward), lax.ppermute(first, axis, backward)
+
+
+def swept(field):
+    rows = field.shape[0]
+    for sweep_index in range(SWEEPS):
+        low = pltpu.roll(field, 1, 0)
+        high = pltpu.roll(field, rows - 1, 0)
+        field = field + diffusion * ((low - 2.0 * field) + high)
+    return field
+
+
+def inside_kernel(control, perturb, total, ends, factors):
+    members, columns, levels = control.shape
+    summed = None
+    for member in range(members):
+        field = control[member].astype(jnp.float32)
+        factor = perturb[member].astype(jnp.float32)
+        ends[member, :EDGE] = field[:EDGE]
+        ends[member, EDGE:] = field[columns - EDGE:]
+        factors[member, :EDGE] = factor[:EDGE]
+        factors[member, EDGE:] = factor[columns - EDGE:]
+        part = swept(field) * factor
+        summed = part if summed is None else summed + part
+    total[...] = summed
+
+
+def edge_kernel(core, inside, ends, factors, low, high, keep, send, total, *, owners):
+    members = ends.shape[0]
+    columns, levels = total.shape
+    total[...] = inside[...]
+    windows = []
+    for member in range(members):
+        windows += [low[member], ends[member], high[member]]
+    field = swept(jnp.concatenate(windows, axis=0))
+    size = 4 * EDGE
+    start = jnp.zeros((EDGE, levels), jnp.float32)
+    stop = start
+    for member in range(members):
+        base = size * member + EDGE
+        start = start + field[base:base + EDGE] * factors[member, :EDGE]
+        stop = stop + field[base + EDGE:base + 2 * EDGE] * factors[member, EDGE:]
+    rows = lax.broadcasted_iota(jnp.int32, (EDGE, levels), 0)
+    total[:EDGE] = jnp.where(rows < SWEEPS, start, total[:EDGE])
+    total[columns - EDGE:] = jnp.where(rows >= EDGE - SWEEPS, stop, total[columns - EDGE:])
+    owned = columns // owners
+    for chip in range(owners // 2):
+        here = pl.multiple_of((2 * chip + core[0]) * owned, owned)
+        there = pl.multiple_of((2 * chip + 1 - core[0]) * owned, owned)
+        keep[chip * owned:(chip + 1) * owned] = total[pl.ds(here, owned)]
+        send[chip * owned:(chip + 1) * owned] = total[pl.ds(there, owned)]
+
+
+def member_sum(control, perturb, core, owners):
+    members, columns, levels = control.shape
+    low, high = edge_columns(control, "sub")
+    ends = pltpu.VMEM((members, 2 * EDGE, levels), jnp.float32)
+    whole = pltpu.VMEM((columns, levels), jnp.float32)
+    total, fields, factors = pl.pallas_call(
+        inside_kernel,
+        out_shape=(whole, ends, ends),
+        in_specs=[ON_CHIP] * 2,
+        out_specs=(ON_CHIP,) * 3,
+        name="inside",
+    )(control, perturb)
+    half = pltpu.VMEM((columns // 2, levels), jnp.float32)
+    return pl.pallas_call(
+        functools.partial(edge_kernel, owners=owners),
+        out_shape=(half, half),
+        in_specs=[pl.BlockSpec(memory_space=pltpu.SMEM)] + [ON_CHIP] * 5,
+        out_specs=(ON_CHIP,) * 2,
+        scratch_shapes=[whole],
+        name="edges",
+    )(core, *near(total, fields, factors, low, high))
+
+
+def bit_swap(block, axis, bit):
+    count = lax.axis_size(axis)
+    return lax.ppermute(block, axis, [(i, i ^ bit) for i in range(count)])
 
 
 def pick(block, dim, which):
     return lax.squeeze(lax.dynamic_slice_in_dim(block, which, 1, dim), (dim,))
 
 
-def chip_bits(count):
-    return [1 << step for step in range(1, count.bit_length() - 1)]
-
-
-def reduce_pairs(block, axis):
+def reduce_pairs(keep, send, axis):
     count = lax.axis_size(axis)
-    core = lax.axis_index(axis) & 1
-    sides = block.reshape((count // 2, 2, block.shape[0] // count) + block.shape[1:])
-    mine = pick(sides, 1, core) + pair_swap(pick(sides, 1, 1 - core), axis, 1, 1)
-    bits = chip_bits(count)
-    for low_bit, high_bit in zip(bits, bits[::-1]):
-        mine = mine + pair_swap(mine, axis, low_bit, high_bit)
-    mine = mine.reshape((-1,) + block.shape[1:])
-    return mine, pair_swap(mine, axis, 1, 1)
+    mine = keep + bit_swap(send, axis, 1)
+    if count <= 8:
+        parts = [bit_swap(mine, axis, bit) for bit in range(2, count, 2)]
+        for part in parts:
+            mine = mine + part
+    else:
+        for step in range(1, count.bit_length() - 1):
+            mine = mine + bit_swap(mine, axis, 1 << step)
+    return mine, bit_swap(mine, axis, 1)
 
 
 def scatter_pairs(keep, send, axis):
     count = lax.axis_size(axis)
     me = lax.axis_index(axis)
-    block = keep + pair_swap(send, axis, 1, 1)
-    for bit in chip_bits(count):
-        side = (me // bit) & 1
-        halves = block.reshape((-1, 2) + keep.shape[1:])
-        block = pick(halves, 1, side) + pair_swap(pick(halves, 1, 1 - side), axis, bit, bit)
-    return block.reshape(keep.shape[1:])
+    block = keep + bit_swap(send, axis, 1)
+    block = block.reshape((count // 2, -1) + block.shape[1:])
+    for step in range(1, count.bit_length() - 1):
+        side = (me >> step) & 1
+        halves = block.reshape((-1, 2) + block.shape[1:])
+        block = pick(halves, 1, side) + bit_swap(pick(halves, 1, 1 - side), axis, 1 << step)
+    return block.reshape(block.shape[1:])
 
 
 def observe_kernel(
@@ -81,6 +149,7 @@
     top = increment.astype(jnp.bfloat16)
     rest = (increment - top.astype(jnp.float32)).astype(jnp.bfloat16)
     table = jnp.concatenate([top, rest], axis=1)
+    half_bias = 0.5 * b_in[...]
 
     def start(index):
         base = index * block
@@ -89,18 +158,17 @@
         picked = across.astype(jnp.float32).astype(jnp.bfloat16)
         pair = lax.dot_general(picked, table, (((0,), (0,)), ((), ())), preferred_element_type=jnp.float32)
         sampled = pair[:, :levels] + pair[:, levels:]
-        inputs = (background[base:base + block, :].astype(jnp.float32) + sampled).astype(jnp.bfloat16)
+        inputs = 0.5 * (background[base:base + block, :].astype(jnp.float32) + sampled).astype(jnp.bfloat16)
         return dict(base=base, slot=index % 2, picked=picked, inputs=inputs, outputs=None, back=None)
 
     def forward(st, c):
         sl = slice(c, c + chunk)
-        pre = jnp.dot(st["inputs"], w_in[:, sl], preferred_element_type=jnp.float32) + b_in[0:1, sl]
-        square = pre * pre
-        bend = jnp.tanh(pre * (GELU_ROOT + GELU_ROOT * GELU_CUBE * square))
-        half = 0.5 * pre
+        half = jnp.dot(st["inputs"], w_in[:, sl], preferred_element_type=jnp.float32) + half_bias[0:1, sl]
+        square = half * half
+        bend = jnp.tanh(half * (2.0 * GELU_ROOT + 8.0 * GELU_ROOT * GELU_CUBE * square))
         lift = 1.0 + bend
         st_hidden = (half * lift).astype(jnp.bfloat16)
-        rise = GELU_ROOT + 3.0 * GELU_ROOT * GELU_CUBE * square
+        rise = GELU_ROOT + 12.0 * GELU_ROOT * GELU_CUBE * square
         tilt = lift * (0.5 + half * ((1.0 - bend) * rise))
         slope[st["slot"], :, sl] = tilt
         part = jnp.dot(st_hidden, w_out[sl, :], preferred_element_type=jnp.float32)
@@ -150,18 +218,17 @@
 
 
 def observe_call(mine, other, indices, weights, background, targets, w_in, b_in, w_out, scale):
-    vm = pl.BlockSpec(memory_space=pltpu.VMEM)
     block = largest_part(background.shape[0], 512)
     chunk = largest_part(w_in.shape[1], 256)
-    half = jax.ShapeDtypeStruct(mine.shape, jnp.float32)
+    half = pltpu.VMEM(mine.shape, jnp.float32)
     return pl.pallas_call(
         functools.partial(observe_kernel, scale=scale, block=block, chunk=chunk),
         out_shape=(half, half),
-        in_specs=[vm] * 9,
-        out_specs=(vm, vm),
+        in_specs=[ON_CHIP] * 9,
+        out_specs=(ON_CHIP, ON_CHIP),
         scratch_shapes=[pltpu.VMEM((2, block, w_in.shape[1]), jnp.float32)],
         name="observe",
-    )(mine, other, indices, weights, background, targets, w_in, b_in, w_out)
+    )(*near(mine, other, indices, weights, background, targets, w_in, b_in, w_out))
 
 
 def per_device(
@@ -176,29 +243,25 @@
     b_in,
     w_out,
 ):
-    field = control.astype(jnp.float32)
-    padded = padded_2(field, (("sub", 1),), SWEEPS)
-    for sweep_index in range(SWEEPS):
-        padded = sweep(padded)
-    field = padded
-    partial_sum = jnp.sum(field * perturb.astype(jnp.float32), axis=0)
     members = perturb.shape[0] * lax.axis_size("mem")
     scale = (members - 1) ** (-0.5)
     count = lax.axis_size("mem")
     me = lax.axis_index("mem")
-    columns = partial_sum.shape[0]
+    columns = control.shape[1]
     owned = columns // count
     indices = obs_column.reshape(1, -1)
     slots = indices.shape[1]
     paired = count > 1 and count & (count - 1) == 0
+    core = me & 1 if paired else jnp.int32(0)
+    keep, send = member_sum(control, perturb, core.reshape(1), count if paired else 2)
     if paired:
         owner = indices // owned
         side = ((owner ^ me) & 1) * (columns // 2)
         indices = side + (owner // 2) * owned + indices % owned
-        mine, other = reduce_pairs(partial_sum, "mem")
+        mine, other = reduce_pairs(keep, send, "mem")
         increment = pick(mine.reshape(count // 2, owned, -1), 0, me // 2) * scale
     else:
-        summed = lax.psum(partial_sum, "mem")
+        summed = lax.psum(jnp.concatenate([keep, send], axis=0), "mem")
         mine, other = summed[: columns // 2], summed[columns // 2 :]
         increment = lax.dynamic_slice_in_dim(summed, me * owned, owned, 0) * scale
     slot_ids = lax.broadcasted_iota(jnp.int32, (1, slots), 1)
@@ -216,8 +279,7 @@
         scale,
     )
     if paired:
-        halves = (count // 2, owned, keep.shape[1])
-        grad_columns = scatter_pairs(keep.reshape(halves), send.reshape(halves), "mem")
+        grad_columns = scatter_pairs(keep, send, "mem")
     else:
         gradient = jnp.concatenate([keep, send], axis=0)
         grad_columns = lax.psum_scatter(gradient, "mem", scatter_dimension=0, tiled=True)

time: 46.8 us -> 37.1 us (0.79)
  other arithmetic: 6.63 us -> 2.08 us
  waiting for transfers between devices: 15.1 us -> 13.1 us
  local copies, waits for them, and re-layouts: 2.13 us -> 0.62 us
  starting transfers between devices: 11.7 us -> 10.2 us
    pallas_call x0 -> x2, Pallas kernels: none -> 3.03 us  [the longest x1 2.85 us: member_sum(): pl.pallas_call(inside_kernel, out_shape=(whole, ends, ends), in_specs=[ON...]
    pallas_call x1, Pallas kernels: 9.39 us -> 6.36 us  [observe_call(): pl.pallas_call(functools.partial(observe_kernel, scale=scale, block=block...]
    ppermute x9 -> x10, waiting for transfers between devices: 15.1 us -> 13.1 us  [the longest x8 13.1 us: bit_swap(): return lax.ppermute(block, axis, [(i, i ^ bit) for i in range(count)])]
    add x8 -> x4, other arithmetic: 1.85 us -> 0.05 us  [the longest x1 0.03 us: reduce_pairs(): mine = mine + part]
    ppermute x9 -> x10, starting transfers between devices: 11.7 us -> 10.2 us  [the longest x8 5.08 us: bit_swap(): return lax.ppermute(block, axis, [(i, i ^ bit) for i in range(count)])]
    unnamed x10 -> x14, local copies, waits for them, and re-layouts: 1.35 us -> 0.6 us
    slice x1 -> x0, local copies, waits for them, and re-layouts: 0.75 us -> none  [padded_2(): lax.slice_in_dim(block, block.shape[dim] - width, None, axis=dim)]
    mul x1, other arithmetic: 1.32 us -> 0.61 us  [per_device(): increment = pick(mine.reshape(count // 2, owned, -1), 0, me // 2) * scale]
  transfers between devices with their start and end apart: 9 -> 10, of which waited for: 9 -> 8; matrix products, arithmetic and copies ran while one was open for 8% -> 2% of each run, Pallas kernels for 0% -> 8%
where the time goes in v3:
time: 37.1 us; the launch traced here: 36.9 us
  waiting for transfers between devices  13.1 us (35%)
  starting transfers between devices  10.2 us (27%)
  Pallas kernels  9.4 us (25%)
  other arithmetic  2.08 us (6%)
  between operations  1.4 us (4%)
  local copies, waits for them, and re-layouts  0.62 us (2%)
    ppermute x8, waiting for transfers between devices, bit_swap(): return lax.ppermute(block, axis, [(i, i ^ bit) for i in range(count)])  13.1 us
    pallas_call x1, Pallas kernels, observe_call(): pl.pallas_call(functools.partial(observe_kernel, scale=scale, block=block...  6.36 us
    ppermute x8, starting transfers between devices, bit_swap(): return lax.ppermute(block, axis, [(i, i ^ bit) for i in range(count)])  5.08 us
    ppermute x1, starting transfers between devices, edge_columns(): lax.ppermute(last, axis, forward)  3.05 us
    pallas_call x1, Pallas kernels, member_sum(): pl.pallas_call(inside_kernel, out_shape=(whole, ends, ends), in_specs=[ON...  2.85 us
    ppermute x1, starting transfers between devices, edge_columns(): lax.ppermute(first, axis, backward)  2.08 us
    convert_element_type x1, other arithmetic, edge_columns(): first = block[:, :EDGE].astype(jnp.float32)  0.74 us
  transfers between devices with their start and end apart: 10, of which 8 were waited for; matrix products, arithmetic and copies ran while one was open for 2% of the time, Pallas kernels for 8%

profile of v3, /device:TPU:0, one launch (start us, length us, event | category | flops | bytes accessed | tf_op | source)
XLA Modules:
  0.0 36.9 jit_solution(7737768837521916784)
XLA Ops:
  0.6 0.7 %slice_convert_fusion = (f32[8,8,128]{2,1,0:T(8,128)S(1)}, f32[8,8,128]{2,1,0:T(8,128)S(1)}) fusion(bf16[8,256,128]{2,1,0:T(8,128)(2,1)} %control.1), kind=kLoop, calls=%fused_computation.5 | loop fusion | flops 16384 | bytes 98304 | tf_op jit(solution)/shard_map/convert_element_type | solution.py:29
  1.4 3.1 %collective-permute-start = (f32[8,8,128]{2,1,0:T(8,128)S(1)}, f32[8,8,128]{2,1,0:T(8,128)S(1)}, u32[]{:S(2)}, u32[]{:S(2)}) collective-permute-start(f32[8,8,128]{2,1,0:T(8,128)S(1)} %get-tuple-element.17), channel_id=1, source_target_pairs={{0,1},{1,2},{2,3},{3,0},{4,5},{5,6},{6,7},{7,4},{8,9},{9,10},{10,1... | collective-permute-start | bytes 98312 | tf_op jit(solution)/shard_map/ppermute | solution.py:31
  4.4 2.1 %collective-permute-start.1 = (f32[8,8,128]{2,1,0:T(8,128)S(1)}, f32[8,8,128]{2,1,0:T(8,128)S(1)}, u32[]{:S(2)}, u32[]{:S(2)}) collective-permute-start(f32[8,8,128]{2,1,0:T(8,128)S(1)} %get-tuple-element.16), channel_id=1, source_target_pairs={{1,0},{2,1},{3,2},{0,3},{5,4},{6,5},{7,6},{4,7},{9,8},{10,9},{11,1... | collective-permute-start | bytes 98312 | tf_op jit(solution)/shard_map/ppermute | solution.py:31
  6.5 2.9 %inside.1 = (f32[256,128]{1,0:T(8,128)S(1)}, f32[8,16,128]{2,1,0:T(8,128)S(1)}, f32[8,16,128]{2,1,0:T(8,128)S(1)}) custom-call(bf16[8,256,128]{2,1,0:T(8,128)(2,1)} %control.1, bf16[8,256,128]{2,1,0:T(8,128)(2,1)} %perturb.1), custom_call_target="tpu_custom_call" | custom-call | tf_op jit(solution)/shard_map/inside/pallas_call | solution.py:89
  9.4 0.2 edges.1
  9.6 0.1 collective-permute-start.2
  9.7 1.2 %collective-permute-done.2 = f32[128,128]{1,0:T(8,128)S(1)} collective-permute-done((f32[128,128]{1,0:T(8,128)S(1)}, f32[128,128]{1,0:T(8,128)S(1)}, u32[]{:S(2)}, u32[]{:S(2)}) %collective-permute-start.2) | collective-permute-done | bytes 65568 | tf_op jit(solution)/shard_map/ppermute | solution.py:109
  10.9 1.7 %collective-permute-start.3 = (f32[128,128]{1,0:T(8,128)S(1)}, f32[128,128]{1,0:T(8,128)S(1)}, u32[]{:S(2)}, u32[]{:S(2)}) collective-permute-start(f32[128,128]{1,0:T(8,128)S(1)} %add.85), channel_id=1, source_target_pairs={{0,8},{4,12},{8,0},{12,4},{16,24},{20,28},{24,16},{28,20},{1,9},{5... | collective-permute-start | bytes 196616 | tf_op jit(solution)/shard_map/ppermute | solution.py:109
  12.7 1.5 %collective-permute-start.4 = (f32[128,128]{1,0:T(8,128)S(1)}, f32[128,128]{1,0:T(8,128)S(1)}, u32[]{:S(2)}, u32[]{:S(2)}) collective-permute-start(f32[128,128]{1,0:T(8,128)S(1)} %add.85), channel_id=1, source_target_pairs={{0,16},{4,20},{8,24},{12,28},{16,0},{20,4},{24,8},{28,12},{1,17},{... | collective-permute-start | bytes 196616 | tf_op jit(solution)/shard_map/ppermute | solution.py:109
  14.2 0.3 collective-permute-start.5
  15.3 1.7 %collective-permute-done.4 = f32[128,128]{1,0:T(8,128)S(1)} collective-permute-done((f32[128,128]{1,0:T(8,128)S(1)}, f32[128,128]{1,0:T(8,128)S(1)}, u32[]{:S(2)}, u32[]{:S(2)}) %collective-permute-start.4) | collective-permute-done | bytes 65568 | tf_op jit(solution)/shard_map/ppermute | solution.py:109
  16.9 2.4 %collective-permute-done.5 = f32[128,128]{1,0:T(8,128)S(1)} collective-permute-done((f32[128,128]{1,0:T(8,128)S(1)}, f32[128,128]{1,0:T(8,128)S(1)}, u32[]{:S(2)}, u32[]{:S(2)}) %collective-permute-start.5) | collective-permute-done | bytes 65568 | tf_op jit(solution)/shard_map/ppermute | solution.py:109
  19.4 0.1 collective-permute-start.6
  19.5 0.6 %copy-done.6 = f32[1,1,1024]{2,1,0:T(1,128)S(1)} copy-done((f32[1,1,1024]{2,1,0:T(1,128)S(1)}, f32[1,1,1024]{2,1,0:T(1,128)}, u32[]{:S(2)}) %copy-start.6) | copy-done | bytes 4120
  20.0 0.7 %collective-permute-done.6.other = f32[128,128]{1,0:T(8,128)S(1)} collective-permute-done((f32[128,128]{1,0:T(8,128)S(1)}, f32[128,128]{1,0:T(8,128)S(1)}, u32[]{:S(2)}, u32[]{:S(2)}) %collective-permute-start.6) | collective-permute-done | bytes 65568 | tf_op jit(solution)/shard_map/ppermute | solution.py:109
  20.7 6.4 %observe.1 = (f32[128,128]{1,0:T(8,128)S(1)}, f32[128,128]{1,0:T(8,128)S(1)}) custom-call(f32[128,128]{1,0:T(8,128)S(1)} %add_add_fusion.mine, f32[128,128]{1,0:T(8,128)S(1)} %collective-permute-done.6.other, s32[1,1024]{1,0:T(1,128)S(1)} %fusion.indices, f32[1,1024]{1,0:T(1,128)S(1)} %compare_select_fusion.weights, bf16[1024,128]{1,0:T(8,128)(2,1)S(1)} %bitcast.32, ...), custom_call_target="tpu_custom_call" | custom-call | tf_op jit(solution)/shard_map/observe/pallas_call | solution.py:224
  27.1 0.2 collective-permute-start.7
  27.3 1.1 %collective-permute-done.7 = f32[128,128]{1,0:T(8,128)S(1)} collective-permute-done((f32[128,128]{1,0:T(8,128)S(1)}, f32[128,128]{1,0:T(8,128)S(1)}, u32[]{:S(2)}, u32[]{:S(2)}) %collective-permute-start.7) | collective-permute-done | bytes 65568 | tf_op jit(solution)/shard_map/ppermute | solution.py:109
  28.5 0.6 %collective-permute-start.8 = (f32[2,32,128]{2,1,0:T(8,128)S(1)}, f32[2,32,128]{2,1,0:T(8,128)S(1)}, u32[]{:S(2)}, u32[]{:S(2)}) collective-permute-start(f32[2,32,128]{2,1,0:T(8,128)S(1)} %dynamic-slice_bitcast_fusion), channel_id=1, source_target_pairs={{0,8},{4,12},{8,0},{12,4},{16,24},{20,28},{24,16},{28,20},{1,9},{5... | collective-permute-start | bytes 98312 | tf_op jit(solution)/shard_map/ppermute | solution.py:109
  29.1 3.4 %collective-permute-done.8 = f32[2,32,128]{2,1,0:T(8,128)S(1)} collective-permute-done((f32[2,32,128]{2,1,0:T(8,128)S(1)}, f32[2,32,128]{2,1,0:T(8,128)S(1)}, u32[]{:S(2)}, u32[]{:S(2)}) %collective-permute-start.8) | collective-permute-done | bytes 32800 | tf_op jit(solution)/shard_map/ppermute | solution.py:109
  32.4 0.6 %collective-permute-start.9 = (f32[1,32,128]{2,1,0:T(8,128)S(1)}, f32[1,32,128]{2,1,0:T(8,128)S(1)}, u32[]{:S(2)}, u32[]{:S(2)}) collective-permute-start(f32[1,32,128]{2,1,0:T(8,128)S(1)} %constant_dynamic-slice_fusion), channel_id=1, source_target_pairs={{0,16},{4,20},{8,24},{12,28},{16,0},{20,4},{24,8},{28,12},{1,17},{... | collective-permute-start | bytes 49160 | tf_op jit(solution)/shard_map/ppermute | solution.py:109
  33.0 0.6 %multiply_bitcast_fusion = f32[32,128]{1,0:T(8,128)} fusion(f32[4,32,128]{2,1,0:T(8,128)S(1)} %bitcast.31, s32[]{:T(128)S(6)} %select_n.59), kind=kLoop, calls=%fused_computation.4 | loop fusion | flops 4096 | bytes 32772 | tf_op jit(solution)/shard_map/mul | solution.py:262
  33.6 2.6 %collective-permute-done.9 = f32[1,32,128]{2,1,0:T(8,128)S(1)} collective-permute-done((f32[1,32,128]{2,1,0:T(8,128)S(1)}, f32[1,32,128]{2,1,0:T(8,128)S(1)}, u32[]{:S(2)}, u32[]{:S(2)}) %collective-permute-start.9) | collective-permute-done | bytes 16416 | tf_op jit(solution)/shard_map/ppermute | solution.py:109
  36.2 0.6 %add_bitcast_fusion = f32[32,128]{1,0:T(8,128)} fusion(f32[1,32,128]{2,1,0:T(8,128)S(1)} %collective-permute-done.9, f32[2,32,128]{2,1,0:T(8,128)S(1)} %bitcast_add_fusion, s32[]{:T(128)S(6)} %select_n.65), kind=kLoop, calls=%fused_computation.3 | loop fusion | flops 4096 | bytes 49156 | tf_op jit(solution)/shard_map/reshape | solution.py:138
  (24 shorter events, 0.2 us)
Async XLA Ops:
  1.4 8.0 %collective-permute-start = (f32[8,8,128]{2,1,0:T(8,128)S(1)}, f32[8,8,128]{2,1,0:T(8,128)S(1)}, u32[]{:S(2)}, u32[]{:S(2)}) collective-permute-start(f32[8,8,128]{2,1,0:T(8,128)S(1)} %get-tuple-element.17), channel_id=1, source_target_pairs={{0,1},{1,2},{2,3},{3,0},{4,5},{5,6},{6,7},{7,4},{8,9},{9,10},{10,1... | collective-permute-start | bytes 98312 | tf_op jit(solution)/shard_map/ppermute | solution.py:31
  4.4 5.0 %collective-permute-start.1 = (f32[8,8,128]{2,1,0:T(8,128)S(1)}, f32[8,8,128]{2,1,0:T(8,128)S(1)}, u32[]{:S(2)}, u32[]{:S(2)}) collective-permute-start(f32[8,8,128]{2,1,0:T(8,128)S(1)} %get-tuple-element.16), channel_id=1, source_target_pairs={{1,0},{2,1},{3,2},{0,3},{5,4},{6,5},{7,6},{4,7},{9,8},{10,9},{11,1... | collective-permute-start | bytes 98312 | tf_op jit(solution)/shard_map/ppermute | solution.py:31
  6.5 14.2 %copy-start.1 = (bf16[2048,128]{1,0:T(8,128)(2,1)S(1)}, bf16[2048,128]{1,0:T(8,128)(2,1)}, u32[]{:S(2)}) copy-start(bf16[2048,128]{1,0:T(8,128)(2,1)} %w_out.1) | copy-start | bytes 1572868
  6.5 14.2 %copy-start.3 = (bf16[1,1,1024,128]{3,2,1,0:T(8,128)(2,1)S(1)}, bf16[1,1,1024,128]{3,2,1,0:T(8,128)(2,1)}, u32[]{:S(2)}) copy-start(bf16[1,1,1024,128]{3,2,1,0:T(8,128)(2,1)} %param.15) | copy-start | bytes 786436
  9.4 11.3 %copy-start = (bf16[128,2048]{1,0:T(8,128)(2,1)S(1)}, bf16[128,2048]{1,0:T(8,128)(2,1)}, u32[]{:S(2)}) copy-start(bf16[128,2048]{1,0:T(8,128)(2,1)} %w_in.1) | copy-start | bytes 1572868
  9.4 5.1 %copy-start.5 = (s32[1,1,1024]{2,1,0:T(1,128)S(1)}, s32[1,1,1024]{2,1,0:T(1,128)}, u32[]{:S(2)}) copy-start(s32[1,1,1024]{2,1,0:T(1,128)} %param.12) | copy-start | bytes 12292
  9.6 1.3 %collective-permute-start.2 = (f32[128,128]{1,0:T(8,128)S(1)}, f32[128,128]{1,0:T(8,128)S(1)}, u32[]{:S(2)}, u32[]{:S(2)}) collective-permute-start(f32[128,128]{1,0:T(8,128)S(1)} %get-tuple-element.13), channel_id=1, source_target_pairs={{0,4},{4,0},{8,12},{12,8},{16,20},{20,16},{24,28},{28,24},{1,5},{5... | collective-permute-start | bytes 196616 | tf_op jit(solution)/shard_map/ppermute | solution.py:109
  10.9 9.8 %copy-start.2 = (bf16[1,1,1024,128]{3,2,1,0:T(8,128)(2,1)S(1)}, bf16[1,1,1024,128]{3,2,1,0:T(8,128)(2,1)}, u32[]{:S(2)}) copy-start(bf16[1,1,1024,128]{3,2,1,0:T(8,128)(2,1)} %param.14) | copy-start | bytes 786436
  10.9 4.3 %collective-permute-start.3 = (f32[128,128]{1,0:T(8,128)S(1)}, f32[128,128]{1,0:T(8,128)S(1)}, u32[]{:S(2)}, u32[]{:S(2)}) collective-permute-start(f32[128,128]{1,0:T(8,128)S(1)} %add.85), channel_id=1, source_target_pairs={{0,8},{4,12},{8,0},{12,4},{16,24},{20,28},{24,16},{28,20},{1,9},{5... | collective-permute-start | bytes 196616 | tf_op jit(solution)/shard_map/ppermute | solution.py:109
  12.7 4.3 %collective-permute-start.4 = (f32[128,128]{1,0:T(8,128)S(1)}, f32[128,128]{1,0:T(8,128)S(1)}, u32[]{:S(2)}, u32[]{:S(2)}) collective-permute-start(f32[128,128]{1,0:T(8,128)S(1)} %add.85), channel_id=1, source_target_pairs={{0,16},{4,20},{8,24},{12,28},{16,0},{20,4},{24,8},{28,12},{1,17},{... | collective-permute-start | bytes 196616 | tf_op jit(solution)/shard_map/ppermute | solution.py:109
  14.2 5.2 %collective-permute-start.5 = (f32[128,128]{1,0:T(8,128)S(1)}, f32[128,128]{1,0:T(8,128)S(1)}, u32[]{:S(2)}, u32[]{:S(2)}) collective-permute-start(f32[128,128]{1,0:T(8,128)S(1)} %add.85), channel_id=1, source_target_pairs={{0,24},{4,28},{8,16},{12,20},{16,8},{20,12},{24,0},{28,4},{1,25},{... | collective-permute-start | bytes 196616 | tf_op jit(solution)/shard_map/ppermute | solution.py:109
  19.3 0.7 %copy-start.6 = (f32[1,1,1024]{2,1,0:T(1,128)S(1)}, f32[1,1,1024]{2,1,0:T(1,128)}, u32[]{:S(2)}) copy-start(f32[1,1,1024]{2,1,0:T(1,128)} %param.16) | copy-start | bytes 12292
  19.4 1.4 %copy-start.4 = (f32[2048]{0:T(1024)S(1)}, f32[2048]{0:T(1024)}, u32[]{:S(2)}) copy-start(f32[2048]{0:T(1024)} %param.18) | copy-start | bytes 24580
  19.4 1.3 %collective-permute-start.6 = (f32[128,128]{1,0:T(8,128)S(1)}, f32[128,128]{1,0:T(8,128)S(1)}, u32[]{:S(2)}, u32[]{:S(2)}) collective-permute-start(f32[128,128]{1,0:T(8,128)S(1)} %add_add_fusion.mine), channel_id=1, source_target_pairs={{0,4},{4,0},{8,12},{12,8},{16,20},{20,16},{24,28},{28,24},{1,5},{5... | collective-permute-start | bytes 196616 | tf_op jit(solution)/shard_map/ppermute | solution.py:109
  27.1 1.3 %collective-permute-start.7 = (f32[128,128]{1,0:T(8,128)S(1)}, f32[128,128]{1,0:T(8,128)S(1)}, u32[]{:S(2)}, u32[]{:S(2)}) collective-permute-start(f32[128,128]{1,0:T(8,128)S(1)} %get-tuple-element.15), channel_id=1, source_target_pairs={{0,4},{4,0},{8,12},{12,8},{16,20},{20,16},{24,28},{28,24},{1,5},{5... | collective-permute-start | bytes 196616 | tf_op jit(solution)/shard_map/ppermute | solution.py:109
  28.5 4.0 %collective-permute-start.8 = (f32[2,32,128]{2,1,0:T(8,128)S(1)}, f32[2,32,128]{2,1,0:T(8,128)S(1)}, u32[]{:S(2)}, u32[]{:S(2)}) collective-permute-start(f32[2,32,128]{2,1,0:T(8,128)S(1)} %dynamic-slice_bitcast_fusion), channel_id=1, source_target_pairs={{0,8},{4,12},{8,0},{12,4},{16,24},{20,28},{24,16},{28,20},{1,9},{5... | collective-permute-start | bytes 98312 | tf_op jit(solution)/shard_map/ppermute | solution.py:109
  32.4 3.8 %collective-permute-start.9 = (f32[1,32,128]{2,1,0:T(8,128)S(1)}, f32[1,32,128]{2,1,0:T(8,128)S(1)}, u32[]{:S(2)}, u32[]{:S(2)}) collective-permute-start(f32[1,32,128]{2,1,0:T(8,128)S(1)} %constant_dynamic-slice_fusion), channel_id=1, source_target_pairs={{0,16},{4,20},{8,24},{12,28},{16,0},{20,4},{24,8},{28,12},{1,17},{... | collective-permute-start | bytes 49160 | tf_op jit(solution)/shard_map/ppermute | solution.py:109

commit v4 on v3

--- a/solution.py
+++ b/solution.py
@@ -20,6 +20,10 @@
 
 def near(*arrays):
     return [pltpu.with_memory_space_constraint(a, pltpu.VMEM) for a in arrays]
+
+
+def room(mebibytes):
+    return pltpu.CompilerParams(vmem_limit_bytes=mebibytes << 20)
 
 
 def edge_columns(block, axis):
@@ -40,12 +44,23 @@
     return field
 
 
-def inside_kernel(control, perturb, total, ends, factors):
+def inside_kernel(control, perturb, total, ends, factors, fields, weights, arrived):
     members, columns, levels = control.shape
+    copies = []
+    for member in range(members):
+        copies.append((
+            pltpu.make_async_copy(control.at[member], fields.at[member], arrived.at[0, member]),
+            pltpu.make_async_copy(perturb.at[member], weights.at[member], arrived.at[1, member]),
+        ))
+    for pair in copies:
+        for copy in pair:
+            copy.start()
     summed = None
     for member in range(members):
-        field = control[member].astype(jnp.float32)
-        factor = perturb[member].astype(jnp.float32)
+        for copy in copies[member]:
+            copy.wait()
+        field = fields[member].astype(jnp.float32)
+        factor = weights[member].astype(jnp.float32)
         ends[member, :EDGE] = field[:EDGE]
         ends[member, EDGE:] = field[columns - EDGE:]
         factors[member, :EDGE] = factor[:EDGE]
@@ -89,10 +104,16 @@
     total, fields, factors = pl.pallas_call(
         inside_kernel,
         out_shape=(whole, ends, ends),
-        in_specs=[ON_CHIP] * 2,
+        in_specs=[pl.BlockSpec(memory_space=pltpu.HBM)] * 2,
         out_specs=(ON_CHIP,) * 3,
+        scratch_shapes=[
+            pltpu.VMEM(control.shape, control.dtype),
+            pltpu.VMEM(perturb.shape, perturb.dtype),
+            pltpu.SemaphoreType.DMA((2, members)),
+        ],
+        compiler_params=room(16),
         name="inside",
-    )(control, perturb)
+    )(*(pltpu.with_memory_space_constraint(a, pltpu.HBM) for a in (control, perturb)))
     half = pltpu.VMEM((columns // 2, levels), jnp.float32)
     return pl.pallas_call(
         functools.partial(edge_kernel, owners=owners),
@@ -100,6 +121,7 @@
         in_specs=[pl.BlockSpec(memory_space=pltpu.SMEM)] + [ON_CHIP] * 5,
         out_specs=(ON_CHIP,) * 2,
         scratch_shapes=[whole],
+        compiler_params=room(16),
         name="edges",
     )(core, *near(total, fields, factors, low, high))
 
@@ -131,6 +153,14 @@
     me = lax.axis_index(axis)
     block = keep + bit_swap(send, axis, 1)
     block = block.reshape((count // 2, -1) + block.shape[1:])
+    if count <= 8:
+        chip = me >> 1
+        bits = list(range(1, count // 2))
+        parts = [bit_swap(pick(block, 0, chip ^ bit), axis, 2 * bit) for bit in bits[-1:] + bits[:-1]]
+        owned = pick(block, 0, chip)
+        for part in parts:
+            owned = owned + part
+        return owned
     for step in range(1, count.bit_length() - 1):
         side = (me >> step) & 1
         halves = block.reshape((-1, 2) + block.shape[1:])
@@ -138,12 +168,38 @@
     return block.reshape(block.shape[1:])
 
 
+def layout_kernel(count, indices, weights, by_column, by_slot, spread):
+    columns, slots = by_column.shape
+    lanes = spread.shape[1]
+    row = indices[...]
+    picked = (lax.broadcasted_iota(jnp.int32, (columns, slots), 0) == row).astype(jnp.float32)
+    by_column[...] = picked.astype(jnp.bfloat16)
+    by_slot[...] = jnp.transpose(picked).astype(jnp.bfloat16)
+    live = lax.broadcasted_iota(jnp.int32, (1, slots), 1) < count[0, 0]
+    spread[...] = jnp.transpose(jnp.broadcast_to(jnp.where(live, weights[...], 0.0), (lanes, slots)))
+
+
+def layout_call(count, indices, weights, columns, lanes):
+    slots = indices.shape[1]
+    return pl.pallas_call(
+        layout_kernel,
+        out_shape=(
+            pltpu.VMEM((columns, slots), jnp.bfloat16),
+            pltpu.VMEM((slots, columns), jnp.bfloat16),
+            pltpu.VMEM((slots, lanes), jnp.float32),
+        ),
+        in_specs=[pl.BlockSpec(memory_space=pltpu.SMEM)] + [ON_CHIP] * 2,
+        out_specs=(ON_CHIP,) * 3,
+        compiler_params=room(16),
+        name="layout",
+    )(count, *near(indices, weights))
+
+
 def observe_kernel(
-    mine, other, indices, weights, background, targets, w_in, b_in, w_out, keep, send, slope, *, scale, block, chunk
+    mine, other, by_column, by_slot, spread, background, targets, w_in, b_in, w_out, keep, send, slope, *, scale, block, chunk
 ):
     slots, levels = background.shape
     half_columns = mine.shape[0]
-    columns = 2 * half_columns
     hidden = w_in.shape[1]
     increment = jnp.concatenate([mine[...], other[...]], axis=0) * scale
     top = increment.astype(jnp.bfloat16)
@@ -153,13 +209,10 @@
 
     def start(index):
         base = index * block
-        row = indices[0:1, base:base + block]
-        across = lax.broadcasted_iota(jnp.int32, (columns, block), 0) == row
-        picked = across.astype(jnp.float32).astype(jnp.bfloat16)
-        pair = lax.dot_general(picked, table, (((0,), (0,)), ((), ())), preferred_element_type=jnp.float32)
+        pair = jnp.dot(by_slot[base:base + block, :], table, preferred_element_type=jnp.float32)
         sampled = pair[:, :levels] + pair[:, levels:]
         inputs = 0.5 * (background[base:base + block, :].astype(jnp.float32) + sampled).astype(jnp.bfloat16)
-        return dict(base=base, slot=index % 2, picked=picked, inputs=inputs, outputs=None, back=None)
+        return dict(base=base, slot=index % 2, inputs=inputs, outputs=None, back=None)
 
     def forward(st, c):
         sl = slice(c, c + chunk)
@@ -176,8 +229,7 @@
 
     def middle(st):
         base = st["base"]
-        row = weights[0:1, base:base + block]
-        col = jnp.transpose(jnp.broadcast_to(row, (targets.shape[1], block)))
+        col = spread[base:base + block, :]
         st["misfit"] = ((st["outputs"] - targets[base:base + block, :].astype(jnp.float32)) * col).astype(jnp.bfloat16)
 
     def backward(st, c):
@@ -188,7 +240,8 @@
         st["back"] = part if st["back"] is None else st["back"] + part
 
     def finish(st, total):
-        part = jnp.dot(st["picked"], st["back"].astype(jnp.bfloat16), preferred_element_type=jnp.float32)
+        picked = by_column[:, st["base"]:st["base"] + block]
+        part = jnp.dot(picked, st["back"].astype(jnp.bfloat16), preferred_element_type=jnp.float32)
         return part if total is None else total + part
 
     blocks = slots // block
@@ -217,18 +270,19 @@
     return part
 
 
-def observe_call(mine, other, indices, weights, background, targets, w_in, b_in, w_out, scale):
+def observe_call(mine, other, by_column, by_slot, spread, background, targets, w_in, b_in, w_out, scale):
     block = largest_part(background.shape[0], 512)
     chunk = largest_part(w_in.shape[1], 256)
     half = pltpu.VMEM(mine.shape, jnp.float32)
     return pl.pallas_call(
         functools.partial(observe_kernel, scale=scale, block=block, chunk=chunk),
         out_shape=(half, half),
-        in_specs=[ON_CHIP] * 9,
+        in_specs=[ON_CHIP] * 10,
         out_specs=(ON_CHIP, ON_CHIP),
         scratch_shapes=[pltpu.VMEM((2, block, w_in.shape[1]), jnp.float32)],
+        compiler_params=room(32),
         name="observe",
-    )(*near(mine, other, indices, weights, background, targets, w_in, b_in, w_out))
+    )(*near(mine, other, by_column, by_slot, spread, background, targets, w_in, b_in, w_out))
 
 
 def per_device(
@@ -264,13 +318,11 @@
         summed = lax.psum(jnp.concatenate([keep, send], axis=0), "mem")
         mine, other = summed[: columns // 2], summed[columns // 2 :]
         increment = lax.dynamic_slice_in_dim(summed, me * owned, owned, 0) * scale
-    slot_ids = lax.broadcasted_iota(jnp.int32, (1, slots), 1)
-    live = (slot_ids < obs_count.reshape(())).astype(jnp.float32)
+    layouts = layout_call(obs_count, indices, obs_weight.reshape(1, slots), columns, obs_value.shape[-1])
     keep, send = observe_call(
         mine,
         other,
-        indices,
-        obs_weight.reshape(1, slots) * live,
+        *layouts,
         obs_background.reshape(slots, -1),
         obs_value.reshape(slots, -1),
         w_in,

time: 37.1 us -> 34.9 us (0.941)
  waiting for transfers between devices: 13.1 us -> 8.77 us
  starting transfers between devices: 10.2 us -> 12.9 us
  local copies, waits for them, and re-layouts: 0.62 us -> 0.23 us
    ppermute x8 -> x9, waiting for transfers between devices: 13.1 us -> 8.76 us  [bit_swap(): return lax.ppermute(block, axis, [(i, i ^ bit) for i in range(count)])]
    ppermute x8 -> x9, starting transfers between devices: 5.08 us -> 7.79 us  [bit_swap(): return lax.ppermute(block, axis, [(i, i ^ bit) for i in range(count)])]
    reshape x1 -> x0, other arithmetic: 0.61 us -> none  [scatter_pairs(): return block.reshape(block.shape[1:])]
    add x1, other arithmetic: 0.01 us -> 0.61 us  [scatter_pairs(): owned = owned + part]
    unnamed x14, local copies, waits for them, and re-layouts: 0.6 us -> 0.22 us
    pallas_call x1 -> x2, Pallas kernels: 2.85 us -> 2.87 us  [the longest x1 2.53 us: member_sum(): pl.pallas_call(inside_kernel, out_shape=(whole, ends, ends), in_specs=[pl...]
  transfers between devices with their start and end apart: 10 -> 11, of which waited for: 8 -> 8; matrix products, arithmetic and copies ran while one was open for 2% -> 2% of each run, Pallas kernels for 8% -> 8%
where the time goes in v4:
time: 34.9 us; the launch traced here: 34.6 us
  starting transfers between devices  12.9 us (37%)
  Pallas kernels  9.21 us (26%)
  waiting for transfers between devices  8.77 us (25%)
  other arithmetic  2.06 us (6%)
  between operations  1.43 us (4%)
    ppermute x9, waiting for transfers between devices, bit_swap(): return lax.ppermute(block, axis, [(i, i ^ bit) for i in range(count)])  8.76 us
    ppermute x9, starting transfers between devices, bit_swap(): return lax.ppermute(block, axis, [(i, i ^ bit) for i in range(count)])  7.79 us
    pallas_call x1, Pallas kernels, observe_call(): pl.pallas_call(functools.partial(observe_kernel, scale=scale, block=block...  6.15 us
    ppermute x1, starting transfers between devices, edge_columns(): lax.ppermute(last, axis, forward)  3.05 us
    pallas_call x1, Pallas kernels, member_sum(): pl.pallas_call(inside_kernel, out_shape=(whole, ends, ends), in_specs=[pl...  2.53 us
    ppermute x1, starting transfers between devices, edge_columns(): lax.ppermute(first, axis, backward)  2.08 us
    convert_element_type x1, other arithmetic, edge_columns(): first = block[:, :EDGE].astype(jnp.float32)  0.74 us
  transfers between devices with their start and end apart: 11, of which 8 were waited for; matrix products, arithmetic and copies ran while one was open for 2% of the time, Pallas kernels for 8%

profile of v4, /device:TPU:0, one launch (start us, length us, event | category | flops | bytes accessed | tf_op | source)
XLA Modules:
  0.0 34.6 jit_solution(15312545602131068440)
XLA Ops:
  0.6 0.7 %slice_convert_fusion = (f32[8,8,128]{2,1,0:T(8,128)S(1)}, f32[8,8,128]{2,1,0:T(8,128)S(1)}) fusion(bf16[8,256,128]{2,1,0:T(8,128)(2,1)} %control.1), kind=kLoop, calls=%fused_computation.8 | loop fusion | flops 16384 | bytes 98304 | tf_op jit(solution)/shard_map/convert_element_type | solution.py:33
  1.4 3.1 %collective-permute-start = (f32[8,8,128]{2,1,0:T(8,128)S(1)}, f32[8,8,128]{2,1,0:T(8,128)S(1)}, u32[]{:S(2)}, u32[]{:S(2)}) collective-permute-start(f32[8,8,128]{2,1,0:T(8,128)S(1)} %get-tuple-element.23), channel_id=1, source_target_pairs={{0,1},{1,2},{2,3},{3,0},{4,5},{5,6},{6,7},{7,4},{8,9},{9,10},{10,1... | collective-permute-start | bytes 98312 | tf_op jit(solution)/shard_map/ppermute | solution.py:35
  4.4 2.1 %collective-permute-start.1 = (f32[8,8,128]{2,1,0:T(8,128)S(1)}, f32[8,8,128]{2,1,0:T(8,128)S(1)}, u32[]{:S(2)}, u32[]{:S(2)}) collective-permute-start(f32[8,8,128]{2,1,0:T(8,128)S(1)} %get-tuple-element.22), channel_id=1, source_target_pairs={{1,0},{2,1},{3,2},{0,3},{5,4},{6,5},{7,6},{4,7},{9,8},{10,9},{11,1... | collective-permute-start | bytes 98312 | tf_op jit(solution)/shard_map/ppermute | solution.py:35
  6.5 2.5 %inside.1 = (f32[256,128]{1,0:T(8,128)S(1)}, f32[8,16,128]{2,1,0:T(8,128)S(1)}, f32[8,16,128]{2,1,0:T(8,128)S(1)}) custom-call(bf16[8,256,128]{2,1,0:T(8,128)(2,1)} %control.1, bf16[8,256,128]{2,1,0:T(8,128)(2,1)} %perturb.1), custom_call_target="tpu_custom_call" | custom-call | tf_op jit(solution)/shard_map/inside/pallas_call | solution.py:104
  9.1 0.2 edges.1
  9.3 1.2 %collective-permute-done.2 = f32[128,128]{1,0:T(8,128)S(1)} collective-permute-done((f32[128,128]{1,0:T(8,128)S(1)}, f32[128,128]{1,0:T(8,128)S(1)}, u32[]{:S(2)}, u32[]{:S(2)}) %collective-permute-start.2) | collective-permute-done | bytes 65568 | tf_op jit(solution)/shard_map/ppermute | solution.py:131
  10.6 1.7 %collective-permute-start.3 = (f32[128,128]{1,0:T(8,128)S(1)}, f32[128,128]{1,0:T(8,128)S(1)}, u32[]{:S(2)}, u32[]{:S(2)}) collective-permute-start(f32[128,128]{1,0:T(8,128)S(1)} %add.86), channel_id=1, source_target_pairs={{0,8},{4,12},{8,0},{12,4},{16,24},{20,28},{24,16},{28,20},{1,9},{5... | collective-permute-start | bytes 196616 | tf_op jit(solution)/shard_map/ppermute | solution.py:131
  12.3 1.5 %collective-permute-start.4 = (f32[128,128]{1,0:T(8,128)S(1)}, f32[128,128]{1,0:T(8,128)S(1)}, u32[]{:S(2)}, u32[]{:S(2)}) collective-permute-start(f32[128,128]{1,0:T(8,128)S(1)} %add.86), channel_id=1, source_target_pairs={{0,16},{4,20},{8,24},{12,28},{16,0},{20,4},{24,8},{28,12},{1,17},{... | collective-permute-start | bytes 196616 | tf_op jit(solution)/shard_map/ppermute | solution.py:131
  13.9 0.3 collective-permute-start.5
  14.2 0.8 %collective-permute-done.3 = f32[128,128]{1,0:T(8,128)S(1)} collective-permute-done((f32[128,128]{1,0:T(8,128)S(1)}, f32[128,128]{1,0:T(8,128)S(1)}, u32[]{:S(2)}, u32[]{:S(2)}) %collective-permute-start.3) | collective-permute-done | bytes 65568 | tf_op jit(solution)/shard_map/ppermute | solution.py:131
  14.9 1.7 %collective-permute-done.4 = f32[128,128]{1,0:T(8,128)S(1)} collective-permute-done((f32[128,128]{1,0:T(8,128)S(1)}, f32[128,128]{1,0:T(8,128)S(1)}, u32[]{:S(2)}, u32[]{:S(2)}) %collective-permute-start.4) | collective-permute-done | bytes 65568 | tf_op jit(solution)/shard_map/ppermute | solution.py:131
  16.6 2.4 %collective-permute-done.5 = f32[128,128]{1,0:T(8,128)S(1)} collective-permute-done((f32[128,128]{1,0:T(8,128)S(1)}, f32[128,128]{1,0:T(8,128)S(1)}, u32[]{:S(2)}, u32[]{:S(2)}) %collective-permute-start.5) | collective-permute-done | bytes 65568 | tf_op jit(solution)/shard_map/ppermute | solution.py:131
  19.9 0.3 layout.1
  20.4 0.2 copy-done.4
  20.6 6.1 %observe.1 = (f32[128,128]{1,0:T(8,128)S(1)}, f32[128,128]{1,0:T(8,128)S(1)}) custom-call(f32[128,128]{1,0:T(8,128)S(1)} %add_add_fusion.mine, f32[128,128]{1,0:T(8,128)S(1)} %collective-permute-done.6.other, bf16[256,1024]{1,0:T(8,128)(2,1)S(1)} %get-tuple-element.17.by_column, bf16[1024,256]{1,0:T(8,128)(2,1)S(1)} %get-tuple-element.18.by_slot, ...), custom_call_target="tpu_custom_call" | custom-call | tf_op jit(solution)/shard_map/observe/pallas_call | solution.py:277
  26.7 0.5 %collective-permute-start.7 = (f32[128,128]{1,0:T(8,128)S(1)}, f32[128,128]{1,0:T(8,128)S(1)}, u32[]{:S(2)}, u32[]{:S(2)}) collective-permute-start(f32[128,128]{1,0:T(8,128)S(1)} %get-tuple-element.21), channel_id=1, source_target_pairs={{0,4},{4,0},{8,12},{12,8},{16,20},{20,16},{24,28},{28,24},{1,5},{5... | collective-permute-start | bytes 196616 | tf_op jit(solution)/shard_map/ppermute | solution.py:131
  27.3 0.9 %collective-permute-done.7 = f32[128,128]{1,0:T(8,128)S(1)} collective-permute-done((f32[128,128]{1,0:T(8,128)S(1)}, f32[128,128]{1,0:T(8,128)S(1)}, u32[]{:S(2)}, u32[]{:S(2)}) %collective-permute-start.7) | collective-permute-done | bytes 65568 | tf_op jit(solution)/shard_map/ppermute | solution.py:131
  28.2 0.6 %collective-permute-start.10 = (f32[32,128]{1,0:T(8,128)S(1)}, f32[32,128]{1,0:T(8,128)S(1)}, u32[]{:S(2)}, u32[]{:S(2)}) collective-permute-start(f32[32,128]{1,0:T(8,128)S(1)} %get-tuple-element.25), channel_id=1, source_target_pairs={{0,16},{4,20},{8,24},{12,28},{16,0},{20,4},{24,8},{28,12},{1,17},{... | collective-permute-start | bytes 49160 | tf_op jit(solution)/shard_map/ppermute | solution.py:131
  28.8 1.5 %collective-permute-start.8 = (f32[32,128]{1,0:T(8,128)S(1)}, f32[32,128]{1,0:T(8,128)S(1)}, u32[]{:S(2)}, u32[]{:S(2)}) collective-permute-start(f32[32,128]{1,0:T(8,128)S(1)} %get-tuple-element.24), channel_id=1, source_target_pairs={{0,24},{4,28},{8,16},{12,20},{16,8},{20,12},{24,0},{28,4},{1,25},{... | collective-permute-start | bytes 49160 | tf_op jit(solution)/shard_map/ppermute | solution.py:131
  30.3 1.5 %collective-permute-start.9 = (f32[32,128]{1,0:T(8,128)S(1)}, f32[32,128]{1,0:T(8,128)S(1)}, u32[]{:S(2)}, u32[]{:S(2)}) collective-permute-start(f32[32,128]{1,0:T(8,128)S(1)} %get-tuple-element.26), channel_id=1, source_target_pairs={{0,8},{4,12},{8,0},{12,4},{16,24},{20,28},{24,16},{28,20},{1,9},{5... | collective-permute-start | bytes 49160 | tf_op jit(solution)/shard_map/ppermute | solution.py:131
  31.8 0.6 %multiply_bitcast_fusion = f32[32,128]{1,0:T(8,128)} fusion(f32[4,32,128]{2,1,0:T(8,128)S(1)} %bitcast.34, s32[]{:T(128)S(6)} %select_n.59), kind=kLoop, calls=%fused_computation.7 | loop fusion | flops 4096 | bytes 32772 | tf_op jit(solution)/shard_map/mul | solution.py:316
  32.4 1.0 %collective-permute-done.8 = f32[32,128]{1,0:T(8,128)S(1)} collective-permute-done((f32[32,128]{1,0:T(8,128)S(1)}, f32[32,128]{1,0:T(8,128)S(1)}, u32[]{:S(2)}, u32[]{:S(2)}) %collective-permute-start.8) | collective-permute-done | bytes 16416 | tf_op jit(solution)/shard_map/ppermute | solution.py:131
  33.4 0.6 %collective-permute-done.9 = f32[32,128]{1,0:T(8,128)S(1)} collective-permute-done((f32[32,128]{1,0:T(8,128)S(1)}, f32[32,128]{1,0:T(8,128)S(1)}, u32[]{:S(2)}, u32[]{:S(2)}) %collective-permute-start.9) | collective-permute-done | bytes 16416 | tf_op jit(solution)/shard_map/ppermute | solution.py:131
  34.0 0.6 %fusion.1 = f32[32,128]{1,0:T(8,128)} fusion(f32[32,128]{1,0:T(8,128)S(1)} %collective-permute-done.10, f32[32,128]{1,0:T(8,128)S(1)} %collective-permute-done.9, f32[32,128]{1,0:T(8,128)S(1)} %collective-permute-done.8, f32[4,32,128]{2,1,0:T(8,128)S(1)} %bitcast.40, s32[]{:T(128)S(6)} %select_n.63), kind=kLoop, calls=%fused_computation.3 | loop fusion | flops 12288 | bytes 81924 | tf_op jit(solution)/shard_map/add | solution.py:162
  (24 shorter events, 0.4 us)
Async XLA Ops:
  1.4 7.7 %collective-permute-start = (f32[8,8,128]{2,1,0:T(8,128)S(1)}, f32[8,8,128]{2,1,0:T(8,128)S(1)}, u32[]{:S(2)}, u32[]{:S(2)}) collective-permute-start(f32[8,8,128]{2,1,0:T(8,128)S(1)} %get-tuple-element.23), channel_id=1, source_target_pairs={{0,1},{1,2},{2,3},{3,0},{4,5},{5,6},{6,7},{7,4},{8,9},{9,10},{10,1... | collective-permute-start | bytes 98312 | tf_op jit(solution)/shard_map/ppermute | solution.py:35
  4.4 4.7 %collective-permute-start.1 = (f32[8,8,128]{2,1,0:T(8,128)S(1)}, f32[8,8,128]{2,1,0:T(8,128)S(1)}, u32[]{:S(2)}, u32[]{:S(2)}) collective-permute-start(f32[8,8,128]{2,1,0:T(8,128)S(1)} %get-tuple-element.22), channel_id=1, source_target_pairs={{1,0},{2,1},{3,2},{0,3},{5,4},{6,5},{7,6},{4,7},{9,8},{10,9},{11,1... | collective-permute-start | bytes 98312 | tf_op jit(solution)/shard_map/ppermute | solution.py:35
  6.5 13.9 %copy-start.1 = (bf16[2048,128]{1,0:T(8,128)(2,1)S(1)}, bf16[2048,128]{1,0:T(8,128)(2,1)}, u32[]{:S(2)}) copy-start(bf16[2048,128]{1,0:T(8,128)(2,1)} %w_out.1) | copy-start | bytes 1572868
  6.5 13.9 %copy-start.3 = (bf16[1,1,1024,128]{3,2,1,0:T(8,128)(2,1)S(1)}, bf16[1,1,1024,128]{3,2,1,0:T(8,128)(2,1)}, u32[]{:S(2)}) copy-start(bf16[1,1,1024,128]{3,2,1,0:T(8,128)(2,1)} %param.15) | copy-start | bytes 786436
  9.0 11.3 %copy-start = (bf16[128,2048]{1,0:T(8,128)(2,1)S(1)}, bf16[128,2048]{1,0:T(8,128)(2,1)}, u32[]{:S(2)}) copy-start(bf16[128,2048]{1,0:T(8,128)(2,1)} %w_in.1) | copy-start | bytes 1572868
  9.3 1.3 %collective-permute-start.2 = (f32[128,128]{1,0:T(8,128)S(1)}, f32[128,128]{1,0:T(8,128)S(1)}, u32[]{:S(2)}, u32[]{:S(2)}) collective-permute-start(f32[128,128]{1,0:T(8,128)S(1)} %get-tuple-element.16), channel_id=1, source_target_pairs={{0,4},{4,0},{8,12},{12,8},{16,20},{20,16},{24,28},{28,24},{1,5},{5... | collective-permute-start | bytes 196616 | tf_op jit(solution)/shard_map/ppermute | solution.py:131
  10.6 9.8 %copy-start.2 = (bf16[1,1,1024,128]{3,2,1,0:T(8,128)(2,1)S(1)}, bf16[1,1,1024,128]{3,2,1,0:T(8,128)(2,1)}, u32[]{:S(2)}) copy-start(bf16[1,1,1024,128]{3,2,1,0:T(8,128)(2,1)} %param.14) | copy-start | bytes 786436
  10.6 8.5 %copy-start.6 = (s32[1,1,1024]{2,1,0:T(1,128)S(1)}, s32[1,1,1024]{2,1,0:T(1,128)}, u32[]{:S(2)}) copy-start(s32[1,1,1024]{2,1,0:T(1,128)} %param.12) | copy-start | bytes 12292
  10.6 4.3 %collective-permute-start.3 = (f32[128,128]{1,0:T(8,128)S(1)}, f32[128,128]{1,0:T(8,128)S(1)}, u32[]{:S(2)}, u32[]{:S(2)}) collective-permute-start(f32[128,128]{1,0:T(8,128)S(1)} %add.86), channel_id=1, source_target_pairs={{0,8},{4,12},{8,0},{12,4},{16,24},{20,28},{24,16},{28,20},{1,9},{5... | collective-permute-start | bytes 196616 | tf_op jit(solution)/shard_map/ppermute | solution.py:131
  12.3 4.3 %collective-permute-start.4 = (f32[128,128]{1,0:T(8,128)S(1)}, f32[128,128]{1,0:T(8,128)S(1)}, u32[]{:S(2)}, u32[]{:S(2)}) collective-permute-start(f32[128,128]{1,0:T(8,128)S(1)} %add.86), channel_id=1, source_target_pairs={{0,16},{4,20},{8,24},{12,28},{16,0},{20,4},{24,8},{28,12},{1,17},{... | collective-permute-start | bytes 196616 | tf_op jit(solution)/shard_map/ppermute | solution.py:131
  13.9 5.2 %collective-permute-start.5 = (f32[128,128]{1,0:T(8,128)S(1)}, f32[128,128]{1,0:T(8,128)S(1)}, u32[]{:S(2)}, u32[]{:S(2)}) collective-permute-start(f32[128,128]{1,0:T(8,128)S(1)} %add.86), channel_id=1, source_target_pairs={{0,24},{4,28},{8,16},{12,20},{16,8},{20,12},{24,0},{28,4},{1,25},{... | collective-permute-start | bytes 196616 | tf_op jit(solution)/shard_map/ppermute | solution.py:131
  19.0 1.3 %collective-permute-start.6 = (f32[128,128]{1,0:T(8,128)S(1)}, f32[128,128]{1,0:T(8,128)S(1)}, u32[]{:S(2)}, u32[]{:S(2)}) collective-permute-start(f32[128,128]{1,0:T(8,128)S(1)} %add_add_fusion.mine), channel_id=1, source_target_pairs={{0,4},{4,0},{8,12},{12,8},{16,20},{20,16},{24,28},{28,24},{1,5},{5... | collective-permute-start | bytes 196616 | tf_op jit(solution)/shard_map/ppermute | solution.py:131
  19.1 0.7 %copy-start.5 = (f32[1,1,1024]{2,1,0:T(1,128)S(1)}, f32[1,1,1024]{2,1,0:T(1,128)}, u32[]{:S(2)}) copy-start(f32[1,1,1024]{2,1,0:T(1,128)} %param.16) | copy-start | bytes 12292
  19.9 0.7 %copy-start.4 = (f32[2048]{0:T(1024)S(1)}, f32[2048]{0:T(1024)}, u32[]{:S(2)}) copy-start(f32[2048]{0:T(1024)} %param.18) | copy-start | bytes 24580
  26.7 1.4 %collective-permute-start.7 = (f32[128,128]{1,0:T(8,128)S(1)}, f32[128,128]{1,0:T(8,128)S(1)}, u32[]{:S(2)}, u32[]{:S(2)}) collective-permute-start(f32[128,128]{1,0:T(8,128)S(1)} %get-tuple-element.21), channel_id=1, source_target_pairs={{0,4},{4,0},{8,12},{12,8},{16,20},{20,16},{24,28},{28,24},{1,5},{5... | collective-permute-start | bytes 196616 | tf_op jit(solution)/shard_map/ppermute | solution.py:131
  28.2 4.2 %collective-permute-start.10 = (f32[32,128]{1,0:T(8,128)S(1)}, f32[32,128]{1,0:T(8,128)S(1)}, u32[]{:S(2)}, u32[]{:S(2)}) collective-permute-start(f32[32,128]{1,0:T(8,128)S(1)} %get-tuple-element.25), channel_id=1, source_target_pairs={{0,16},{4,20},{8,24},{12,28},{16,0},{20,4},{24,8},{28,12},{1,17},{... | collective-permute-start | bytes 49160 | tf_op jit(solution)/shard_map/ppermute | solution.py:131
  28.8 4.6 %collective-permute-start.8 = (f32[32,128]{1,0:T(8,128)S(1)}, f32[32,128]{1,0:T(8,128)S(1)}, u32[]{:S(2)}, u32[]{:S(2)}) collective-permute-start(f32[32,128]{1,0:T(8,128)S(1)} %get-tuple-element.24), channel_id=1, source_target_pairs={{0,24},{4,28},{8,16},{12,20},{16,8},{20,12},{24,0},{28,4},{1,25},{... | collective-permute-start | bytes 49160 | tf_op jit(solution)/shard_map/ppermute | solution.py:131
  30.3 3.7 %collective-permute-start.9 = (f32[32,128]{1,0:T(8,128)S(1)}, f32[32,128]{1,0:T(8,128)S(1)}, u32[]{:S(2)}, u32[]{:S(2)}) collective-permute-start(f32[32,128]{1,0:T(8,128)S(1)} %get-tuple-element.26), channel_id=1, source_target_pairs={{0,8},{4,12},{8,0},{12,4},{16,24},{20,28},{24,16},{28,20},{1,9},{5... | collective-permute-start | bytes 49160 | tf_op jit(solution)/shard_map/ppermute | solution.py:131

commit v5 on v4

--- a/solution.py
+++ b/solution.py
@@ -32,48 +32,85 @@
     backward = [(target, source) for source, target in forward]
     first = block[:, :EDGE].astype(jnp.float32)
     last = block[:, -EDGE:].astype(jnp.float32)
-    return lax.ppermute(last, axis, forward), lax.ppermute(first, axis, backward)
+    low = lax.ppermute(last, axis, forward)
+    high = lax.ppermute(first, axis, backward)
+    return low, high
 
 
 def swept(field):
     rows = field.shape[0]
-    for sweep_index in range(SWEEPS):
+    for _ in range(SWEEPS):
         low = pltpu.roll(field, 1, 0)
         high = pltpu.roll(field, rows - 1, 0)
         field = field + diffusion * ((low - 2.0 * field) + high)
     return field
 
 
-def inside_kernel(control, perturb, total, ends, factors, fields, weights, arrived):
+def stencil_matrix(columns):
+    taps = [1.0]
+    for _ in range(SWEEPS):
+        wide = [0.0] + taps + [0.0]
+        taps = [
+            (1.0 - 2.0 * diffusion) * wide[i]
+            + diffusion * ((wide[i - 1] if i else 0.0) + (wide[i + 1] if i + 1 < len(wide) else 0.0))
+            for i in range(len(wide))
+        ]
+    row = lax.broadcasted_iota(jnp.int32, (columns, columns), 0)
+    apart = jnp.abs(row - lax.broadcasted_iota(jnp.int32, (columns, columns), 1))
+    matrix = jnp.zeros((columns, columns), jnp.float32)
+    for distance in range(SWEEPS + 1):
+        matrix = jnp.where(apart == distance, taps[SWEEPS + distance], matrix)
+    top = matrix.astype(jnp.bfloat16)
+    return top, (matrix - top.astype(jnp.float32)).astype(jnp.bfloat16)
+
+
+def inside_kernel(core, control, perturb, keep, send, ends, factors, fields, weights, total, arrived, *, owners):
     members, columns, levels = control.shape
     copies = []
     for member in range(members):
+        lanes = slice(member * levels, (member + 1) * levels)
         copies.append((
-            pltpu.make_async_copy(control.at[member], fields.at[member], arrived.at[0, member]),
-            pltpu.make_async_copy(perturb.at[member], weights.at[member], arrived.at[1, member]),
+            pltpu.make_async_copy(control.at[member], fields.at[:, lanes], arrived.at[0, member]),
+            pltpu.make_async_copy(perturb.at[member], weights.at[:, lanes], arrived.at[1, member]),
         ))
     for pair in copies:
         for copy in pair:
             copy.start()
+    top, rest = stencil_matrix(columns)
     summed = None
-    for member in range(members):
-        for copy in copies[member]:
-            copy.wait()
-        field = fields[member].astype(jnp.float32)
-        factor = weights[member].astype(jnp.float32)
-        ends[member, :EDGE] = field[:EDGE]
-        ends[member, EDGE:] = field[columns - EDGE:]
-        factors[member, :EDGE] = factor[:EDGE]
-        factors[member, EDGE:] = factor[columns - EDGE:]
-        part = swept(field) * factor
-        summed = part if summed is None else summed + part
+    group = 2 if members % 2 == 0 else 1
+    for first in range(0, members, group):
+        for member in range(first, first + group):
+            for copy in copies[member]:
+                copy.wait()
+        lanes = slice(first * levels, (first + group) * levels)
+        field = fields[:, lanes]
+        factor = weights[:, lanes].astype(jnp.float32)
+        local = jnp.dot(top, field, preferred_element_type=jnp.float32)
+        local = local + jnp.dot(rest, field, preferred_element_type=jnp.float32)
+        product = local * factor
+        for step in range(group):
+            here = slice(step * levels, (step + 1) * levels)
+            summed = product[:, here] if summed is None else summed + product[:, here]
+            member = first + step
+            ends[member, :EDGE] = field[:EDGE, here].astype(jnp.float32)
+            ends[member, EDGE:] = field[columns - EDGE:, here].astype(jnp.float32)
+            factors[member, :EDGE] = factor[:EDGE, here]
+            factors[member, EDGE:] = factor[columns - EDGE:, here]
+    rows = lax.broadcasted_iota(jnp.int32, (EDGE, levels), 0)
     total[...] = summed
-
-
-def edge_kernel(core, inside, ends, factors, low, high, keep, send, total, *, owners):
-    members = ends.shape[0]
-    columns, levels = total.shape
-    total[...] = inside[...]
+    total[:EDGE] = jnp.where(rows < SWEEPS, 0.0, summed[:EDGE])
+    total[columns - EDGE:] = jnp.where(rows >= EDGE - SWEEPS, 0.0, summed[columns - EDGE:])
+    owned = columns // owners
+    for chip in range(owners // 2):
+        here = pl.multiple_of((2 * chip + core[0]) * owned, owned)
+        there = pl.multiple_of((2 * chip + 1 - core[0]) * owned, owned)
+        keep[chip * owned:(chip + 1) * owned] = total[pl.ds(here, owned)]
+        send[chip * owned:(chip + 1) * owned] = total[pl.ds(there, owned)]
+
+
+def edge_kernel(ends, factors, low, high, edges):
+    members, _, levels = ends.shape
     windows = []
     for member in range(members):
         windows += [low[member], ends[member], high[member]]
@@ -86,44 +123,38 @@
         start = start + field[base:base + EDGE] * factors[member, :EDGE]
         stop = stop + field[base + EDGE:base + 2 * EDGE] * factors[member, EDGE:]
     rows = lax.broadcasted_iota(jnp.int32, (EDGE, levels), 0)
-    total[:EDGE] = jnp.where(rows < SWEEPS, start, total[:EDGE])
-    total[columns - EDGE:] = jnp.where(rows >= EDGE - SWEEPS, stop, total[columns - EDGE:])
-    owned = columns // owners
-    for chip in range(owners // 2):
-        here = pl.multiple_of((2 * chip + core[0]) * owned, owned)
-        there = pl.multiple_of((2 * chip + 1 - core[0]) * owned, owned)
-        keep[chip * owned:(chip + 1) * owned] = total[pl.ds(here, owned)]
-        send[chip * owned:(chip + 1) * owned] = total[pl.ds(there, owned)]
+    edges[:EDGE] = jnp.where(rows < SWEEPS, start, 0.0)
+    edges[EDGE:] = jnp.where(rows >= EDGE - SWEEPS, stop, 0.0)
 
 
 def member_sum(control, perturb, core, owners):
     members, columns, levels = control.shape
     low, high = edge_columns(control, "sub")
     ends = pltpu.VMEM((members, 2 * EDGE, levels), jnp.float32)
-    whole = pltpu.VMEM((columns, levels), jnp.float32)
-    total, fields, factors = pl.pallas_call(
-        inside_kernel,
-        out_shape=(whole, ends, ends),
-        in_specs=[pl.BlockSpec(memory_space=pltpu.HBM)] * 2,
-        out_specs=(ON_CHIP,) * 3,
+    half = pltpu.VMEM((columns // 2, levels), jnp.float32)
+    keep, send, fields, factors = pl.pallas_call(
+        functools.partial(inside_kernel, owners=owners),
+        out_shape=(half, half, ends, ends),
+        in_specs=[pl.BlockSpec(memory_space=pltpu.SMEM)] + [pl.BlockSpec(memory_space=pltpu.HBM)] * 2,
+        out_specs=(ON_CHIP,) * 4,
         scratch_shapes=[
-            pltpu.VMEM(control.shape, control.dtype),
-            pltpu.VMEM(perturb.shape, perturb.dtype),
+            pltpu.VMEM((columns, members * levels), control.dtype),
+            pltpu.VMEM((columns, members * levels), perturb.dtype),
+            pltpu.VMEM((columns, levels), jnp.float32),
             pltpu.SemaphoreType.DMA((2, members)),
         ],
         compiler_params=room(16),
         name="inside",
-    )(*(pltpu.with_memory_space_constraint(a, pltpu.HBM) for a in (control, perturb)))
-    half = pltpu.VMEM((columns // 2, levels), jnp.float32)
-    return pl.pallas_call(
-        functools.partial(edge_kernel, owners=owners),
-        out_shape=(half, half),
-        in_specs=[pl.BlockSpec(memory_space=pltpu.SMEM)] + [ON_CHIP] * 5,
-        out_specs=(ON_CHIP,) * 2,
-        scratch_shapes=[whole],
+    )(core, *(pltpu.with_memory_space_constraint(a, pltpu.HBM) for a in (control, perturb)))
+    edges = pl.pallas_call(
+        edge_kernel,
+        out_shape=pltpu.VMEM((2 * EDGE, levels), jnp.float32),
+        in_specs=[ON_CHIP] * 4,
+        out_specs=ON_CHIP,
         compiler_params=room(16),
         name="edges",
-    )(core, *near(total, fields, factors, low, high))
+    )(*near(fields, factors, low, high))
+    return keep, send, edges
 
 
 def bit_swap(block, axis, bit):
@@ -135,9 +166,10 @@
     return lax.squeeze(lax.dynamic_slice_in_dim(block, which, 1, dim), (dim,))
 
 
-def reduce_pairs(keep, send, axis):
+def reduce_pairs(keep, send, edges, layouts, axis):
     count = lax.axis_size(axis)
-    mine = keep + bit_swap(send, axis, 1)
+    arrived = bit_swap(send, axis, 1)
+    mine = jnp.concatenate([keep + arrived, edges], axis=0)
     if count <= 8:
         parts = [bit_swap(mine, axis, bit) for bit in range(2, count, 2)]
         for part in parts:
@@ -145,7 +177,8 @@
     else:
         for step in range(1, count.bit_length() - 1):
             mine = mine + bit_swap(mine, axis, 1 << step)
-    return mine, bit_swap(mine, axis, 1)
+    mine, layouts = lax.optimization_barrier((mine, layouts))
+    return mine, bit_swap(mine, axis, 1), layouts
 
 
 def scatter_pairs(keep, send, axis):
@@ -196,12 +229,25 @@
 
 
 def observe_kernel(
-    mine, other, by_column, by_slot, spread, background, targets, w_in, b_in, w_out, keep, send, slope, *, scale, block, chunk
+    core, mine, other, by_column, by_slot, spread, background, targets, w_in, b_in, w_out, keep, send, whole, slope, *, scale, block, chunk
 ):
     slots, levels = background.shape
-    half_columns = mine.shape[0]
+    half_columns = mine.shape[0] - 2 * EDGE
     hidden = w_in.shape[1]
-    increment = jnp.concatenate([mine[...], other[...]], axis=0) * scale
+    edges = mine[half_columns:] + other[half_columns:]
+    first = edges[:EDGE]
+    last = edges[EDGE:]
+    even = core[0] == 0
+    none = jnp.zeros_like(first)
+    parts = []
+    for rows, low, high in ((mine, even, ~even), (other, ~even, even)):
+        parts += [
+            rows[:EDGE] + jnp.where(low, first, none),
+            rows[EDGE:half_columns - EDGE],
+            rows[half_columns - EDGE:half_columns] + jnp.where(high, last, none),
+        ]
+    increment = jnp.concatenate(parts, axis=0) * scale
+    whole[...] = increment[:half_columns]
     top = increment.astype(jnp.bfloat16)
     rest = (increment - top.astype(jnp.float32)).astype(jnp.bfloat16)
     table = jnp.concatenate([top, rest], axis=1)
@@ -270,19 +316,19 @@
     return part
 
 
-def observe_call(mine, other, by_column, by_slot, spread, background, targets, w_in, b_in, w_out, scale):
+def observe_call(core, mine, other, by_column, by_slot, spread, background, targets, w_in, b_in, w_out, scale):
     block = largest_part(background.shape[0], 512)
     chunk = largest_part(w_in.shape[1], 256)
-    half = pltpu.VMEM(mine.shape, jnp.float32)
+    half = pltpu.VMEM((mine.shape[0] - 2 * EDGE, mine.shape[1]), jnp.float32)
     return pl.pallas_call(
         functools.partial(observe_kernel, scale=scale, block=block, chunk=chunk),
-        out_shape=(half, half),
-        in_specs=[ON_CHIP] * 10,
-        out_specs=(ON_CHIP, ON_CHIP),
+        out_shape=(half,) * 3,
+        in_specs=[pl.BlockSpec(memory_space=pltpu.SMEM)] + [ON_CHIP] * 10,
+        out_specs=(ON_CHIP,) * 3,
         scratch_shapes=[pltpu.VMEM((2, block, w_in.shape[1]), jnp.float32)],
         compiler_params=room(32),
         name="observe",
-    )(*near(mine, other, by_column, by_slot, spread, background, targets, w_in, b_in, w_out))
+    )(core, *near(mine, other, by_column, by_slot, spread, background, targets, w_in, b_in, w_out))
 
 
 def per_device(
@@ -306,20 +352,20 @@
     indices = obs_column.reshape(1, -1)
     slots = indices.shape[1]
     paired = count > 1 and count & (count - 1) == 0
-    core = me & 1 if paired else jnp.int32(0)
-    keep, send = member_sum(control, perturb, core.reshape(1), count if paired else 2)
+    core = (me & 1 if paired else jnp.int32(0)).reshape(1)
+    keep, send, edges = member_sum(control, perturb, core, count if paired else 2)
     if paired:
         owner = indices // owned
         side = ((owner ^ me) & 1) * (columns // 2)
         indices = side + (owner // 2) * owned + indices % owned
-        mine, other = reduce_pairs(keep, send, "mem")
-        increment = pick(mine.reshape(count // 2, owned, -1), 0, me // 2) * scale
+    layouts = layout_call(obs_count, indices, obs_weight.reshape(1, slots), columns, obs_value.shape[-1])
+    if paired:
+        mine, other, layouts = reduce_pairs(keep, send, edges, layouts, "mem")
     else:
-        summed = lax.psum(jnp.concatenate([keep, send], axis=0), "mem")
-        mine, other = summed[: columns // 2], summed[columns // 2 :]
-        increment = lax.dynamic_slice_in_dim(summed, me * owned, owned, 0) * scale
-    layouts = layout_call(obs_count, indices, obs_weight.reshape(1, slots), columns, obs_value.shape[-1])
-    keep, send = observe_call(
+        mine = lax.psum(jnp.concatenate([keep, edges], axis=0), "mem")
+        other = jnp.pad(lax.psum(send, "mem"), ((0, edges.shape[0]), (0, 0)))
+    keep, send, whole = observe_call(
+        core,
         mine,
         other,
         *layouts,
@@ -331,8 +377,13 @@
         scale,
     )
     if paired:
+        increment = pick(whole.reshape(count // 2, owned, -1), 0, me // 2)
         grad_columns = scatter_pairs(keep, send, "mem")
     else:
+        halo = mine[columns // 2 :]
+        full = jnp.concatenate([mine[: columns // 2], other[: columns // 2]], axis=0)
+        full = full.at[:EDGE].add(halo[:EDGE]).at[-EDGE:].add(halo[EDGE:])
+        increment = lax.dynamic_slice_in_dim(full, me * owned, owned, 0) * scale
         gradient = jnp.concatenate([keep, send], axis=0)
         grad_columns = lax.psum_scatter(gradient, "mem", scatter_dimension=0, tiled=True)
     return (increment, grad_columns)

time: 34.9 us -> 35.5 us (1.017)
  waiting for transfers between devices: 8.77 us -> 9.97 us
  other arithmetic: 2.06 us -> 1.47 us
  local copies, waits for them, and re-layouts: 0.23 us -> 0.66 us
    ppermute x2, waiting for transfers between devices: 0.01 us -> 2.27 us  [the longest x1 1.96 us: edge_columns(): low = lax.ppermute(last, axis, forward)]
    ppermute x9, waiting for transfers between devices: 8.76 us -> 7.7 us  [bit_swap(): return lax.ppermute(block, axis, [(i, i ^ bit) for i in range(count)])]
    mul x1 -> x0, other arithmetic: 0.61 us -> none  [per_device(): increment = pick(mine.reshape(count // 2, owned, -1), 0, me // 2) * scale]
    squeeze x1 -> x2, local copies, waits for them, and re-layouts: 0.01 us -> 0.62 us  [pick(): return lax.squeeze(lax.dynamic_slice_in_dim(block, which, 1, dim), (dim,))]
    ppermute x2, starting transfers between devices: 5.14 us -> 4.73 us  [the longest x1 2.64 us: edge_columns(): low = lax.ppermute(last, axis, forward)]
  transfers between devices with their start and end apart: 11 -> 11, of which waited for: 8 -> 8; matrix products, arithmetic and copies ran while one was open for 2% -> 4% of each run, Pallas kernels for 8% -> 1%
where the time goes in v5:
time: 35.5 us; the launch traced here: 35.4 us
  starting transfers between devices  12.7 us (36%)
  waiting for transfers between devices  9.97 us (28%)
  Pallas kernels  9.15 us (26%)
  other arithmetic  1.47 us (4%)
  between operations  1.45 us (4%)
  local copies, waits for them, and re-layouts  0.66 us (2%)
    ppermute x9, starting transfers between devices, bit_swap(): return lax.ppermute(block, axis, [(i, i ^ bit) for i in range(count)])  7.95 us
    ppermute x9, waiting for transfers between devices, bit_swap(): return lax.ppermute(block, axis, [(i, i ^ bit) for i in range(count)])  7.7 us
    pallas_call x1, Pallas kernels, observe_call(): pl.pallas_call(functools.partial(observe_kernel, scale=scale, block=block...  6.32 us
    ppermute x1, starting transfers between devices, edge_columns(): low = lax.ppermute(last, axis, forward)  2.64 us
    pallas_call x1, Pallas kernels, member_sum(): pl.pallas_call(functools.partial(inside_kernel, owners=owners), out_shape...  2.31 us
    ppermute x1, starting transfers between devices, edge_columns(): high = lax.ppermute(first, axis, backward)  2.08 us
    ppermute x1, waiting for transfers between devices, edge_columns(): low = lax.ppermute(last, axis, forward)  1.96 us
    convert_element_type x1, other arithmetic, edge_columns(): first = block[:, :EDGE].astype(jnp.float32)  0.74 us
  transfers between devices with their start and end apart: 11, of which 8 were waited for; matrix products, arithmetic and copies ran while one was open for 4% of the time, Pallas kernels for 1%

profile of v5, /device:TPU:0, one launch (start us, length us, event | category | flops | bytes accessed | tf_op | source)
XLA Modules:
  0.0 35.4 jit_solution(17846802921975704493)
XLA Ops:
  0.7 2.3 %inside.1 = (f32[128,128]{1,0:T(8,128)S(1)}, f32[128,128]{1,0:T(8,128)S(1)}, f32[8,16,128]{2,1,0:T(8,128)S(1)}, f32[8,16,128]{2,1,0:T(8,128)S(1)}) custom-call(s32[1]{0:T(128)} %bitcast.core, bf16[8,256,128]{2,1,0:T(8,128)(2,1)} %control.1, bf16[8,256,128]{2,1,0:T(8,128)(2,1)} %perturb.1), custom_call_target="tpu_custom_call" | custom-call | tf_op jit(solution)/shard_map/inside/pallas_call | solution.py:135
  3.0 0.6 %collective-permute-start = (f32[128,128]{1,0:T(8,128)S(1)}, f32[128,128]{1,0:T(8,128)S(1)}, u32[]{:S(2)}, u32[]{:S(2)}) collective-permute-start(f32[128,128]{1,0:T(8,128)S(1)} %get-tuple-element.17), channel_id=1, source_target_pairs={{0,4},{4,0},{8,12},{12,8},{16,20},{20,16},{24,28},{28,24},{1,5},{5... | collective-permute-start | bytes 196616 | tf_op jit(solution)/shard_map/ppermute | solution.py:162
  3.6 0.7 %slice_convert_fusion = (f32[8,8,128]{2,1,0:T(8,128)S(1)}, f32[8,8,128]{2,1,0:T(8,128)S(1)}) fusion(bf16[8,256,128]{2,1,0:T(8,128)(2,1)} %control.1), kind=kLoop, calls=%fused_computation.9 | loop fusion | flops 16384 | bytes 98304 | tf_op jit(solution)/shard_map/convert_element_type | solution.py:33
  4.3 2.6 %collective-permute-start.1 = (f32[8,8,128]{2,1,0:T(8,128)S(1)}, f32[8,8,128]{2,1,0:T(8,128)S(1)}, u32[]{:S(2)}, u32[]{:S(2)}) collective-permute-start(f32[8,8,128]{2,1,0:T(8,128)S(1)} %get-tuple-element.31), channel_id=1, source_target_pairs={{0,1},{1,2},{2,3},{3,0},{4,5},{5,6},{6,7},{7,4},{8,9},{9,10},{10,1... | collective-permute-start | bytes 98312 | tf_op jit(solution)/shard_map/ppermute | solution.py:35
  7.0 2.1 %collective-permute-start.2 = (f32[8,8,128]{2,1,0:T(8,128)S(1)}, f32[8,8,128]{2,1,0:T(8,128)S(1)}, u32[]{:S(2)}, u32[]{:S(2)}) collective-permute-start(f32[8,8,128]{2,1,0:T(8,128)S(1)} %get-tuple-element.30), channel_id=1, source_target_pairs={{1,0},{2,1},{3,2},{0,3},{5,4},{6,5},{7,6},{4,7},{9,8},{10,9},{11,1... | collective-permute-start | bytes 98312 | tf_op jit(solution)/shard_map/ppermute | solution.py:36
  9.0 2.0 %collective-permute-done.1.low = f32[8,8,128]{2,1,0:T(8,128)S(1)} collective-permute-done((f32[8,8,128]{2,1,0:T(8,128)S(1)}, f32[8,8,128]{2,1,0:T(8,128)S(1)}, u32[]{:S(2)}, u32[]{:S(2)}) %collective-permute-start.1) | collective-permute-done | bytes 32800 | tf_op jit(solution)/shard_map/ppermute | solution.py:35
  11.0 0.3 collective-permute-done.2.high
  11.5 1.6 %collective-permute-start.3 = (f32[144,128]{1,0:T(8,128)S(1)}, f32[144,128]{1,0:T(8,128)S(1)}, u32[]{:S(2)}, u32[]{:S(2)}) collective-permute-start(f32[144,128]{1,0:T(8,128)S(1)} %pad_maximum_fusion), channel_id=1, source_target_pairs={{0,8},{4,12},{8,0},{12,4},{16,24},{20,28},{24,16},{28,20},{1,9},{5... | collective-permute-start | bytes 221192 | tf_op jit(solution)/shard_map/ppermute | solution.py:162
  13.1 1.5 %collective-permute-start.4 = (f32[144,128]{1,0:T(8,128)S(1)}, f32[144,128]{1,0:T(8,128)S(1)}, u32[]{:S(2)}, u32[]{:S(2)}) collective-permute-start(f32[144,128]{1,0:T(8,128)S(1)} %pad_maximum_fusion), channel_id=1, source_target_pairs={{0,16},{4,20},{8,24},{12,28},{16,0},{20,4},{24,8},{28,12},{1,17},{... | collective-permute-start | bytes 221192 | tf_op jit(solution)/shard_map/ppermute | solution.py:162
  14.6 0.5 %collective-permute-start.5 = (f32[144,128]{1,0:T(8,128)S(1)}, f32[144,128]{1,0:T(8,128)S(1)}, u32[]{:S(2)}, u32[]{:S(2)}) collective-permute-start(f32[144,128]{1,0:T(8,128)S(1)} %pad_maximum_fusion), channel_id=1, source_target_pairs={{0,24},{4,28},{8,16},{12,20},{16,8},{20,12},{24,0},{28,4},{1,25},{... | collective-permute-start | bytes 221192 | tf_op jit(solution)/shard_map/ppermute | solution.py:162
  15.8 0.3 layout.1
  16.2 2.0 %collective-permute-done.4 = f32[144,128]{1,0:T(8,128)S(1)} collective-permute-done((f32[144,128]{1,0:T(8,128)S(1)}, f32[144,128]{1,0:T(8,128)S(1)}, u32[]{:S(2)}, u32[]{:S(2)}) %collective-permute-start.4) | collective-permute-done | bytes 73760 | tf_op jit(solution)/shard_map/ppermute | solution.py:162
  18.2 1.6 %collective-permute-done.5 = f32[144,128]{1,0:T(8,128)S(1)} collective-permute-done((f32[144,128]{1,0:T(8,128)S(1)}, f32[144,128]{1,0:T(8,128)S(1)}, u32[]{:S(2)}, u32[]{:S(2)}) %collective-permute-start.5) | collective-permute-done | bytes 73760 | tf_op jit(solution)/shard_map/ppermute | solution.py:162
  20.0 1.3 %collective-permute-done.6.other = f32[144,128]{1,0:T(8,128)S(1)} collective-permute-done((f32[144,128]{1,0:T(8,128)S(1)}, f32[144,128]{1,0:T(8,128)S(1)}, u32[]{:S(2)}, u32[]{:S(2)}) %collective-permute-start.6) | collective-permute-done | bytes 73760 | tf_op jit(solution)/shard_map/ppermute | solution.py:162
  21.3 6.3 %observe.1 = (f32[128,128]{1,0:T(8,128)S(1)}, f32[128,128]{1,0:T(8,128)S(1)}, f32[128,128]{1,0:T(8,128)S(1)}) custom-call(s32[1]{0:T(128)} %bitcast.core, f32[144,128]{1,0:T(8,128)S(1)} %add_add_fusion.mine, f32[144,128]{1,0:T(8,128)S(1)} %collective-permute-done.6.other, bf16[256,1024]{1,0:T(8,128)(2,1)S(1)} %get-tuple-element.24.by_column, ...), custom_call_target="tpu_custom_call" | custom-call | tf_op jit(solution)/shard_map/observe/pallas_call | solution.py:323
  27.6 0.2 collective-permute-start.7
  27.8 1.1 %collective-permute-done.7 = f32[128,128]{1,0:T(8,128)S(1)} collective-permute-done((f32[128,128]{1,0:T(8,128)S(1)}, f32[128,128]{1,0:T(8,128)S(1)}, u32[]{:S(2)}, u32[]{:S(2)}) %collective-permute-start.7) | collective-permute-done | bytes 65568 | tf_op jit(solution)/shard_map/ppermute | solution.py:162
  28.9 0.6 %collective-permute-start.10 = (f32[32,128]{1,0:T(8,128)S(1)}, f32[32,128]{1,0:T(8,128)S(1)}, u32[]{:S(2)}, u32[]{:S(2)}) collective-permute-start(f32[32,128]{1,0:T(8,128)S(1)} %get-tuple-element.33), channel_id=1, source_target_pairs={{0,16},{4,20},{8,24},{12,28},{16,0},{20,4},{24,8},{28,12},{1,17},{... | collective-permute-start | bytes 49160 | tf_op jit(solution)/shard_map/ppermute | solution.py:162
  29.5 1.5 %collective-permute-start.8 = (f32[32,128]{1,0:T(8,128)S(1)}, f32[32,128]{1,0:T(8,128)S(1)}, u32[]{:S(2)}, u32[]{:S(2)}) collective-permute-start(f32[32,128]{1,0:T(8,128)S(1)} %get-tuple-element.32), channel_id=1, source_target_pairs={{0,24},{4,28},{8,16},{12,20},{16,8},{20,12},{24,0},{28,4},{1,25},{... | collective-permute-start | bytes 49160 | tf_op jit(solution)/shard_map/ppermute | solution.py:162
  31.0 1.5 %collective-permute-start.9 = (f32[32,128]{1,0:T(8,128)S(1)}, f32[32,128]{1,0:T(8,128)S(1)}, u32[]{:S(2)}, u32[]{:S(2)}) collective-permute-start(f32[32,128]{1,0:T(8,128)S(1)} %get-tuple-element.34), channel_id=1, source_target_pairs={{0,8},{4,12},{8,0},{12,4},{16,24},{20,28},{24,16},{28,20},{1,9},{5... | collective-permute-start | bytes 49160 | tf_op jit(solution)/shard_map/ppermute | solution.py:162
  32.5 0.6 %dynamic-slice_bitcast_fusion.3 = f32[32,128]{1,0:T(8,128)} fusion(f32[4,32,128]{2,1,0:T(8,128)S(1)} %bitcast.37, s32[]{:T(128)S(6)} %select_n.62), kind=kLoop, calls=%fused_computation.8 | loop fusion | bytes 32772 | tf_op jit(solution)/shard_map/squeeze | solution.py:166
  33.1 1.0 %collective-permute-done.8 = f32[32,128]{1,0:T(8,128)S(1)} collective-permute-done((f32[32,128]{1,0:T(8,128)S(1)}, f32[32,128]{1,0:T(8,128)S(1)}, u32[]{:S(2)}, u32[]{:S(2)}) %collective-permute-start.8) | collective-permute-done | bytes 16416 | tf_op jit(solution)/shard_map/ppermute | solution.py:162
  34.2 0.6 %collective-permute-done.9 = f32[32,128]{1,0:T(8,128)S(1)} collective-permute-done((f32[32,128]{1,0:T(8,128)S(1)}, f32[32,128]{1,0:T(8,128)S(1)}, u32[]{:S(2)}, u32[]{:S(2)}) %collective-permute-start.9) | collective-permute-done | bytes 16416 | tf_op jit(solution)/shard_map/ppermute | solution.py:162
  34.7 0.6 %fusion.1 = f32[32,128]{1,0:T(8,128)} fusion(f32[32,128]{1,0:T(8,128)S(1)} %collective-permute-done.10, f32[32,128]{1,0:T(8,128)S(1)} %collective-permute-done.9, f32[32,128]{1,0:T(8,128)S(1)} %collective-permute-done.8, f32[4,32,128]{2,1,0:T(8,128)S(1)} %bitcast.40, s32[]{:T(128)S(6)} %select_n.63), kind=kLoop, calls=%fused_computation.4 | loop fusion | flops 12288 | bytes 81924 | tf_op jit(solution)/shard_map/add | solution.py:195
  (25 shorter events, 0.4 us)
Async XLA Ops:
  0.6 14.5 %copy-start.6 = (s32[1,1,1024]{2,1,0:T(1,128)S(1)}, s32[1,1,1024]{2,1,0:T(1,128)}, u32[]{:S(2)}) copy-start(s32[1,1,1024]{2,1,0:T(1,128)} %param.12) | copy-start | bytes 12292
  0.6 15.2 %copy-start.5 = (f32[1,1,1024]{2,1,0:T(1,128)S(1)}, f32[1,1,1024]{2,1,0:T(1,128)}, u32[]{:S(2)}) copy-start(f32[1,1,1024]{2,1,0:T(1,128)} %param.16) | copy-start | bytes 12292
  0.7 20.6 %copy-start.2 = (bf16[1,1,1024,128]{3,2,1,0:T(8,128)(2,1)S(1)}, bf16[1,1,1024,128]{3,2,1,0:T(8,128)(2,1)}, u32[]{:S(2)}) copy-start(bf16[1,1,1024,128]{3,2,1,0:T(8,128)(2,1)} %param.14) | copy-start | bytes 786436
  0.7 20.6 %copy-start.3 = (bf16[1,1,1024,128]{3,2,1,0:T(8,128)(2,1)S(1)}, bf16[1,1,1024,128]{3,2,1,0:T(8,128)(2,1)}, u32[]{:S(2)}) copy-start(bf16[1,1,1024,128]{3,2,1,0:T(8,128)(2,1)} %param.15) | copy-start | bytes 786436
  3.0 18.2 %copy-start = (bf16[128,2048]{1,0:T(8,128)(2,1)S(1)}, bf16[128,2048]{1,0:T(8,128)(2,1)}, u32[]{:S(2)}) copy-start(bf16[128,2048]{1,0:T(8,128)(2,1)} %w_in.1) | copy-start | bytes 1572868
  3.0 18.2 %copy-start.1 = (bf16[2048,128]{1,0:T(8,128)(2,1)S(1)}, bf16[2048,128]{1,0:T(8,128)(2,1)}, u32[]{:S(2)}) copy-start(bf16[2048,128]{1,0:T(8,128)(2,1)} %w_out.1) | copy-start | bytes 1572868
  3.0 8.5 %collective-permute-start = (f32[128,128]{1,0:T(8,128)S(1)}, f32[128,128]{1,0:T(8,128)S(1)}, u32[]{:S(2)}, u32[]{:S(2)}) collective-permute-start(f32[128,128]{1,0:T(8,128)S(1)} %get-tuple-element.17), channel_id=1, source_target_pairs={{0,4},{4,0},{8,12},{12,8},{16,20},{20,16},{24,28},{28,24},{1,5},{5... | collective-permute-start | bytes 196616 | tf_op jit(solution)/shard_map/ppermute | solution.py:162
  4.3 6.7 %collective-permute-start.1 = (f32[8,8,128]{2,1,0:T(8,128)S(1)}, f32[8,8,128]{2,1,0:T(8,128)S(1)}, u32[]{:S(2)}, u32[]{:S(2)}) collective-permute-start(f32[8,8,128]{2,1,0:T(8,128)S(1)} %get-tuple-element.31), channel_id=1, source_target_pairs={{0,1},{1,2},{2,3},{3,0},{4,5},{5,6},{6,7},{7,4},{8,9},{9,10},{10,1... | collective-permute-start | bytes 98312 | tf_op jit(solution)/shard_map/ppermute | solution.py:35
  7.0 4.4 %collective-permute-start.2 = (f32[8,8,128]{2,1,0:T(8,128)S(1)}, f32[8,8,128]{2,1,0:T(8,128)S(1)}, u32[]{:S(2)}, u32[]{:S(2)}) collective-permute-start(f32[8,8,128]{2,1,0:T(8,128)S(1)} %get-tuple-element.30), channel_id=1, source_target_pairs={{1,0},{2,1},{3,2},{0,3},{5,4},{6,5},{7,6},{4,7},{9,8},{10,9},{11,1... | collective-permute-start | bytes 98312 | tf_op jit(solution)/shard_map/ppermute | solution.py:36
  11.5 4.7 %collective-permute-start.3 = (f32[144,128]{1,0:T(8,128)S(1)}, f32[144,128]{1,0:T(8,128)S(1)}, u32[]{:S(2)}, u32[]{:S(2)}) collective-permute-start(f32[144,128]{1,0:T(8,128)S(1)} %pad_maximum_fusion), channel_id=1, source_target_pairs={{0,8},{4,12},{8,0},{12,4},{16,24},{20,28},{24,16},{28,20},{1,9},{5... | collective-permute-start | bytes 221192 | tf_op jit(solution)/shard_map/ppermute | solution.py:162
  13.1 5.1 %collective-permute-start.4 = (f32[144,128]{1,0:T(8,128)S(1)}, f32[144,128]{1,0:T(8,128)S(1)}, u32[]{:S(2)}, u32[]{:S(2)}) collective-permute-start(f32[144,128]{1,0:T(8,128)S(1)} %pad_maximum_fusion), channel_id=1, source_target_pairs={{0,16},{4,20},{8,24},{12,28},{16,0},{20,4},{24,8},{28,12},{1,17},{... | collective-permute-start | bytes 221192 | tf_op jit(solution)/shard_map/ppermute | solution.py:162
  14.6 5.3 %collective-permute-start.5 = (f32[144,128]{1,0:T(8,128)S(1)}, f32[144,128]{1,0:T(8,128)S(1)}, u32[]{:S(2)}, u32[]{:S(2)}) collective-permute-start(f32[144,128]{1,0:T(8,128)S(1)} %pad_maximum_fusion), channel_id=1, source_target_pairs={{0,24},{4,28},{8,16},{12,20},{16,8},{20,12},{24,0},{28,4},{1,25},{... | collective-permute-start | bytes 221192 | tf_op jit(solution)/shard_map/ppermute | solution.py:162
  19.9 1.4 %copy-start.4 = (f32[2048]{0:T(1024)S(1)}, f32[2048]{0:T(1024)}, u32[]{:S(2)}) copy-start(f32[2048]{0:T(1024)} %param.18) | copy-start | bytes 24580
  19.9 1.3 %collective-permute-start.6 = (f32[144,128]{1,0:T(8,128)S(1)}, f32[144,128]{1,0:T(8,128)S(1)}, u32[]{:S(2)}, u32[]{:S(2)}) collective-permute-start(f32[144,128]{1,0:T(8,128)S(1)} %add_add_fusion.mine), channel_id=1, source_target_pairs={{0,4},{4,0},{8,12},{12,8},{16,20},{20,16},{24,28},{28,24},{1,5},{5... | collective-permute-start | bytes 221192 | tf_op jit(solution)/shard_map/ppermute | solution.py:162
  27.6 1.3 %collective-permute-start.7 = (f32[128,128]{1,0:T(8,128)S(1)}, f32[128,128]{1,0:T(8,128)S(1)}, u32[]{:S(2)}, u32[]{:S(2)}) collective-permute-start(f32[128,128]{1,0:T(8,128)S(1)} %get-tuple-element.29), channel_id=1, source_target_pairs={{0,4},{4,0},{8,12},{12,8},{16,20},{20,16},{24,28},{28,24},{1,5},{5... | collective-permute-start | bytes 196616 | tf_op jit(solution)/shard_map/ppermute | solution.py:162
  28.9 4.2 %collective-permute-start.10 = (f32[32,128]{1,0:T(8,128)S(1)}, f32[32,128]{1,0:T(8,128)S(1)}, u32[]{:S(2)}, u32[]{:S(2)}) collective-permute-start(f32[32,128]{1,0:T(8,128)S(1)} %get-tuple-element.33), channel_id=1, source_target_pairs={{0,16},{4,20},{8,24},{12,28},{16,0},{20,4},{24,8},{28,12},{1,17},{... | collective-permute-start | bytes 49160 | tf_op jit(solution)/shard_map/ppermute | solution.py:162
  29.5 4.6 %collective-permute-start.8 = (f32[32,128]{1,0:T(8,128)S(1)}, f32[32,128]{1,0:T(8,128)S(1)}, u32[]{:S(2)}, u32[]{:S(2)}) collective-permute-start(f32[32,128]{1,0:T(8,128)S(1)} %get-tuple-element.32), channel_id=1, source_target_pairs={{0,24},{4,28},{8,16},{12,20},{16,8},{20,12},{24,0},{28,4},{1,25},{... | collective-permute-start | bytes 49160 | tf_op jit(solution)/shard_map/ppermute | solution.py:162
  31.0 3.7 %collective-permute-start.9 = (f32[32,128]{1,0:T(8,128)S(1)}, f32[32,128]{1,0:T(8,128)S(1)}, u32[]{:S(2)}, u32[]{:S(2)}) collective-permute-start(f32[32,128]{1,0:T(8,128)S(1)} %get-tuple-element.34), channel_id=1, source_target_pairs={{0,8},{4,12},{8,0},{12,4},{16,24},{20,28},{24,16},{28,20},{1,9},{5... | collective-permute-start | bytes 49160 | tf_op jit(solution)/shard_map/ppermute | solution.py:162

commit v6 on v5

--- a/solution.py
+++ b/solution.py
@@ -15,7 +15,7 @@
 GELU_CUBE = 0.044715
 
 ON_CHIP = pl.BlockSpec(memory_space=pltpu.VMEM)
-EDGE = 8 * -(-SWEEPS // 8)
+EDGE = 8 * -(-2 * SWEEPS // 8)
 
 
 def near(*arrays):
@@ -123,8 +123,7 @@
         start = start + field[base:base + EDGE] * factors[member, :EDGE]
         stop = stop + field[base + EDGE:base + 2 * EDGE] * factors[member, EDGE:]
     rows = lax.broadcasted_iota(jnp.int32, (EDGE, levels), 0)
-    edges[:EDGE] = jnp.where(rows < SWEEPS, start, 0.0)
-    edges[EDGE:] = jnp.where(rows >= EDGE - SWEEPS, stop, 0.0)
+    edges[...] = jnp.where(rows < SWEEPS, start, jnp.where(rows >= EDGE - SWEEPS, stop, 0.0))
 
 
 def member_sum(control, perturb, core, owners):
@@ -148,7 +147,7 @@
     )(core, *(pltpu.with_memory_space_constraint(a, pltpu.HBM) for a in (control, perturb)))
     edges = pl.pallas_call(
         edge_kernel,
-        out_shape=pltpu.VMEM((2 * EDGE, levels), jnp.float32),
+        out_shape=pltpu.VMEM((EDGE, levels), jnp.float32),
         in_specs=[ON_CHIP] * 4,
         out_specs=ON_CHIP,
         compiler_params=room(16),
@@ -232,13 +231,14 @@
     core, mine, other, by_column, by_slot, spread, background, targets, w_in, b_in, w_out, keep, send, whole, slope, *, scale, block, chunk
 ):
     slots, levels = background.shape
-    half_columns = mine.shape[0] - 2 * EDGE
+    half_columns = mine.shape[0] - EDGE
     hidden = w_in.shape[1]
     edges = mine[half_columns:] + other[half_columns:]
-    first = edges[:EDGE]
-    last = edges[EDGE:]
+    place = lax.broadcasted_iota(jnp.int32, edges.shape, 0)
+    none = jnp.zeros_like(edges)
+    first = jnp.where(place < SWEEPS, edges, none)
+    last = jnp.where(place >= EDGE - SWEEPS, edges, none)
     even = core[0] == 0
-    none = jnp.zeros_like(first)
     parts = []
     for rows, low, high in ((mine, even, ~even), (other, ~even, even)):
         parts += [
@@ -319,7 +319,7 @@
 def observe_call(core, mine, other, by_column, by_slot, spread, background, targets, w_in, b_in, w_out, scale):
     block = largest_part(background.shape[0], 512)
     chunk = largest_part(w_in.shape[1], 256)
-    half = pltpu.VMEM((mine.shape[0] - 2 * EDGE, mine.shape[1]), jnp.float32)
+    half = pltpu.VMEM((mine.shape[0] - EDGE, mine.shape[1]), jnp.float32)
     return pl.pallas_call(
         functools.partial(observe_kernel, scale=scale, block=block, chunk=chunk),
         out_shape=(half,) * 3,
@@ -382,7 +382,7 @@
     else:
         halo = mine[columns // 2 :]
         full = jnp.concatenate([mine[: columns // 2], other[: columns // 2]], axis=0)
-        full = full.at[:EDGE].add(halo[:EDGE]).at[-EDGE:].add(halo[EDGE:])
+        full = full.at[:SWEEPS].add(halo[:SWEEPS]).at[-SWEEPS:].add(halo[EDGE - SWEEPS :])
         increment = lax.dynamic_slice_in_dim(full, me * owned, owned, 0) * scale
         gradient = jnp.concatenate([keep, send], axis=0)
         grad_columns = lax.psum_scatter(gradient, "mem", scatter_dimension=0, tiled=True)

time: 35.5 us -> 35.5 us (level)
  no operation moved by 1% of the time
where the time goes in v6:
time: 35.5 us; the launch traced here: 35.3 us
  starting transfers between devices  12.7 us (36%)
  waiting for transfers between devices  9.93 us (28%)
  Pallas kernels  9.15 us (26%)
  other arithmetic  1.46 us (4%)
  between operations  1.46 us (4%)
  local copies, waits for them, and re-layouts  0.66 us (2%)
    ppermute x9, starting transfers between devices, bit_swap(): return lax.ppermute(block, axis, [(i, i ^ bit) for i in range(count)])  7.95 us
    ppermute x9, waiting for transfers between devices, bit_swap(): return lax.ppermute(block, axis, [(i, i ^ bit) for i in range(count)])  7.64 us
    pallas_call x1, Pallas kernels, observe_call(): pl.pallas_call(functools.partial(observe_kernel, scale=scale, block=block...  6.32 us
    ppermute x1, starting transfers between devices, edge_columns(): low = lax.ppermute(last, axis, forward)  2.62 us
    pallas_call x1, Pallas kernels, member_sum(): pl.pallas_call(functools.partial(inside_kernel, owners=owners), out_shape...  2.33 us
    ppermute x1, starting transfers between devices, edge_columns(): high = lax.ppermute(first, axis, backward)  2.08 us
    ppermute x1, waiting for transfers between devices, edge_columns(): low = lax.ppermute(last, axis, forward)  1.99 us
    convert_element_type x1, other arithmetic, edge_columns(): first = block[:, :EDGE].astype(jnp.float32)  0.74 us
  transfers between devices with their start and end apart: 11, of which 8 were waited for; matrix products, arithmetic and copies ran while one was open for 4% of the time, Pallas kernels for 1%

profile of v6, /device:TPU:0, one launch (start us, length us, event | category | flops | bytes accessed | tf_op | source)
XLA Modules:
  0.0 35.3 jit_solution(1676533728882718998)
XLA Ops:
  0.7 2.3 %inside.1 = (f32[128,128]{1,0:T(8,128)S(1)}, f32[128,128]{1,0:T(8,128)S(1)}, f32[8,16,128]{2,1,0:T(8,128)S(1)}, f32[8,16,128]{2,1,0:T(8,128)S(1)}) custom-call(s32[1]{0:T(128)} %bitcast.core, bf16[8,256,128]{2,1,0:T(8,128)(2,1)} %control.1, bf16[8,256,128]{2,1,0:T(8,128)(2,1)} %perturb.1), custom_call_target="tpu_custom_call" | custom-call | tf_op jit(solution)/shard_map/inside/pallas_call | solution.py:134
  3.0 0.6 %collective-permute-start = (f32[128,128]{1,0:T(8,128)S(1)}, f32[128,128]{1,0:T(8,128)S(1)}, u32[]{:S(2)}, u32[]{:S(2)}) collective-permute-start(f32[128,128]{1,0:T(8,128)S(1)} %get-tuple-element.17), channel_id=1, source_target_pairs={{0,4},{4,0},{8,12},{12,8},{16,20},{20,16},{24,28},{28,24},{1,5},{5... | collective-permute-start | bytes 196616 | tf_op jit(solution)/shard_map/ppermute | solution.py:161
  3.6 0.7 %slice_convert_fusion = (f32[8,8,128]{2,1,0:T(8,128)S(1)}, f32[8,8,128]{2,1,0:T(8,128)S(1)}) fusion(bf16[8,256,128]{2,1,0:T(8,128)(2,1)} %control.1), kind=kLoop, calls=%fused_computation.9 | loop fusion | flops 16384 | bytes 98304 | tf_op jit(solution)/shard_map/convert_element_type | solution.py:33
  4.3 2.6 %collective-permute-start.1 = (f32[8,8,128]{2,1,0:T(8,128)S(1)}, f32[8,8,128]{2,1,0:T(8,128)S(1)}, u32[]{:S(2)}, u32[]{:S(2)}) collective-permute-start(f32[8,8,128]{2,1,0:T(8,128)S(1)} %get-tuple-element.31), channel_id=1, source_target_pairs={{0,1},{1,2},{2,3},{3,0},{4,5},{5,6},{6,7},{7,4},{8,9},{9,10},{10,1... | collective-permute-start | bytes 98312 | tf_op jit(solution)/shard_map/ppermute | solution.py:35
  6.9 2.1 %collective-permute-start.2 = (f32[8,8,128]{2,1,0:T(8,128)S(1)}, f32[8,8,128]{2,1,0:T(8,128)S(1)}, u32[]{:S(2)}, u32[]{:S(2)}) collective-permute-start(f32[8,8,128]{2,1,0:T(8,128)S(1)} %get-tuple-element.30), channel_id=1, source_target_pairs={{1,0},{2,1},{3,2},{0,3},{5,4},{6,5},{7,6},{4,7},{9,8},{10,9},{11,1... | collective-permute-start | bytes 98312 | tf_op jit(solution)/shard_map/ppermute | solution.py:36
  9.0 2.0 %collective-permute-done.1.low = f32[8,8,128]{2,1,0:T(8,128)S(1)} collective-permute-done((f32[8,8,128]{2,1,0:T(8,128)S(1)}, f32[8,8,128]{2,1,0:T(8,128)S(1)}, u32[]{:S(2)}, u32[]{:S(2)}) %collective-permute-start.1) | collective-permute-done | bytes 32800 | tf_op jit(solution)/shard_map/ppermute | solution.py:35
  11.0 0.3 collective-permute-done.2.high
  11.5 1.6 %collective-permute-start.3 = (f32[136,128]{1,0:T(8,128)S(1)}, f32[136,128]{1,0:T(8,128)S(1)}, u32[]{:S(2)}, u32[]{:S(2)}) collective-permute-start(f32[136,128]{1,0:T(8,128)S(1)} %pad_maximum_fusion), channel_id=1, source_target_pairs={{0,8},{4,12},{8,0},{12,4},{16,24},{20,28},{24,16},{28,20},{1,9},{5... | collective-permute-start | bytes 208904 | tf_op jit(solution)/shard_map/ppermute | solution.py:161
  13.1 1.5 %collective-permute-start.4 = (f32[136,128]{1,0:T(8,128)S(1)}, f32[136,128]{1,0:T(8,128)S(1)}, u32[]{:S(2)}, u32[]{:S(2)}) collective-permute-start(f32[136,128]{1,0:T(8,128)S(1)} %pad_maximum_fusion), channel_id=1, source_target_pairs={{0,16},{4,20},{8,24},{12,28},{16,0},{20,4},{24,8},{28,12},{1,17},{... | collective-permute-start | bytes 208904 | tf_op jit(solution)/shard_map/ppermute | solution.py:161
  14.6 0.5 %collective-permute-start.5 = (f32[136,128]{1,0:T(8,128)S(1)}, f32[136,128]{1,0:T(8,128)S(1)}, u32[]{:S(2)}, u32[]{:S(2)}) collective-permute-start(f32[136,128]{1,0:T(8,128)S(1)} %pad_maximum_fusion), channel_id=1, source_target_pairs={{0,24},{4,28},{8,16},{12,20},{16,8},{20,12},{24,0},{28,4},{1,25},{... | collective-permute-start | bytes 208904 | tf_op jit(solution)/shard_map/ppermute | solution.py:161
  15.8 0.3 layout.1
  16.2 2.0 %collective-permute-done.4 = f32[136,128]{1,0:T(8,128)S(1)} collective-permute-done((f32[136,128]{1,0:T(8,128)S(1)}, f32[136,128]{1,0:T(8,128)S(1)}, u32[]{:S(2)}, u32[]{:S(2)}) %collective-permute-start.4) | collective-permute-done | bytes 69664 | tf_op jit(solution)/shard_map/ppermute | solution.py:161
  18.2 1.7 %collective-permute-done.5 = f32[136,128]{1,0:T(8,128)S(1)} collective-permute-done((f32[136,128]{1,0:T(8,128)S(1)}, f32[136,128]{1,0:T(8,128)S(1)}, u32[]{:S(2)}, u32[]{:S(2)}) %collective-permute-start.5) | collective-permute-done | bytes 69664 | tf_op jit(solution)/shard_map/ppermute | solution.py:161
  19.9 1.2 %collective-permute-done.6.other = f32[136,128]{1,0:T(8,128)S(1)} collective-permute-done((f32[136,128]{1,0:T(8,128)S(1)}, f32[136,128]{1,0:T(8,128)S(1)}, u32[]{:S(2)}, u32[]{:S(2)}) %collective-permute-start.6) | collective-permute-done | bytes 69664 | tf_op jit(solution)/shard_map/ppermute | solution.py:161
  21.2 6.3 %observe.1 = (f32[128,128]{1,0:T(8,128)S(1)}, f32[128,128]{1,0:T(8,128)S(1)}, f32[128,128]{1,0:T(8,128)S(1)}) custom-call(s32[1]{0:T(128)} %bitcast.core, f32[136,128]{1,0:T(8,128)S(1)} %add_add_fusion.mine, f32[136,128]{1,0:T(8,128)S(1)} %collective-permute-done.6.other, bf16[256,1024]{1,0:T(8,128)(2,1)S(1)} %get-tuple-element.24.by_column, ...), custom_call_target="tpu_custom_call" | custom-call | tf_op jit(solution)/shard_map/observe/pallas_call | solution.py:323
  27.5 0.2 collective-permute-start.7
  27.8 1.1 %collective-permute-done.7 = f32[128,128]{1,0:T(8,128)S(1)} collective-permute-done((f32[128,128]{1,0:T(8,128)S(1)}, f32[128,128]{1,0:T(8,128)S(1)}, u32[]{:S(2)}, u32[]{:S(2)}) %collective-permute-start.7) | collective-permute-done | bytes 65568 | tf_op jit(solution)/shard_map/ppermute | solution.py:161
  28.9 0.6 %collective-permute-start.10 = (f32[32,128]{1,0:T(8,128)S(1)}, f32[32,128]{1,0:T(8,128)S(1)}, u32[]{:S(2)}, u32[]{:S(2)}) collective-permute-start(f32[32,128]{1,0:T(8,128)S(1)} %get-tuple-element.33), channel_id=1, source_target_pairs={{0,16},{4,20},{8,24},{12,28},{16,0},{20,4},{24,8},{28,12},{1,17},{... | collective-permute-start | bytes 49160 | tf_op jit(solution)/shard_map/ppermute | solution.py:161
  29.5 1.5 %collective-permute-start.8 = (f32[32,128]{1,0:T(8,128)S(1)}, f32[32,128]{1,0:T(8,128)S(1)}, u32[]{:S(2)}, u32[]{:S(2)}) collective-permute-start(f32[32,128]{1,0:T(8,128)S(1)} %get-tuple-element.32), channel_id=1, source_target_pairs={{0,24},{4,28},{8,16},{12,20},{16,8},{20,12},{24,0},{28,4},{1,25},{... | collective-permute-start | bytes 49160 | tf_op jit(solution)/shard_map/ppermute | solution.py:161
  31.0 1.5 %collective-permute-start.9 = (f32[32,128]{1,0:T(8,128)S(1)}, f32[32,128]{1,0:T(8,128)S(1)}, u32[]{:S(2)}, u32[]{:S(2)}) collective-permute-start(f32[32,128]{1,0:T(8,128)S(1)} %get-tuple-element.34), channel_id=1, source_target_pairs={{0,8},{4,12},{8,0},{12,4},{16,24},{20,28},{24,16},{28,20},{1,9},{5... | collective-permute-start | bytes 49160 | tf_op jit(solution)/shard_map/ppermute | solution.py:161
  32.5 0.6 %dynamic-slice_bitcast_fusion.3 = f32[32,128]{1,0:T(8,128)} fusion(f32[4,32,128]{2,1,0:T(8,128)S(1)} %bitcast.37, s32[]{:T(128)S(6)} %select_n.62), kind=kLoop, calls=%fused_computation.8 | loop fusion | bytes 32772 | tf_op jit(solution)/shard_map/squeeze | solution.py:165
  33.1 1.0 %collective-permute-done.8 = f32[32,128]{1,0:T(8,128)S(1)} collective-permute-done((f32[32,128]{1,0:T(8,128)S(1)}, f32[32,128]{1,0:T(8,128)S(1)}, u32[]{:S(2)}, u32[]{:S(2)}) %collective-permute-start.8) | collective-permute-done | bytes 16416 | tf_op jit(solution)/shard_map/ppermute | solution.py:161
  34.1 0.6 %collective-permute-done.9 = f32[32,128]{1,0:T(8,128)S(1)} collective-permute-done((f32[32,128]{1,0:T(8,128)S(1)}, f32[32,128]{1,0:T(8,128)S(1)}, u32[]{:S(2)}, u32[]{:S(2)}) %collective-permute-start.9) | collective-permute-done | bytes 16416 | tf_op jit(solution)/shard_map/ppermute | solution.py:161
  34.7 0.6 %fusion.1 = f32[32,128]{1,0:T(8,128)} fusion(f32[32,128]{1,0:T(8,128)S(1)} %collective-permute-done.10, f32[32,128]{1,0:T(8,128)S(1)} %collective-permute-done.9, f32[32,128]{1,0:T(8,128)S(1)} %collective-permute-done.8, f32[4,32,128]{2,1,0:T(8,128)S(1)} %bitcast.40, s32[]{:T(128)S(6)} %select_n.63), kind=kLoop, calls=%fused_computation.4 | loop fusion | flops 12288 | bytes 81924 | tf_op jit(solution)/shard_map/add | solution.py:194
  (25 shorter events, 0.4 us)
Async XLA Ops:
  0.6 20.6 %copy-start.1 = (bf16[2048,128]{1,0:T(8,128)(2,1)S(1)}, bf16[2048,128]{1,0:T(8,128)(2,1)}, u32[]{:S(2)}) copy-start(bf16[2048,128]{1,0:T(8,128)(2,1)} %w_out.1) | copy-start | bytes 1572868
  0.6 20.5 %copy-start.3 = (bf16[1,1,1024,128]{3,2,1,0:T(8,128)(2,1)S(1)}, bf16[1,1,1024,128]{3,2,1,0:T(8,128)(2,1)}, u32[]{:S(2)}) copy-start(bf16[1,1,1024,128]{3,2,1,0:T(8,128)(2,1)} %param.15) | copy-start | bytes 786436
  3.0 18.2 %copy-start = (bf16[128,2048]{1,0:T(8,128)(2,1)S(1)}, bf16[128,2048]{1,0:T(8,128)(2,1)}, u32[]{:S(2)}) copy-start(bf16[128,2048]{1,0:T(8,128)(2,1)} %w_in.1) | copy-start | bytes 1572868
  3.0 8.5 %collective-permute-start = (f32[128,128]{1,0:T(8,128)S(1)}, f32[128,128]{1,0:T(8,128)S(1)}, u32[]{:S(2)}, u32[]{:S(2)}) collective-permute-start(f32[128,128]{1,0:T(8,128)S(1)} %get-tuple-element.17), channel_id=1, source_target_pairs={{0,4},{4,0},{8,12},{12,8},{16,20},{20,16},{24,28},{28,24},{1,5},{5... | collective-permute-start | bytes 196616 | tf_op jit(solution)/shard_map/ppermute | solution.py:161
  4.3 6.7 %collective-permute-start.1 = (f32[8,8,128]{2,1,0:T(8,128)S(1)}, f32[8,8,128]{2,1,0:T(8,128)S(1)}, u32[]{:S(2)}, u32[]{:S(2)}) collective-permute-start(f32[8,8,128]{2,1,0:T(8,128)S(1)} %get-tuple-element.31), channel_id=1, source_target_pairs={{0,1},{1,2},{2,3},{3,0},{4,5},{5,6},{6,7},{7,4},{8,9},{9,10},{10,1... | collective-permute-start | bytes 98312 | tf_op jit(solution)/shard_map/ppermute | solution.py:35
  6.9 4.4 %collective-permute-start.2 = (f32[8,8,128]{2,1,0:T(8,128)S(1)}, f32[8,8,128]{2,1,0:T(8,128)S(1)}, u32[]{:S(2)}, u32[]{:S(2)}) collective-permute-start(f32[8,8,128]{2,1,0:T(8,128)S(1)} %get-tuple-element.30), channel_id=1, source_target_pairs={{1,0},{2,1},{3,2},{0,3},{5,4},{6,5},{7,6},{4,7},{9,8},{10,9},{11,1... | collective-permute-start | bytes 98312 | tf_op jit(solution)/shard_map/ppermute | solution.py:36
  11.5 3.6 %copy-start.6 = (s32[1,1,1024]{2,1,0:T(1,128)S(1)}, s32[1,1,1024]{2,1,0:T(1,128)}, u32[]{:S(2)}) copy-start(s32[1,1,1024]{2,1,0:T(1,128)} %param.12) | copy-start | bytes 12292
  11.5 4.3 %copy-start.5 = (f32[1,1,1024]{2,1,0:T(1,128)S(1)}, f32[1,1,1024]{2,1,0:T(1,128)}, u32[]{:S(2)}) copy-start(f32[1,1,1024]{2,1,0:T(1,128)} %param.16) | copy-start | bytes 12292
  11.5 9.7 %copy-start.2 = (bf16[1,1,1024,128]{3,2,1,0:T(8,128)(2,1)S(1)}, bf16[1,1,1024,128]{3,2,1,0:T(8,128)(2,1)}, u32[]{:S(2)}) copy-start(bf16[1,1,1024,128]{3,2,1,0:T(8,128)(2,1)} %param.14) | copy-start | bytes 786436
  11.5 4.6 %collective-permute-start.3 = (f32[136,128]{1,0:T(8,128)S(1)}, f32[136,128]{1,0:T(8,128)S(1)}, u32[]{:S(2)}, u32[]{:S(2)}) collective-permute-start(f32[136,128]{1,0:T(8,128)S(1)} %pad_maximum_fusion), channel_id=1, source_target_pairs={{0,8},{4,12},{8,0},{12,4},{16,24},{20,28},{24,16},{28,20},{1,9},{5... | collective-permute-start | bytes 208904 | tf_op jit(solution)/shard_map/ppermute | solution.py:161
  13.1 5.1 %collective-permute-start.4 = (f32[136,128]{1,0:T(8,128)S(1)}, f32[136,128]{1,0:T(8,128)S(1)}, u32[]{:S(2)}, u32[]{:S(2)}) collective-permute-start(f32[136,128]{1,0:T(8,128)S(1)} %pad_maximum_fusion), channel_id=1, source_target_pairs={{0,16},{4,20},{8,24},{12,28},{16,0},{20,4},{24,8},{28,12},{1,17},{... | collective-permute-start | bytes 208904 | tf_op jit(solution)/shard_map/ppermute | solution.py:161
  14.6 5.2 %collective-permute-start.5 = (f32[136,128]{1,0:T(8,128)S(1)}, f32[136,128]{1,0:T(8,128)S(1)}, u32[]{:S(2)}, u32[]{:S(2)}) collective-permute-start(f32[136,128]{1,0:T(8,128)S(1)} %pad_maximum_fusion), channel_id=1, source_target_pairs={{0,24},{4,28},{8,16},{12,20},{16,8},{20,12},{24,0},{28,4},{1,25},{... | collective-permute-start | bytes 208904 | tf_op jit(solution)/shard_map/ppermute | solution.py:161
  19.9 1.4 %copy-start.4 = (f32[2048]{0:T(1024)S(1)}, f32[2048]{0:T(1024)}, u32[]{:S(2)}) copy-start(f32[2048]{0:T(1024)} %param.18) | copy-start | bytes 24580
  19.9 1.3 %collective-permute-start.6 = (f32[136,128]{1,0:T(8,128)S(1)}, f32[136,128]{1,0:T(8,128)S(1)}, u32[]{:S(2)}, u32[]{:S(2)}) collective-permute-start(f32[136,128]{1,0:T(8,128)S(1)} %add_add_fusion.mine), channel_id=1, source_target_pairs={{0,4},{4,0},{8,12},{12,8},{16,20},{20,16},{24,28},{28,24},{1,5},{5... | collective-permute-start | bytes 208904 | tf_op jit(solution)/shard_map/ppermute | solution.py:161
  27.5 1.3 %collective-permute-start.7 = (f32[128,128]{1,0:T(8,128)S(1)}, f32[128,128]{1,0:T(8,128)S(1)}, u32[]{:S(2)}, u32[]{:S(2)}) collective-permute-start(f32[128,128]{1,0:T(8,128)S(1)} %get-tuple-element.29), channel_id=1, source_target_pairs={{0,4},{4,0},{8,12},{12,8},{16,20},{20,16},{24,28},{28,24},{1,5},{5... | collective-permute-start | bytes 196616 | tf_op jit(solution)/shard_map/ppermute | solution.py:161
  28.9 4.2 %collective-permute-start.10 = (f32[32,128]{1,0:T(8,128)S(1)}, f32[32,128]{1,0:T(8,128)S(1)}, u32[]{:S(2)}, u32[]{:S(2)}) collective-permute-start(f32[32,128]{1,0:T(8,128)S(1)} %get-tuple-element.33), channel_id=1, source_target_pairs={{0,16},{4,20},{8,24},{12,28},{16,0},{20,4},{24,8},{28,12},{1,17},{... | collective-permute-start | bytes 49160 | tf_op jit(solution)/shard_map/ppermute | solution.py:161
  29.5 4.6 %collective-permute-start.8 = (f32[32,128]{1,0:T(8,128)S(1)}, f32[32,128]{1,0:T(8,128)S(1)}, u32[]{:S(2)}, u32[]{:S(2)}) collective-permute-start(f32[32,128]{1,0:T(8,128)S(1)} %get-tuple-element.32), channel_id=1, source_target_pairs={{0,24},{4,28},{8,16},{12,20},{16,8},{20,12},{24,0},{28,4},{1,25},{... | collective-permute-start | bytes 49160 | tf_op jit(solution)/shard_map/ppermute | solution.py:161
  31.0 3.7 %collective-permute-start.9 = (f32[32,128]{1,0:T(8,128)S(1)}, f32[32,128]{1,0:T(8,128)S(1)}, u32[]{:S(2)}, u32[]{:S(2)}) collective-permute-start(f32[32,128]{1,0:T(8,128)S(1)} %get-tuple-element.34), channel_id=1, source_target_pairs={{0,8},{4,12},{8,0},{12,4},{16,24},{20,28},{24,16},{28,20},{1,9},{5... | collective-permute-start | bytes 49160 | tf_op jit(solution)/shard_map/ppermute | solution.py:161
